TPU v7x, 256 devices: a whole 4x4x8 slice. The times are simulated.
256 devices in a mesh: lines: 4 (over y), buses: 64 (over z, x, core).
Axes of the slice: x: 4, y: 4, z: 8, core: 2. Of those that a mesh axis runs over, the one named last changes fastest.
Arguments:
- ptdf: bfloat16 [4096, 81920], P('lines', 'buses'), may hold values from -0.0625 to 0.0625
- load: float32 [384, 81920], P(None, 'buses'), may hold values from 0.03 to 3.8, as said below
- ratings: float32 [32768], replicated, may hold values from 0.3 to 3
- line_index: int32 [4096], P('lines'), may hold values from 0 to 32767
- gen_bus: int32 [16384], P('buses'), may hold values from 0 to 81919, as said below
- gen_quad: float32 [16384], P('buses'), may hold values from 0.05 to 0.5
- gen_lin: float32 [16384], P('buses'), may hold values from 0.5 to 2.5
- gen_max: float32 [16384], P('buses'), may hold values from 0.8 to 4
- gen_start: float32 [384, 16384], P(None, 'buses'), may hold values from 0 to 2
- stor_bus: int32 [8192], P('buses'), may hold values from 0 to 1279
- stor_quad: float32 [8192], P('buses'), may hold values from 0.05 to 0.5
- stor_rate: float32 [8192], P('buses'), may hold values from 0.3 to 1.5
- stor_energy: float32 [8192], P('buses'), may hold values from 1 to 8
- stor_start: float32 [384, 8192], P(None, 'buses'), may hold values from -0.5 to 0.5
- lam_start: float32 [384], replicated, may hold values from -4 to 4
- mu_start: float32 [384, 4096], P(None, ('lines', 'buses')), may hold values from -3 to 3
- omega_start: float32 [384, 8192], P(None, 'buses'), may hold values from -2 to 2
Outputs:
- gen_out: float32 [384, 16384], P(None, 'buses')
- stor_out: float32 [384, 8192], P(None, 'buses')
- lam_out: float32 [384], replicated
- mu_out: float32 [384, 4096], P(None, ('lines', 'buses'))
- omega_out: float32 [384, 8192], P(None, 'buses')
Inputs may be any that keep to these rules, and one draw needn't show every extreme that they name: `gen_bus`: of the 256 generators of one area at most 8 sit on the buses of any one area (1280 consecutive buses); in every draw one area holds exactly 8 generators of every area, and the others of an area spread over the remaining areas as evenly as counts allow. `load`: loads are positive.
All inputs are finite; a program needn't handle non-finite values.
Results may differ from a plain program's by a relative error of at most 0.0075.
Values may be sent and summed in bfloat16 or wider, within the bound.
No kernel may reach another device: no remote copies, remote signals or barrier semaphores. Data moves between devices by JAX's collectives and lax.ppermute only.
A program may use at most 64 MiB of HBM per device.

v0:
```python
import jax
import jax.numpy as jnp
from jax import lax
from jax.sharding import Mesh
from jax.sharding import PartitionSpec as P

HOURS = 24
Z, X, CORES = (8, 4, 2)


TAU = 0.25
SIGMA_FLOW = 4.0
SIGMA_STORE = 0.25
KAPPA = 1.0
THETA = 0.5

AREAS = ("z", "x", "core")
CHIPS = ("z", "x")


def rounded(x):
    return lax.reduce_precision(x, 8, 7)


def swapped(x):
    return lax.ppermute(x, "core", [(0, 1), (1, 0)])


def sum_over_lines(part):
    low = part.astype(jnp.bfloat16)
    near = [
        lax.ppermute(low, "lines", [(i, (i + s) % 4) for i in range(4)]).astype(jnp.float32)
        for s in (1, 2, 3)
    ]
    return (rounded(part) + near[1]) + (near[0] + near[2])


def sent_to_chips(x):
    size = Z * X
    sent = jnp.broadcast_to(x[None], (size, *x.shape))
    return lax.all_to_all(sent, CHIPS, 0, 0, tiled=True)


def gathered_duals(share):
    own = sent_to_chips(share.astype(jnp.bfloat16)).reshape(-1, share.shape[1])
    return own, swapped(own)


def hour_sums(row_count, later):
    row = jnp.arange(row_count, dtype=jnp.int32)
    same = (row[:, None] // HOURS) == (row[None, :] // HOURS)
    side = (row[None, :] >= row[:, None]) if later else (row[None, :] <= row[:, None])
    return jnp.where(same & side, 1.0, 0.0).astype(jnp.float32)


def summed_hours(values, later):
    return jnp.dot(
        hour_sums(values.shape[0], later),
        values,
        precision=lax.Precision.HIGHEST,
        preferred_element_type=jnp.float32,
    )


def dual_step(dual_now, image_term, step_size, low_bound, high_bound):
    shifted = dual_now + step_size * image_term
    return shifted - step_size * jnp.clip(shifted / step_size, low_bound, high_bound)


def shards(
    ptdf,
    load,
    ratings,
    line_index,
    gen_bus,
    gen_quad,
    gen_lin,
    gen_max,
    gen_start,
    stor_bus,
    stor_quad,
    stor_rate,
    stor_energy,
    stor_start,
    lam_start,
    mu_start,
    omega_start,
):
    row_count = load.shape[0]
    line_count, bus_count = ptdf.shape
    gen_count = gen_bus.shape[0]
    stor_count = stor_bus.shape[0]
    area_count = Z * X * CORES
    chip_count = Z * X
    slots = max(8, (gen_count + area_count - 1) // area_count)
    share_len = line_count // area_count
    core = lax.axis_index("core")
    area = (lax.axis_index("z") * X + lax.axis_index("x")) * CORES + core

    target = gen_bus // bus_count
    local_bus = gen_bus % bus_count
    order = jnp.arange(gen_count, dtype=jnp.int32)
    earlier = (target[:, None] == target[None, :]) & (order[None, :] < order[:, None])
    column = target * slots + jnp.sum(earlier.astype(jnp.int32), axis=1)
    slot_of = jnp.arange(area_count * slots, dtype=jnp.int32)
    placed = slot_of[:, None] == column[None, :]
    slot_bus = jnp.sum(jnp.where(placed, local_bus[None, :] + 1, 0), axis=1) - 1
    wanted = lax.all_to_all(slot_bus.reshape(area_count, slots), AREAS, 0, 0, tiled=True)

    dual_flow = mu_start.T
    dual_own, dual_other = gathered_duals(dual_flow)

    bus_ids = jnp.arange(bus_count, dtype=jnp.int32)
    sel_gen = (wanted.reshape(-1)[:, None] == bus_ids[None, :]).astype(jnp.bfloat16)
    sel_stor = (stor_bus[:, None] == bus_ids[None, :]).astype(jnp.bfloat16)
    contract_minor = (((1,), (1,)), ((), ()))
    sent_columns = lax.dot_general(
        sel_gen, ptdf, contract_minor, preferred_element_type=jnp.float32
    ).astype(jnp.bfloat16)
    columns = lax.all_to_all(sent_columns, AREAS, 0, 0, tiled=True)
    weight_stor = lax.dot_general(
        ptdf, sel_stor, contract_minor, preferred_element_type=jnp.float32
    ).astype(jnp.bfloat16)
    pick = (column[:, None] == slot_of[None, :]).astype(jnp.bfloat16)
    weight_gen = lax.dot_general(
        columns, pick, (((0,), (1,)), ((), ())), preferred_element_type=jnp.float32
    ).astype(jnp.bfloat16)
    weight = jnp.concatenate([weight_gen, weight_stor], axis=1)

    def by_core(x):
        split = x.reshape(chip_count, CORES, share_len, x.shape[1])
        own = lax.dynamic_index_in_dim(split, core, 1, keepdims=False)
        other = lax.dynamic_index_in_dim(split, 1 - core, 1, keepdims=False)
        return own.reshape(-1, x.shape[1]), other.reshape(-1, x.shape[1])

    weight_own, weight_other = by_core(weight)
    load_own, load_other = by_core(
        lax.dot_general(
            ptdf, load.astype(jnp.bfloat16), contract_minor, preferred_element_type=jnp.float32
        )
    )
    load_flow = load_own + swapped(load_other)
    load_total = jnp.sum(load, axis=1)

    limit = jnp.take(ratings, lax.dynamic_slice_in_dim(line_index, area * share_len, share_len))[:, None]
    hour_of = jnp.arange(row_count, dtype=jnp.int32) % HOURS
    last_hour = (hour_of == HOURS - 1)[:, None]
    half_energy = (0.5 * stor_energy)[None, :]
    low_bound = jnp.where(last_hour, jnp.zeros_like(half_energy), -half_energy)
    high_bound = jnp.where(last_hour, jnp.zeros_like(half_energy), half_energy)
    total_units = (gen_count + stor_count) * area_count
    gen_now, stor_now = (gen_start, stor_start)
    gen_old, stor_old = (gen_start, stor_start)
    price_level, dual_store = (lam_start, omega_start)
    contract_major = (((0,), (0,)), ((), ()))
    for iteration in range(2):
        if iteration == 0:
            gen_mid, stor_mid = (gen_now, stor_now)
        else:
            gen_mid = gen_now + THETA * (gen_now - gen_old)
            stor_mid = stor_now + THETA * (stor_now - stor_old)
        price = sum_over_lines(
            lax.dot_general(dual_own, weight_own, contract_major, preferred_element_type=jnp.float32)
            + lax.dot_general(dual_other, weight_other, contract_major, preferred_element_type=jnp.float32)
        )
        gen_price, stor_price = price[:, :gen_count], price[:, gen_count:]
        gen_grad = 2.0 * gen_quad * gen_mid + gen_lin + price_level[:, None] + gen_price
        gen_next = jnp.clip(gen_mid - TAU * gen_grad, 0.0, gen_max)
        stor_grad = (
            2.0 * stor_quad * stor_mid
            + price_level[:, None]
            + stor_price
            + summed_hours(dual_store, True)
        )
        stor_next = jnp.clip(stor_mid - TAU * stor_grad, -stor_rate, stor_rate)
        gen_bar = 2.0 * gen_next - gen_now
        stor_bar = 2.0 * stor_next - stor_now
        balance = jnp.sum(gen_bar, axis=1) + jnp.sum(stor_bar, axis=1) - load_total
        bar_low = jnp.concatenate([gen_bar, stor_bar], axis=1).astype(jnp.bfloat16)
        flow_other = lax.dot_general(
            weight_other, bar_low, contract_minor, preferred_element_type=jnp.float32
        )
        flow_own = lax.dot_general(
            weight_own, bar_low, contract_minor, preferred_element_type=jnp.float32
        )
        flow_part = flow_own + swapped(flow_other) - load_flow
        balance = balance + swapped(balance)
        high = rounded(balance)
        lanes = row_count // 3
        tail = jnp.concatenate(
            [
                high.reshape(3, lanes),
                (balance - high).reshape(3, lanes),
                jnp.zeros((share_len - 6, lanes), jnp.float32),
            ],
            axis=0,
        )
        sent = jnp.concatenate(
            [
                flow_part.reshape(chip_count, share_len, row_count),
                jnp.broadcast_to(tail[None], (chip_count, share_len, lanes)),
            ],
            axis=2,
        ).astype(jnp.bfloat16)
        received = lax.all_to_all(sent, CHIPS, 0, 0, tiled=True)
        summed = jnp.sum(received.astype(jnp.float32), axis=0)
        flow_share = summed[:, :row_count]
        balance = (summed[:3, row_count:] + summed[3:6, row_count:]).reshape(row_count)
        dual_flow = dual_step(dual_flow, flow_share, SIGMA_FLOW, -limit, limit)
        if iteration == 0:
            dual_own, dual_other = gathered_duals(dual_flow)
        price_level = price_level + KAPPA / total_units * balance
        dual_store = dual_step(
            dual_store, summed_hours(stor_bar, False), SIGMA_STORE, low_bound, high_bound
        )
        gen_old, stor_old = (gen_now, stor_now)
        gen_now, stor_now = (gen_next, stor_next)
    return (gen_now, stor_now, price_level, dual_flow.T, dual_store)


def solution(mesh):
    fine = Mesh(
        mesh.devices.reshape(mesh.shape["lines"], Z, X, CORES), ("lines", "z", "x", "core")
    )
    by_area = P(AREAS)
    by_column = P(None, AREAS)
    return jax.shard_map(
        shards,
        mesh=fine,
        in_specs=(
            P("lines", AREAS),
            by_column,
            P(),
            P("lines"),
            by_area,
            by_area,
            by_area,
            by_area,
            by_column,
            by_area,
            by_area,
            by_area,
            by_area,
            by_column,
            P(),
            P(None, ("lines", *AREAS)),
            by_column,
        ),
        out_specs=(by_column, by_column, P(), P(None, ("lines", *AREAS)), by_column),
        check_vma=False,
    )
```

profile of v0, /device:TPU:1, one launch (start us, length us, event | category | flops | bytes accessed | tf_op | source)
XLA Modules:
  0.0 208.4 jit_solution(17964249165999538123)
XLA Ops:
  2.6 13.0 %all-to-all-start = ((s32[64,1,8]{2,1,0:T(1,128)}), s32[64,1,8]{2,1,0:T(1,128)S(1)}, u32[]{:S(2)}, u32[]{:S(2)}) async-start(s32[64,1,8]{2,1,0:T(1,128)} %bitcast), calls=%async_computation | async-start | bytes 65536 | tf_op jit(solution)/shard_map/all_to_all | solution.py:108
  16.3 8.6 %all-to-all-done = s32[64,1,8]{2,1,0:T(1,128)S(1)} async-done(((s32[64,1,8]{2,1,0:T(1,128)}), s32[64,1,8]{2,1,0:T(1,128)S(1)}, u32[]{:S(2)}, u32[]{:S(2)}) %all-to-all-start) | async-done | bytes 2080 | tf_op jit(solution)/shard_map/all_to_all | solution.py:108
  25.6 4.6 %all-to-all-start.2 = ((bf16[32,16,384]{2,1,0:T(8,128)(2,1)}), bf16[32,16,384]{2,1,0:T(8,128)(2,1)}, u32[]{:S(2)}, u32[]{:S(2)}) async-start(bf16[32,16,384]{2,1,0:T(8,128)(2,1)} %broadcast_in_dim.86), calls=%async_computation.2 | async-start | bytes 786432 | tf_op jit(solution)/shard_map/all_to_all | solution.py:41
  31.6 2.5 %fusion.2 = bf16[64,8,1024]{2,1,0:T(8,128)(2,1)} fusion(bf16[1024,1280]{1,0:T(8,128)(2,1)S(1)} %copy-done, s32[512]{0:T(512)S(1)} %eq.141), kind=kOutput, calls=%fused_computation.4 | convolution fusion | flops 1343356928 | bytes 3672064 | tf_op jit(solution)/shard_map/dot_general | solution.py:117
  34.1 10.1 %all-to-all-done.2 = bf16[32,16,384]{2,1,0:T(8,128)(2,1)} async-done(((bf16[32,16,384]{2,1,0:T(8,128)(2,1)}), bf16[32,16,384]{2,1,0:T(8,128)(2,1)}, u32[]{:S(2)}, u32[]{:S(2)}) %all-to-all-start.2) | async-done | bytes 393248 | tf_op jit(solution)/shard_map/all_to_all | solution.py:41
  44.2 7.1 %all-to-all-start.1 = ((bf16[64,8,1024]{2,1,0:T(8,128)(2,1)}), bf16[64,8,1024]{2,1,0:T(8,128)(2,1)}, u32[]{:S(2)}, u32[]{:S(2)}) async-start(bf16[64,8,1024]{2,1,0:T(8,128)(2,1)} %fusion.2), calls=%async_computation.1 | async-start | bytes 2097152 | tf_op jit(solution)/shard_map/all_to_all | solution.py:120
  51.3 3.1 %fusion.12 = f32[1024,384]{1,0:T(8,128)S(1)} fusion(bf16[1024,1280]{1,0:T(8,128)(2,1)S(1)} %copy-done, f32[384,1280]{1,0:T(8,128)} %param.18), kind=kOutput, calls=%fused_computation.24 | convolution fusion | flops 1007124480 | bytes 6160384 | tf_op jit(solution)/shard_map/dot_general | solution.py:138
  57.3 1.7 reduce_sum.85
  60.0 1.7 fusion.8
  61.7 17.9 %all-to-all-done.1 = bf16[64,8,1024]{2,1,0:T(8,128)(2,1)} async-done(((bf16[64,8,1024]{2,1,0:T(8,128)(2,1)}), bf16[64,8,1024]{2,1,0:T(8,128)(2,1)}, u32[]{:S(2)}, u32[]{:S(2)}) %all-to-all-start.1) | async-done | bytes 1048608 | tf_op jit(solution)/shard_map/all_to_all | solution.py:120
  79.5 1.7 convolution_convert_fusion
  87.6 2.8 %collective-permute-start.3 = (bf16[384,384]{0,1:T(8,128)(2,1)S(1)}, bf16[384,384]{0,1:T(8,128)(2,1)S(1)}, u32[]{:S(2)}, u32[]{:S(2)}) collective-permute-start(bf16[384,384]{0,1:T(8,128)(2,1)S(1)} %convert_bitcast_fusion), channel_id=1, source_target_pairs={{0,192},{64,0},{128,64},{192,128},{1,193},{65,1},{129,65},{193,129... | collective-permute-start | bytes 884744 | tf_op jit(solution)/shard_map/ppermute | solution.py:32
  90.4 1.6 collective-permute-start.1
  92.1 4.6 %collective-permute-done.3 = bf16[384,384]{0,1:T(8,128)(2,1)S(1)} collective-permute-done((bf16[384,384]{0,1:T(8,128)(2,1)S(1)}, bf16[384,384]{0,1:T(8,128)(2,1)S(1)}, u32[]{:S(2)}, u32[]{:S(2)}) %collective-permute-start.3) | collective-permute-done | bytes 294944 | tf_op jit(solution)/shard_map/ppermute | solution.py:32
  96.7 3.1 %collective-permute-done.2 = bf16[384,384]{0,1:T(8,128)(2,1)S(1)} collective-permute-done((bf16[384,384]{0,1:T(8,128)(2,1)S(1)}, bf16[384,384]{0,1:T(8,128)(2,1)S(1)}, u32[]{:S(2)}, u32[]{:S(2)}) %collective-permute-start.2) | collective-permute-done | bytes 294944 | tf_op jit(solution)/shard_map/ppermute | solution.py:32
  99.8 4.3 %collective-permute-done.1 = bf16[384,384]{0,1:T(8,128)(2,1)S(1)} collective-permute-done((bf16[384,384]{0,1:T(8,128)(2,1)S(1)}, bf16[384,384]{0,1:T(8,128)(2,1)S(1)}, u32[]{:S(2)}, u32[]{:S(2)}) %collective-permute-start.1) | collective-permute-done | bytes 294944 | tf_op jit(solution)/shard_map/ppermute | solution.py:32
  104.6 1.5 fusion.110
  106.5 3.3 %collective-permute-start.4 = (f32[512,384]{1,0:T(8,128)S(1)}, f32[512,384]{1,0:T(8,128)S(1)}, u32[]{:S(2)}, u32[]{:S(2)}) collective-permute-start(f32[512,384]{1,0:T(8,128)S(1)} %fusion.67), channel_id=1, source_target_pairs={{0,1},{1,0},{2,3},{3,2},{4,5},{5,4},{6,7},{7,6},{8,9},{9,8},{10,11... | collective-permute-start | bytes 2359304 | tf_op jit(solution)/shard_map/ppermute | solution.py:26
  113.4 5.0 %all-to-all-start.3 = ((bf16[32,16,512]{2,1,0:T(8,128)(2,1)}), bf16[32,16,512]{2,1,0:T(8,128)(2,1)}, u32[]{:S(2)}, u32[]{:S(2)}) async-start(bf16[32,16,512]{2,1,0:T(8,128)(2,1)} %pad_maximum_fusion.1), calls=%async_computation.3 | async-start | bytes 1048576 | tf_op jit(solution)/shard_map/all_to_all | solution.py:205
  121.1 13.9 %all-to-all-done.3 = bf16[32,16,512]{2,1,0:T(8,128)(2,1)} async-done(((bf16[32,16,512]{2,1,0:T(8,128)(2,1)}), bf16[32,16,512]{2,1,0:T(8,128)(2,1)}, u32[]{:S(2)}, u32[]{:S(2)}) %all-to-all-start.3) | async-done | bytes 524320 | tf_op jit(solution)/shard_map/all_to_all | solution.py:205
  137.0 17.7 %all_to_all.38 = bf16[32,16,384]{2,1,0:T(8,128)(2,1)} all-to-all(bf16[32,16,384]{2,1,0:T(8,128)(2,1)S(1)} %broadcast_in_dim.91), channel_id=1, replica_groups=mesh['lines'=4,'z'=8,'x'=4,'core'=2] {'z','x'}, dimensions={0} | all-to-all | bytes 786432 | tf_op jit(solution)/shard_map/all_to_all | solution.py:41
  154.7 3.4 %collective-permute-start.7 = (bf16[512,384]{1,0:T(8,128)(2,1)}, bf16[512,384]{1,0:T(8,128)(2,1)}, u32[]{:S(2)}, u32[]{:S(2)}) collective-permute-start(bf16[512,384]{1,0:T(8,128)(2,1)} %bitcast.18), channel_id=1, source_target_pairs={{0,1},{1,0},{2,3},{3,2},{4,5},{5,4},{6,7},{7,6},{8,9},{9,8},{10,11... | collective-permute-start | bytes 1179656 | tf_op jit(solution)/shard_map/ppermute | solution.py:26
  158.7 1.7 copy.86
  166.2 5.9 %collective-permute-done.10 = bf16[384,384]{0,1:T(8,128)(2,1)S(1)} collective-permute-done((bf16[384,384]{0,1:T(8,128)(2,1)S(1)}, bf16[384,384]{0,1:T(8,128)(2,1)S(1)}, u32[]{:S(2)}, u32[]{:S(2)}) %collective-permute-start.10) | collective-permute-done | bytes 294944 | tf_op jit(solution)/shard_map/ppermute | solution.py:32
  172.1 7.4 %collective-permute-done.9 = bf16[384,384]{0,1:T(8,128)(2,1)S(1)} collective-permute-done((bf16[384,384]{0,1:T(8,128)(2,1)S(1)}, bf16[384,384]{0,1:T(8,128)(2,1)S(1)}, u32[]{:S(2)}, u32[]{:S(2)}) %collective-permute-start.9) | collective-permute-done | bytes 294944 | tf_op jit(solution)/shard_map/ppermute | solution.py:32
  180.0 1.5 fusion.112
  183.2 1.7 collective-permute-done.12
  186.4 4.0 %all-to-all-start.5 = ((bf16[32,16,512]{2,1,0:T(8,128)(2,1)}), bf16[32,16,512]{2,1,0:T(8,128)(2,1)S(1)}, u32[]{:S(2)}, u32[]{:S(2)}) async-start(bf16[32,16,512]{2,1,0:T(8,128)(2,1)} %pad_maximum_fusion.2), calls=%async_computation.5 | async-start | bytes 1048576 | tf_op jit(solution)/shard_map/all_to_all | solution.py:205
  190.4 1.9 copy.88
  193.1 2.5 %fusion.51 = f32[384,128]{0,1:T(8,128)} fusion(f32[384,128]{0,1:T(8,128)} %copy-done.37, s32[384]{0:T(512)S(1)} %copy-done.24, f32[128]{0:T(128)S(1)} %get-tuple-element.46, f32[128]{0:T(128)S(1)} %get-tuple-element.45, pred[384]{0:T(512)(128)(4,1)S(1)} %fusion.80, f32[384,128]{0,1:T(8,128)} %get-tuple-element.47, f32[384,128]{0,1:T(8,128)S(1)} %copy-done.16), kind=kOutput, calls=%fused_computation.90 | convolution fusion | flops 227622912 | bytes 789376 | tf_op jit(solution)/shard_map/dot_general | solution.py:57
  195.7 1.7 copy.90
  197.4 9.6 %all-to-all-done.5 = bf16[32,16,512]{2,1,0:T(8,128)(2,1)S(1)} async-done(((bf16[32,16,512]{2,1,0:T(8,128)(2,1)}), bf16[32,16,512]{2,1,0:T(8,128)(2,1)S(1)}, u32[]{:S(2)}, u32[]{:S(2)}) %all-to-all-start.5) | async-done | bytes 524320 | tf_op jit(solution)/shard_map/all_to_all | solution.py:205
  (156 shorter events, 35.8 us)
Async XLA Ops:
  0.6 31.0 %copy-start = (bf16[1024,1280]{1,0:T(8,128)(2,1)S(1)}, bf16[1024,1280]{1,0:T(8,128)(2,1)}, u32[]{:S(2)}) copy-start(bf16[1024,1280]{1,0:T(8,128)(2,1)} %param.17) | copy-start | bytes 7864324
  2.6 22.3 %all-to-all-start = ((s32[64,1,8]{2,1,0:T(1,128)}), s32[64,1,8]{2,1,0:T(1,128)S(1)}, u32[]{:S(2)}, u32[]{:S(2)}) async-start(s32[64,1,8]{2,1,0:T(1,128)} %bitcast), calls=%async_computation | async-start | bytes 65536 | tf_op jit(solution)/shard_map/all_to_all | solution.py:108
  25.6 18.6 %all-to-all-start.2 = ((bf16[32,16,384]{2,1,0:T(8,128)(2,1)}), bf16[32,16,384]{2,1,0:T(8,128)(2,1)}, u32[]{:S(2)}, u32[]{:S(2)}) async-start(bf16[32,16,384]{2,1,0:T(8,128)(2,1)} %broadcast_in_dim.86), calls=%async_computation.2 | async-start | bytes 786432 | tf_op jit(solution)/shard_map/all_to_all | solution.py:41
  44.2 35.3 %all-to-all-start.1 = ((bf16[64,8,1024]{2,1,0:T(8,128)(2,1)}), bf16[64,8,1024]{2,1,0:T(8,128)(2,1)}, u32[]{:S(2)}, u32[]{:S(2)}) async-start(bf16[64,8,1024]{2,1,0:T(8,128)(2,1)} %fusion.2), calls=%async_computation.1 | async-start | bytes 2097152 | tf_op jit(solution)/shard_map/all_to_all | solution.py:120
  55.8 54.3 %collective-permute-start.5 = (f32[512,384]{1,0:T(8,128)}, f32[512,384]{1,0:T(8,128)}, u32[]{:S(2)}, u32[]{:S(2)}) collective-permute-start(f32[512,384]{1,0:T(8,128)} %bitcast.13), channel_id=1, source_target_pairs={{0,1},{1,0},{2,3},{3,2},{4,5},{5,4},{6,7},{7,6},{8,9},{9,8},{10,11... | collective-permute-start | bytes 2359304 | tf_op jit(solution)/shard_map/ppermute | solution.py:26
  59.8 44.7 %copy-start.32 = (f32[128]{0:T(128)}, f32[128]{0:T(128)S(1)}, u32[]{:S(2)}) copy-start(f32[128]{0:T(128)S(1)} %neg.15) | copy-start | bytes 1540
  59.9 51.8 %copy-start.25 = (bf16[16]{0:T(256)(128)(2,1)}, bf16[16]{0:T(256)(128)(2,1)S(1)}, u32[]{:S(2)}) copy-start(bf16[16]{0:T(256)(128)(2,1)S(1)} %pad.11.clone) | copy-start | bytes 100
  59.9 44.6 %copy-start.34 = (f32[128]{0:T(128)}, f32[128]{0:T(128)S(1)}, u32[]{:S(2)}) copy-start(f32[128]{0:T(128)S(1)} %broadcast_multiply_fusion.2) | copy-start | bytes 1540
  61.7 24.4 %collective-permute-start = (bf16[512,384]{1,0:T(8,128)(2,1)}, bf16[512,384]{1,0:T(8,128)(2,1)}, u32[]{:S(2)}, u32[]{:S(2)}) collective-permute-start(bf16[512,384]{1,0:T(8,128)(2,1)} %bitcast.7), channel_id=1, source_target_pairs={{0,1},{1,0},{2,3},{3,2},{4,5},{5,4},{6,7},{7,6},{8,9},{9,8},{10,11... | collective-permute-start | bytes 1179656 | tf_op jit(solution)/shard_map/ppermute | solution.py:26
  86.0 18.2 %copy-start.3 = (f32[384,256]{0,1:T(8,128)S(1)}, f32[384,256]{0,1:T(8,128)}, u32[]{:S(2)}) copy-start(f32[384,256]{0,1:T(8,128)} %copy.76) | copy-start | bytes 1179652
  86.1 18.2 %copy-start.18 = (f32[384]{0:T(512)S(1)}, f32[384]{0:T(512)}, u32[]{:S(2)}) copy-start(f32[384]{0:T(512)} %param.31) | copy-start | bytes 4612
  86.1 18.2 %copy-start.19 = (f32[256]{0:T(256)S(1)}, f32[256]{0:T(256)}, u32[]{:S(2)}) copy-start(f32[256]{0:T(256)} %param.23) | copy-start | bytes 3076
  86.1 18.2 %copy-start.21 = (f32[256]{0:T(256)S(1)}, f32[256]{0:T(256)}, u32[]{:S(2)}) copy-start(f32[256]{0:T(256)} %param.24) | copy-start | bytes 3076
  87.6 9.1 %collective-permute-start.3 = (bf16[384,384]{0,1:T(8,128)(2,1)S(1)}, bf16[384,384]{0,1:T(8,128)(2,1)S(1)}, u32[]{:S(2)}, u32[]{:S(2)}) collective-permute-start(bf16[384,384]{0,1:T(8,128)(2,1)S(1)} %convert_bitcast_fusion), channel_id=1, source_target_pairs={{0,192},{64,0},{128,64},{192,128},{1,193},{65,1},{129,65},{193,129... | collective-permute-start | bytes 884744 | tf_op jit(solution)/shard_map/ppermute | solution.py:32
  90.4 9.4 %collective-permute-start.2 = (bf16[384,384]{0,1:T(8,128)(2,1)S(1)}, bf16[384,384]{0,1:T(8,128)(2,1)S(1)}, u32[]{:S(2)}, u32[]{:S(2)}) collective-permute-start(bf16[384,384]{0,1:T(8,128)(2,1)S(1)} %convert_bitcast_fusion), channel_id=1, source_target_pairs={{0,64},{64,128},{128,192},{192,0},{1,65},{65,129},{129,193},{193,1... | collective-permute-start | bytes 884744 | tf_op jit(solution)/shard_map/ppermute | solution.py:32
  90.4 13.7 %collective-permute-start.1 = (bf16[384,384]{0,1:T(8,128)(2,1)S(1)}, bf16[384,384]{0,1:T(8,128)(2,1)S(1)}, u32[]{:S(2)}, u32[]{:S(2)}) collective-permute-start(bf16[384,384]{0,1:T(8,128)(2,1)S(1)} %convert_bitcast_fusion), channel_id=1, source_target_pairs={{0,128},{64,192},{128,0},{192,64},{1,129},{65,193},{129,1},{193,65... | collective-permute-start | bytes 884744 | tf_op jit(solution)/shard_map/ppermute | solution.py:32
  106.5 5.3 %collective-permute-start.4 = (f32[512,384]{1,0:T(8,128)S(1)}, f32[512,384]{1,0:T(8,128)S(1)}, u32[]{:S(2)}, u32[]{:S(2)}) collective-permute-start(f32[512,384]{1,0:T(8,128)S(1)} %fusion.67), channel_id=1, source_target_pairs={{0,1},{1,0},{2,3},{3,2},{4,5},{5,4},{6,7},{7,6},{8,9},{9,8},{10,11... | collective-permute-start | bytes 2359304 | tf_op jit(solution)/shard_map/ppermute | solution.py:26
  109.9 1.8 collective-permute-start.6
  113.4 21.6 %all-to-all-start.3 = ((bf16[32,16,512]{2,1,0:T(8,128)(2,1)}), bf16[32,16,512]{2,1,0:T(8,128)(2,1)}, u32[]{:S(2)}, u32[]{:S(2)}) async-start(bf16[32,16,512]{2,1,0:T(8,128)(2,1)} %pad_maximum_fusion.1), calls=%async_computation.3 | async-start | bytes 1048576 | tf_op jit(solution)/shard_map/all_to_all | solution.py:205
  137.0 28.4 %copy-start.24 = (s32[384]{0:T(512)S(1)}, s32[384]{0:T(512)}, u32[]{:S(2)}) copy-start(s32[384]{0:T(512)} %copy-done.23) | copy-start | bytes 4612
  154.7 7.3 %collective-permute-start.7 = (bf16[512,384]{1,0:T(8,128)(2,1)}, bf16[512,384]{1,0:T(8,128)(2,1)}, u32[]{:S(2)}, u32[]{:S(2)}) collective-permute-start(bf16[512,384]{1,0:T(8,128)(2,1)} %bitcast.18), channel_id=1, source_target_pairs={{0,1},{1,0},{2,3},{3,2},{4,5},{5,4},{6,7},{7,6},{8,9},{9,8},{10,11... | collective-permute-start | bytes 1179656 | tf_op jit(solution)/shard_map/ppermute | solution.py:26
  161.9 17.8 %copy-start.4 = (f32[384,256]{0,1:T(8,128)S(1)}, f32[384,256]{0,1:T(8,128)}, u32[]{:S(2)}) copy-start(f32[384,256]{0,1:T(8,128)} %copy.76) | copy-start | bytes 1179652
  162.0 17.8 %copy-start.6 = (f32[384,256]{0,1:T(8,128)S(1)}, f32[384,256]{0,1:T(8,128)}, u32[]{:S(2)}) copy-start(f32[384,256]{0,1:T(8,128)} %copy-done.5) | copy-start | bytes 1179652
  162.0 17.8 %copy-start.20 = (f32[256]{0:T(256)S(1)}, f32[256]{0:T(256)}, u32[]{:S(2)}) copy-start(f32[256]{0:T(256)} %param.23) | copy-start | bytes 3076
  162.0 17.7 %copy-start.22 = (f32[256]{0:T(256)S(1)}, f32[256]{0:T(256)}, u32[]{:S(2)}) copy-start(f32[256]{0:T(256)} %param.24) | copy-start | bytes 3076
  163.5 8.6 %collective-permute-start.10 = (bf16[384,384]{0,1:T(8,128)(2,1)S(1)}, bf16[384,384]{0,1:T(8,128)(2,1)S(1)}, u32[]{:S(2)}, u32[]{:S(2)}) collective-permute-start(bf16[384,384]{0,1:T(8,128)(2,1)S(1)} %get-tuple-element.48), channel_id=1, source_target_pairs={{0,192},{64,0},{128,64},{192,128},{1,193},{65,1},{129,65},{193,129... | collective-permute-start | bytes 884744 | tf_op jit(solution)/shard_map/ppermute | solution.py:32
  163.6 16.0 %collective-permute-start.9 = (bf16[384,384]{0,1:T(8,128)(2,1)S(1)}, bf16[384,384]{0,1:T(8,128)(2,1)S(1)}, u32[]{:S(2)}, u32[]{:S(2)}) collective-permute-start(bf16[384,384]{0,1:T(8,128)(2,1)S(1)} %get-tuple-element.48), channel_id=1, source_target_pairs={{0,64},{64,128},{128,192},{192,0},{1,65},{65,129},{129,193},{193,1... | collective-permute-start | bytes 884744 | tf_op jit(solution)/shard_map/ppermute | solution.py:32
  165.0 14.5 %collective-permute-start.8 = (bf16[384,384]{0,1:T(8,128)(2,1)S(1)}, bf16[384,384]{0,1:T(8,128)(2,1)S(1)}, u32[]{:S(2)}, u32[]{:S(2)}) collective-permute-start(bf16[384,384]{0,1:T(8,128)(2,1)S(1)} %get-tuple-element.48), channel_id=1, source_target_pairs={{0,128},{64,192},{128,0},{192,64},{1,129},{65,193},{129,1},{193,65... | collective-permute-start | bytes 884744 | tf_op jit(solution)/shard_map/ppermute | solution.py:32
  181.9 3.2 %collective-permute-start.11 = (f32[512,384]{1,0:T(8,128)S(1)}, f32[512,384]{1,0:T(8,128)S(1)}, u32[]{:S(2)}, u32[]{:S(2)}) collective-permute-start(f32[512,384]{1,0:T(8,128)S(1)} %fusion.66), channel_id=1, source_target_pairs={{0,1},{1,0},{2,3},{3,2},{4,5},{5,4},{6,7},{7,6},{8,9},{9,8},{10,11... | collective-permute-start | bytes 2359304 | tf_op jit(solution)/shard_map/ppermute | solution.py:26
  183.1 1.8 collective-permute-start.12
  185.5 22.2 %copy-start.11 = (f32[384,16]{0,1:T(8,128)S(1)}, f32[384,16]{0,1:T(8,128)}, u32[]{:S(2)}) copy-start(f32[384,16]{0,1:T(8,128)} %param.32) | copy-start | bytes 73732
  186.4 20.7 %all-to-all-start.5 = ((bf16[32,16,512]{2,1,0:T(8,128)(2,1)}), bf16[32,16,512]{2,1,0:T(8,128)(2,1)S(1)}, u32[]{:S(2)}, u32[]{:S(2)}) async-start(bf16[32,16,512]{2,1,0:T(8,128)(2,1)} %pad_maximum_fusion.2), calls=%async_computation.5 | async-start | bytes 1048576 | tf_op jit(solution)/shard_map/all_to_all | solution.py:205
  (24 other events, 197.3 us)
where the time goes:
time: 210 us; the launch traced here: 208 us
  waiting for transfers between devices  87.6 us (42%)
  starting transfers between devices  48.7 us (23%)
  matrix products  22.6 us (11%)
  blocking collectives  17.7 us (8%)
  local copies, waits for them, and re-layouts  15.5 us (7%)
  other arithmetic  14.9 us (7%)
    ppermute x6, waiting for transfers between devices, sum_over_lines(): lax.ppermute(low, 'lines', [(i, (i + s) % 4) for i in range(4)])  25.4 us
    all_to_all x2, waiting for transfers between devices, shards(): received = lax.all_to_all(sent, CHIPS, 0, 0, tiled=True)  23.5 us
    all_to_all x1, waiting for transfers between devices, shards(): columns = lax.all_to_all(sent_columns, AREAS, 0, 0, tiled=True)  17.9 us
    all_to_all x1, blocking collectives, sent_to_chips(): return lax.all_to_all(sent, CHIPS, 0, 0, tiled=True)  17.7 us
    all_to_all x1, starting transfers between devices, shards(): lax.all_to_all(slot_bus.reshape(area_count, slots), AREAS, 0, 0, tiled=True)  13 us
    all_to_all x1, waiting for transfers between devices, sent_to_chips(): return lax.all_to_all(sent, CHIPS, 0, 0, tiled=True)  10.1 us
    all_to_all x2, starting transfers between devices, shards(): received = lax.all_to_all(sent, CHIPS, 0, 0, tiled=True)  9 us
    ppermute x7, starting transfers between devices, swapped(): return lax.ppermute(x, 'core', [(0, 1), (1, 0)])  8.71 us
  transfers between devices with their start and end apart: 18, of which 12 were waited for; matrix products, arithmetic and copies ran while one was open for 19% of the time, Pallas kernels for 0%

commit v1 on v0

--- a/solution.py
+++ b/solution.py
@@ -43,6 +43,25 @@
 
 def gathered_duals(share):
     own = sent_to_chips(share.astype(jnp.bfloat16)).reshape(-1, share.shape[1])
+    return own, swapped(own)
+
+
+def doubled(x, axis, size, step, dim):
+    other = lax.ppermute(x, axis, [(i, i ^ step) for i in range(size)])
+    first = (lax.axis_index(axis) // step) % 2 == 0
+    return jnp.where(
+        first, jnp.concatenate([x, other], axis=dim), jnp.concatenate([other, x], axis=dim)
+    )
+
+
+def gathered_early(share):
+    share_len, row_count = share.shape
+    held = share.astype(jnp.bfloat16).reshape(1, 1, share_len, row_count)
+    for step in (1, 2, 4):
+        held = doubled(held, "z", Z, step, 0)
+    for step in (1, 2):
+        held = doubled(held, "x", X, step, 1)
+    own = held.reshape(-1, row_count)
     return own, swapped(own)
 
 
@@ -108,7 +127,7 @@
     wanted = lax.all_to_all(slot_bus.reshape(area_count, slots), AREAS, 0, 0, tiled=True)
 
     dual_flow = mu_start.T
-    dual_own, dual_other = gathered_duals(dual_flow)
+    dual_own, dual_other = gathered_early(dual_flow)
 
     bus_ids = jnp.arange(bus_count, dtype=jnp.int32)
     sel_gen = (wanted.reshape(-1)[:, None] == bus_ids[None, :]).astype(jnp.bfloat16)

time: 210 us -> 218 us (1.038)
  starting transfers between devices: 48.7 us -> 60.5 us
  waiting for transfers between devices: 87.6 us -> 83.5 us
    ppermute x0 -> x5, waiting for transfers between devices: none -> 23.1 us  [doubled(): other = lax.ppermute(x, axis, [(i, i ^ step) for i in range(size)])]
    all_to_all x1, waiting for transfers between devices: 17.9 us -> 0.01 us  [shards(): columns = lax.all_to_all(sent_columns, AREAS, 0, 0, tiled=True)]
    ppermute x0 -> x5, starting transfers between devices: none -> 12.1 us  [doubled(): other = lax.ppermute(x, axis, [(i, i ^ step) for i in range(size)])]
    all_to_all x1 -> x0, waiting for transfers between devices: 10.1 us -> none  [sent_to_chips(): return lax.all_to_all(sent, CHIPS, 0, 0, tiled=True)]
    all_to_all x1 -> x0, starting transfers between devices: 4.59 us -> none  [sent_to_chips(): return lax.all_to_all(sent, CHIPS, 0, 0, tiled=True)]
    all_to_all x2, starting transfers between devices: 9 us -> 12.4 us  [shards(): received = lax.all_to_all(sent, CHIPS, 0, 0, tiled=True)]
    ppermute x7, starting transfers between devices: 8.71 us -> 11 us  [swapped(): return lax.ppermute(x, 'core', [(0, 1), (1, 0)])]
  transfers between devices with their start and end apart: 18 -> 22, of which waited for: 12 -> 12; matrix products, arithmetic and copies ran while one was open for 19% -> 19% of each run, Pallas kernels for 0% -> 0%
where the time goes in v1:
time: 218 us; the launch traced here: 216 us
  waiting for transfers between devices  83.5 us (38%)
  starting transfers between devices  60.5 us (28%)
  matrix products  22.8 us (10%)
  blocking collectives  17.7 us (8%)
  other arithmetic  15.9 us (7%)
  local copies, waits for them, and re-layouts  14.7 us (7%)
    ppermute x6, waiting for transfers between devices, sum_over_lines(): lax.ppermute(low, 'lines', [(i, (i + s) % 4) for i in range(4)])  27.5 us
    all_to_all x2, waiting for transfers between devices, shards(): received = lax.all_to_all(sent, CHIPS, 0, 0, tiled=True)  23.5 us
    ppermute x5, waiting for transfers between devices, doubled(): other = lax.ppermute(x, axis, [(i, i ^ step) for i in range(size)])  23.1 us
    all_to_all x1, blocking collectives, sent_to_chips(): return lax.all_to_all(sent, CHIPS, 0, 0, tiled=True)  17.7 us
    all_to_all x1, starting transfers between devices, shards(): lax.all_to_all(slot_bus.reshape(area_count, slots), AREAS, 0, 0, tiled=True)  13 us
    all_to_all x2, starting transfers between devices, shards(): received = lax.all_to_all(sent, CHIPS, 0, 0, tiled=True)  12.4 us
    ppermute x5, starting transfers between devices, doubled(): other = lax.ppermute(x, axis, [(i, i ^ step) for i in range(size)])  12.1 us
    ppermute x7, starting transfers between devices, swapped(): return lax.ppermute(x, 'core', [(0, 1), (1, 0)])  11 us
  transfers between devices with their start and end apart: 22, of which 12 were waited for; matrix products, arithmetic and copies ran while one was open for 19% of the time, Pallas kernels for 0%

profile of v1, /device:TPU:1, one launch (start us, length us, event | category | flops | bytes accessed | tf_op | source)
XLA Modules:
  0.0 216.4 jit_solution(13224243964772058085)
XLA Ops:
  2.6 13.0 %all-to-all-start = ((s32[64,1,8]{2,1,0:T(1,128)}), s32[64,1,8]{2,1,0:T(1,128)S(1)}, u32[]{:S(2)}, u32[]{:S(2)}) async-start(s32[64,1,8]{2,1,0:T(1,128)} %bitcast.11), calls=%async_computation | async-start | bytes 65536 | tf_op jit(solution)/shard_map/all_to_all | solution.py:127
  17.6 7.2 %all-to-all-done = s32[64,1,8]{2,1,0:T(1,128)S(1)} async-done(((s32[64,1,8]{2,1,0:T(1,128)}), s32[64,1,8]{2,1,0:T(1,128)S(1)}, u32[]{:S(2)}, u32[]{:S(2)}) %all-to-all-start) | async-done | bytes 2080 | tf_op jit(solution)/shard_map/all_to_all | solution.py:127
  26.2 2.6 %fusion.2 = bf16[64,8,1024]{2,1,0:T(8,128)(2,1)} fusion(bf16[1024,1280]{1,0:T(8,128)(2,1)S(1)} %copy-done, s32[512]{0:T(512)S(1)} %eq.167), kind=kOutput, calls=%fused_computation.4 | convolution fusion | flops 1343356928 | bytes 3672064 | tf_op jit(solution)/shard_map/dot_general | solution.py:136
  28.8 5.5 %all-to-all-start.1 = ((bf16[64,8,1024]{2,1,0:T(8,128)(2,1)}), bf16[64,8,1024]{2,1,0:T(8,128)(2,1)}, u32[]{:S(2)}, u32[]{:S(2)}) async-start(bf16[64,8,1024]{2,1,0:T(8,128)(2,1)} %fusion.2), calls=%async_computation.1 | async-start | bytes 2097152 | tf_op jit(solution)/shard_map/all_to_all | solution.py:139
  34.3 3.1 %fusion.12 = f32[1024,384]{1,0:T(8,128)S(1)} fusion(bf16[1024,1280]{1,0:T(8,128)(2,1)S(1)} %copy-done, f32[384,1280]{1,0:T(8,128)} %param.18), kind=kOutput, calls=%fused_computation.24 | convolution fusion | flops 1007124480 | bytes 6160384 | tf_op jit(solution)/shard_map/dot_general | solution.py:157
  39.4 2.2 %collective-permute-start.1 = (bf16[2,1,16,384]{3,2,1,0:T(8,128)(2,1)S(1)}, bf16[2,1,16,384]{3,2,1,0:T(8,128)(2,1)S(1)}, u32[]{:S(2)}, u32[]{:S(2)}) collective-permute-start(bf16[2,1,16,384]{3,2,1,0:T(8,128)(2,1)S(1)} %maximum_select_fusion.5), channel_id=1, source_target_pairs={{0,16},{8,24},{16,0},{24,8},{32,48},{40,56},{48,32},{56,40},{1,17}... | collective-permute-start | bytes 73736 | tf_op jit(solution)/shard_map/ppermute | solution.py:50
  41.6 17.3 %collective-permute-done.1 = bf16[2,1,16,384]{3,2,1,0:T(8,128)(2,1)S(1)} collective-permute-done((bf16[2,1,16,384]{3,2,1,0:T(8,128)(2,1)S(1)}, bf16[2,1,16,384]{3,2,1,0:T(8,128)(2,1)S(1)}, u32[]{:S(2)}, u32[]{:S(2)}) %collective-permute-start.1) | collective-permute-done | bytes 24608 | tf_op jit(solution)/shard_map/ppermute | solution.py:50
  58.9 5.2 %collective-permute-start.2 = (bf16[4,1,16,384]{3,2,1,0:T(8,128)(2,1)S(1)}, bf16[4,1,16,384]{3,2,1,0:T(8,128)(2,1)S(1)}, u32[]{:S(2)}, u32[]{:S(2)}) collective-permute-start(bf16[4,1,16,384]{3,2,1,0:T(8,128)(2,1)S(1)} %fusion.72), channel_id=1, source_target_pairs={{0,32},{8,40},{16,48},{24,56},{32,0},{40,8},{48,16},{56,24},{1,33}... | collective-permute-start | bytes 147464 | tf_op jit(solution)/shard_map/ppermute | solution.py:50
  64.2 1.7 collective-permute-done.2
  67.2 1.7 fusion.8
  69.9 1.7 reduce_sum.85
  72.5 2.0 collective-permute-start.4
  74.5 4.1 %collective-permute-done.4 = bf16[8,2,16,384]{3,2,1,0:T(8,128)(2,1)S(1)} collective-permute-done((bf16[8,2,16,384]{3,2,1,0:T(8,128)(2,1)S(1)}, bf16[8,2,16,384]{3,2,1,0:T(8,128)(2,1)S(1)}, u32[]{:S(2)}, u32[]{:S(2)}) %collective-permute-start.4) | collective-permute-done | bytes 196640 | tf_op jit(solution)/shard_map/ppermute | solution.py:50
  79.5 4.2 %collective-permute-start.5 = (bf16[512,384]{1,0:T(8,128)(2,1)}, bf16[512,384]{1,0:T(8,128)(2,1)}, u32[]{:S(2)}, u32[]{:S(2)}) collective-permute-start(bf16[512,384]{1,0:T(8,128)(2,1)} %bitcast.10), channel_id=1, source_target_pairs={{0,1},{1,0},{2,3},{3,2},{4,5},{5,4},{6,7},{7,6},{8,9},{9,8},{10,11... | collective-permute-start | bytes 1179656 | tf_op jit(solution)/shard_map/ppermute | solution.py:26
  83.6 1.7 convolution_convert_fusion
  91.8 3.0 %collective-permute-start.8 = (bf16[384,384]{0,1:T(8,128)(2,1)S(1)}, bf16[384,384]{0,1:T(8,128)(2,1)S(1)}, u32[]{:S(2)}, u32[]{:S(2)}) collective-permute-start(bf16[384,384]{0,1:T(8,128)(2,1)S(1)} %get-tuple-element.49), channel_id=1, source_target_pairs={{0,192},{64,0},{128,64},{192,128},{1,193},{65,1},{129,65},{193,129... | collective-permute-start | bytes 884744 | tf_op jit(solution)/shard_map/ppermute | solution.py:32
  94.8 1.6 collective-permute-start.6
  96.4 10.9 %collective-permute-done.8 = bf16[384,384]{0,1:T(8,128)(2,1)S(1)} collective-permute-done((bf16[384,384]{0,1:T(8,128)(2,1)S(1)}, bf16[384,384]{0,1:T(8,128)(2,1)S(1)}, u32[]{:S(2)}, u32[]{:S(2)}) %collective-permute-start.8) | collective-permute-done | bytes 294944 | tf_op jit(solution)/shard_map/ppermute | solution.py:32
  107.3 3.3 %collective-permute-done.7 = bf16[384,384]{0,1:T(8,128)(2,1)S(1)} collective-permute-done((bf16[384,384]{0,1:T(8,128)(2,1)S(1)}, bf16[384,384]{0,1:T(8,128)(2,1)S(1)}, u32[]{:S(2)}, u32[]{:S(2)}) %collective-permute-start.7) | collective-permute-done | bytes 294944 | tf_op jit(solution)/shard_map/ppermute | solution.py:32
  117.8 8.4 %all-to-all-start.2 = ((bf16[32,16,512]{2,1,0:T(8,128)(2,1)}), bf16[32,16,512]{2,1,0:T(8,128)(2,1)}, u32[]{:S(2)}, u32[]{:S(2)}) async-start(bf16[32,16,512]{2,1,0:T(8,128)(2,1)} %pad_maximum_fusion.1), calls=%async_computation.2 | async-start | bytes 1048576 | tf_op jit(solution)/shard_map/all_to_all | solution.py:224
  128.9 13.9 %all-to-all-done.2 = bf16[32,16,512]{2,1,0:T(8,128)(2,1)} async-done(((bf16[32,16,512]{2,1,0:T(8,128)(2,1)}), bf16[32,16,512]{2,1,0:T(8,128)(2,1)}, u32[]{:S(2)}, u32[]{:S(2)}) %all-to-all-start.2) | async-done | bytes 524320 | tf_op jit(solution)/shard_map/all_to_all | solution.py:224
  144.8 17.7 %all_to_all.33 = bf16[32,16,384]{2,1,0:T(8,128)(2,1)} all-to-all(bf16[32,16,384]{2,1,0:T(8,128)(2,1)S(1)} %broadcast_in_dim.88), channel_id=1, replica_groups=mesh['lines'=4,'z'=8,'x'=4,'core'=2] {'z','x'}, dimensions={0} | all-to-all | bytes 786432 | tf_op jit(solution)/shard_map/all_to_all | solution.py:41
  162.5 3.4 %collective-permute-start.12 = (bf16[512,384]{1,0:T(8,128)(2,1)}, bf16[512,384]{1,0:T(8,128)(2,1)}, u32[]{:S(2)}, u32[]{:S(2)}) collective-permute-start(bf16[512,384]{1,0:T(8,128)(2,1)} %bitcast.25), channel_id=1, source_target_pairs={{0,1},{1,0},{2,3},{3,2},{4,5},{5,4},{6,7},{7,6},{8,9},{9,8},{10,11... | collective-permute-start | bytes 1179656 | tf_op jit(solution)/shard_map/ppermute | solution.py:26
  166.5 1.7 copy.98
  174.0 5.9 %collective-permute-done.15 = bf16[384,384]{0,1:T(8,128)(2,1)S(1)} collective-permute-done((bf16[384,384]{0,1:T(8,128)(2,1)S(1)}, bf16[384,384]{0,1:T(8,128)(2,1)S(1)}, u32[]{:S(2)}, u32[]{:S(2)}) %collective-permute-start.15) | collective-permute-done | bytes 294944 | tf_op jit(solution)/shard_map/ppermute | solution.py:32
  179.9 7.4 %collective-permute-done.14 = bf16[384,384]{0,1:T(8,128)(2,1)S(1)} collective-permute-done((bf16[384,384]{0,1:T(8,128)(2,1)S(1)}, bf16[384,384]{0,1:T(8,128)(2,1)S(1)}, u32[]{:S(2)}, u32[]{:S(2)}) %collective-permute-start.14) | collective-permute-done | bytes 294944 | tf_op jit(solution)/shard_map/ppermute | solution.py:32
  191.2 1.7 collective-permute-done.17
  194.4 4.0 %all-to-all-start.4 = ((bf16[32,16,512]{2,1,0:T(8,128)(2,1)}), bf16[32,16,512]{2,1,0:T(8,128)(2,1)S(1)}, u32[]{:S(2)}, u32[]{:S(2)}) async-start(bf16[32,16,512]{2,1,0:T(8,128)(2,1)} %pad_maximum_fusion.2), calls=%async_computation.4 | async-start | bytes 1048576 | tf_op jit(solution)/shard_map/all_to_all | solution.py:224
  198.4 1.9 copy.100
  201.2 2.5 %fusion.50 = f32[384,128]{0,1:T(8,128)} fusion(f32[384,128]{0,1:T(8,128)} %copy-done.37, s32[384]{0:T(512)S(1)} %copy-done.24, f32[128]{0:T(128)S(1)} %get-tuple-element.48, f32[128]{0:T(128)S(1)} %get-tuple-element.47, pred[384]{0:T(512)(128)(4,1)S(1)} %fusion.83, f32[384,128]{0,1:T(8,128)} %get-tuple-element.51, f32[384,128]{0,1:T(8,128)S(1)} %copy-done.16), kind=kOutput, calls=%fused_computation.89 | convolution fusion | flops 227622912 | bytes 789376 | tf_op jit(solution)/shard_map/dot_general | solution.py:76
  203.7 1.7 copy.102
  205.4 9.6 %all-to-all-done.4 = bf16[32,16,512]{2,1,0:T(8,128)(2,1)S(1)} async-done(((bf16[32,16,512]{2,1,0:T(8,128)(2,1)}), bf16[32,16,512]{2,1,0:T(8,128)(2,1)S(1)}, u32[]{:S(2)}, u32[]{:S(2)}) %all-to-all-start.4) | async-done | bytes 524320 | tf_op jit(solution)/shard_map/all_to_all | solution.py:224
  (171 shorter events, 43.1 us)
Async XLA Ops:
  0.6 25.6 %copy-start = (bf16[1024,1280]{1,0:T(8,128)(2,1)S(1)}, bf16[1024,1280]{1,0:T(8,128)(2,1)}, u32[]{:S(2)}) copy-start(bf16[1024,1280]{1,0:T(8,128)(2,1)} %param.17) | copy-start | bytes 7864324
  2.6 22.3 %all-to-all-start = ((s32[64,1,8]{2,1,0:T(1,128)}), s32[64,1,8]{2,1,0:T(1,128)S(1)}, u32[]{:S(2)}, u32[]{:S(2)}) async-start(s32[64,1,8]{2,1,0:T(1,128)} %bitcast.11), calls=%async_computation | async-start | bytes 65536 | tf_op jit(solution)/shard_map/all_to_all | solution.py:127
  16.3 23.1 %collective-permute-start = (bf16[1,1,16,384]{3,2,1,0:T(8,128)(2,1)S(1)}, bf16[1,1,16,384]{3,2,1,0:T(8,128)(2,1)S(1)}, u32[]{:S(2)}, u32[]{:S(2)}) collective-permute-start(bf16[1,1,16,384]{3,2,1,0:T(8,128)(2,1)S(1)} %get-tuple-element.40), channel_id=1, source_target_pairs={{0,8},{8,0},{16,24},{24,16},{32,40},{40,32},{48,56},{56,48},{1,9},... | collective-permute-start | bytes 36872 | tf_op jit(solution)/shard_map/ppermute | solution.py:50
  28.8 54.8 %all-to-all-start.1 = ((bf16[64,8,1024]{2,1,0:T(8,128)(2,1)}), bf16[64,8,1024]{2,1,0:T(8,128)(2,1)}, u32[]{:S(2)}, u32[]{:S(2)}) async-start(bf16[64,8,1024]{2,1,0:T(8,128)(2,1)} %fusion.2), calls=%async_computation.1 | async-start | bytes 2097152 | tf_op jit(solution)/shard_map/all_to_all | solution.py:139
  37.4 29.8 %copy-start.28 = (s32[128]{0:T(128)S(1)}, s32[128]{0:T(128)}, u32[]{:S(2)}) copy-start(s32[128]{0:T(128)} %param.26) | copy-start | bytes 1540
  38.7 30.2 %copy-start.10 = (f32[384,256]{1,0:T(8,128)S(1)}, f32[384,256]{1,0:T(8,128)}, u32[]{:S(2)}) copy-start(f32[384,256]{1,0:T(8,128)} %param.25) | copy-start | bytes 1179652
  38.7 75.6 %collective-permute-start.10 = (f32[512,384]{1,0:T(8,128)}, f32[512,384]{1,0:T(8,128)}, u32[]{:S(2)}, u32[]{:S(2)}) collective-permute-start(f32[512,384]{1,0:T(8,128)} %bitcast.20), channel_id=1, source_target_pairs={{0,1},{1,0},{2,3},{3,2},{4,5},{5,4},{6,7},{7,6},{8,9},{9,8},{10,11... | collective-permute-start | bytes 2359304 | tf_op jit(solution)/shard_map/ppermute | solution.py:26
  39.4 19.5 %collective-permute-start.1 = (bf16[2,1,16,384]{3,2,1,0:T(8,128)(2,1)S(1)}, bf16[2,1,16,384]{3,2,1,0:T(8,128)(2,1)S(1)}, u32[]{:S(2)}, u32[]{:S(2)}) collective-permute-start(bf16[2,1,16,384]{3,2,1,0:T(8,128)(2,1)S(1)} %maximum_select_fusion.5), channel_id=1, source_target_pairs={{0,16},{8,24},{16,0},{24,8},{32,48},{40,56},{48,32},{56,40},{1,17}... | collective-permute-start | bytes 73736 | tf_op jit(solution)/shard_map/ppermute | solution.py:50
  58.9 7.0 %collective-permute-start.2 = (bf16[4,1,16,384]{3,2,1,0:T(8,128)(2,1)S(1)}, bf16[4,1,16,384]{3,2,1,0:T(8,128)(2,1)S(1)}, u32[]{:S(2)}, u32[]{:S(2)}) collective-permute-start(bf16[4,1,16,384]{3,2,1,0:T(8,128)(2,1)S(1)} %fusion.72), channel_id=1, source_target_pairs={{0,32},{8,40},{16,48},{24,56},{32,0},{40,8},{48,16},{56,24},{1,33}... | collective-permute-start | bytes 147464 | tf_op jit(solution)/shard_map/ppermute | solution.py:50
  65.9 6.6 %collective-permute-start.3 = (bf16[8,1,16,384]{3,2,1,0:T(8,128)(2,1)S(1)}, bf16[8,1,16,384]{3,2,1,0:T(8,128)(2,1)S(1)}, u32[]{:S(2)}, u32[]{:S(2)}) collective-permute-start(bf16[8,1,16,384]{3,2,1,0:T(8,128)(2,1)S(1)} %maximum_select_fusion.2), channel_id=1, source_target_pairs={{0,2},{2,0},{4,6},{6,4},{1,3},{3,1},{5,7},{7,5},{8,10},{10,8},{12,... | collective-permute-start | bytes 294920 | tf_op jit(solution)/shard_map/ppermute | solution.py:50
  72.4 38.6 %copy-start.32 = (f32[128]{0:T(128)}, f32[128]{0:T(128)S(1)}, u32[]{:S(2)}) copy-start(f32[128]{0:T(128)S(1)} %neg.15) | copy-start | bytes 1540
  72.5 43.6 %copy-start.25 = (bf16[16]{0:T(256)(128)(2,1)}, bf16[16]{0:T(256)(128)(2,1)S(1)}, u32[]{:S(2)}) copy-start(bf16[16]{0:T(256)(128)(2,1)S(1)} %pad.11.clone) | copy-start | bytes 100
  72.5 6.1 %collective-permute-start.4 = (bf16[8,2,16,384]{3,2,1,0:T(8,128)(2,1)S(1)}, bf16[8,2,16,384]{3,2,1,0:T(8,128)(2,1)S(1)}, u32[]{:S(2)}, u32[]{:S(2)}) collective-permute-start(bf16[8,2,16,384]{3,2,1,0:T(8,128)(2,1)S(1)} %maximum_select_fusion.1), channel_id=1, source_target_pairs={{0,4},{2,6},{4,0},{6,2},{1,5},{3,7},{5,1},{7,3},{8,12},{10,14},{12... | collective-permute-start | bytes 589832 | tf_op jit(solution)/shard_map/ppermute | solution.py:50
  74.5 36.5 %copy-start.34 = (f32[128]{0:T(128)}, f32[128]{0:T(128)S(1)}, u32[]{:S(2)}) copy-start(f32[128]{0:T(128)S(1)} %broadcast_multiply_fusion.2) | copy-start | bytes 1540
  79.5 9.3 %collective-permute-start.5 = (bf16[512,384]{1,0:T(8,128)(2,1)}, bf16[512,384]{1,0:T(8,128)(2,1)}, u32[]{:S(2)}, u32[]{:S(2)}) collective-permute-start(bf16[512,384]{1,0:T(8,128)(2,1)} %bitcast.10), channel_id=1, source_target_pairs={{0,1},{1,0},{2,3},{3,2},{4,5},{5,4},{6,7},{7,6},{8,9},{9,8},{10,11... | collective-permute-start | bytes 1179656 | tf_op jit(solution)/shard_map/ppermute | solution.py:26
  88.7 22.0 %copy-start.3 = (f32[384,256]{0,1:T(8,128)S(1)}, f32[384,256]{0,1:T(8,128)}, u32[]{:S(2)}) copy-start(f32[384,256]{0,1:T(8,128)} %copy.88) | copy-start | bytes 1179652
  88.8 22.0 %copy-start.18 = (f32[384]{0:T(512)S(1)}, f32[384]{0:T(512)}, u32[]{:S(2)}) copy-start(f32[384]{0:T(512)} %param.31) | copy-start | bytes 4612
  91.8 15.5 %collective-permute-start.8 = (bf16[384,384]{0,1:T(8,128)(2,1)S(1)}, bf16[384,384]{0,1:T(8,128)(2,1)S(1)}, u32[]{:S(2)}, u32[]{:S(2)}) collective-permute-start(bf16[384,384]{0,1:T(8,128)(2,1)S(1)} %get-tuple-element.49), channel_id=1, source_target_pairs={{0,192},{64,0},{128,64},{192,128},{1,193},{65,1},{129,65},{193,129... | collective-permute-start | bytes 884744 | tf_op jit(solution)/shard_map/ppermute | solution.py:32
  94.8 15.8 %collective-permute-start.7 = (bf16[384,384]{0,1:T(8,128)(2,1)S(1)}, bf16[384,384]{0,1:T(8,128)(2,1)S(1)}, u32[]{:S(2)}, u32[]{:S(2)}) collective-permute-start(bf16[384,384]{0,1:T(8,128)(2,1)S(1)} %get-tuple-element.49), channel_id=1, source_target_pairs={{0,64},{64,128},{128,192},{192,0},{1,65},{65,129},{129,193},{193,1... | collective-permute-start | bytes 884744 | tf_op jit(solution)/shard_map/ppermute | solution.py:32
  94.8 15.8 %collective-permute-start.6 = (bf16[384,384]{0,1:T(8,128)(2,1)S(1)}, bf16[384,384]{0,1:T(8,128)(2,1)S(1)}, u32[]{:S(2)}, u32[]{:S(2)}) collective-permute-start(bf16[384,384]{0,1:T(8,128)(2,1)S(1)} %get-tuple-element.49), channel_id=1, source_target_pairs={{0,128},{64,192},{128,0},{192,64},{1,129},{65,193},{129,1},{193,65... | collective-permute-start | bytes 884744 | tf_op jit(solution)/shard_map/ppermute | solution.py:32
  113.0 3.2 %collective-permute-start.9 = (f32[512,384]{1,0:T(8,128)S(1)}, f32[512,384]{1,0:T(8,128)S(1)}, u32[]{:S(2)}, u32[]{:S(2)}) collective-permute-start(f32[512,384]{1,0:T(8,128)S(1)} %fusion.66), channel_id=1, source_target_pairs={{0,1},{1,0},{2,3},{3,2},{4,5},{5,4},{6,7},{7,6},{8,9},{9,8},{10,11... | collective-permute-start | bytes 2359304 | tf_op jit(solution)/shard_map/ppermute | solution.py:26
  114.3 1.8 collective-permute-start.11
  117.8 25.0 %all-to-all-start.2 = ((bf16[32,16,512]{2,1,0:T(8,128)(2,1)}), bf16[32,16,512]{2,1,0:T(8,128)(2,1)}, u32[]{:S(2)}, u32[]{:S(2)}) async-start(bf16[32,16,512]{2,1,0:T(8,128)(2,1)} %pad_maximum_fusion.1), calls=%async_computation.2 | async-start | bytes 1048576 | tf_op jit(solution)/shard_map/all_to_all | solution.py:224
  144.7 28.4 %copy-start.24 = (s32[384]{0:T(512)S(1)}, s32[384]{0:T(512)}, u32[]{:S(2)}) copy-start(s32[384]{0:T(512)} %copy-done.23) | copy-start | bytes 4612
  162.5 7.3 %collective-permute-start.12 = (bf16[512,384]{1,0:T(8,128)(2,1)}, bf16[512,384]{1,0:T(8,128)(2,1)}, u32[]{:S(2)}, u32[]{:S(2)}) collective-permute-start(bf16[512,384]{1,0:T(8,128)(2,1)} %bitcast.25), channel_id=1, source_target_pairs={{0,1},{1,0},{2,3},{3,2},{4,5},{5,4},{6,7},{7,6},{8,9},{9,8},{10,11... | collective-permute-start | bytes 1179656 | tf_op jit(solution)/shard_map/ppermute | solution.py:26
  171.3 8.6 %collective-permute-start.15 = (bf16[384,384]{0,1:T(8,128)(2,1)S(1)}, bf16[384,384]{0,1:T(8,128)(2,1)S(1)}, u32[]{:S(2)}, u32[]{:S(2)}) collective-permute-start(bf16[384,384]{0,1:T(8,128)(2,1)S(1)} %get-tuple-element.52), channel_id=1, source_target_pairs={{0,192},{64,0},{128,64},{192,128},{1,193},{65,1},{129,65},{193,129... | collective-permute-start | bytes 884744 | tf_op jit(solution)/shard_map/ppermute | solution.py:32
  171.4 16.0 %collective-permute-start.14 = (bf16[384,384]{0,1:T(8,128)(2,1)S(1)}, bf16[384,384]{0,1:T(8,128)(2,1)S(1)}, u32[]{:S(2)}, u32[]{:S(2)}) collective-permute-start(bf16[384,384]{0,1:T(8,128)(2,1)S(1)} %get-tuple-element.52), channel_id=1, source_target_pairs={{0,64},{64,128},{128,192},{192,0},{1,65},{65,129},{129,193},{193,1... | collective-permute-start | bytes 884744 | tf_op jit(solution)/shard_map/ppermute | solution.py:32
  172.8 14.5 %collective-permute-start.13 = (bf16[384,384]{0,1:T(8,128)(2,1)S(1)}, bf16[384,384]{0,1:T(8,128)(2,1)S(1)}, u32[]{:S(2)}, u32[]{:S(2)}) collective-permute-start(bf16[384,384]{0,1:T(8,128)(2,1)S(1)} %get-tuple-element.52), channel_id=1, source_target_pairs={{0,128},{64,192},{128,0},{192,64},{1,129},{65,193},{129,1},{193,65... | collective-permute-start | bytes 884744 | tf_op jit(solution)/shard_map/ppermute | solution.py:32
  189.7 3.4 %collective-permute-start.16 = (f32[512,384]{1,0:T(8,128)S(1)}, f32[512,384]{1,0:T(8,128)S(1)}, u32[]{:S(2)}, u32[]{:S(2)}) collective-permute-start(f32[512,384]{1,0:T(8,128)S(1)} %fusion.65), channel_id=1, source_target_pairs={{0,1},{1,0},{2,3},{3,2},{4,5},{5,4},{6,7},{7,6},{8,9},{9,8},{10,11... | collective-permute-start | bytes 2359304 | tf_op jit(solution)/shard_map/ppermute | solution.py:26
  191.2 1.8 collective-permute-start.17
  193.5 22.2 %copy-start.11 = (f32[384,16]{0,1:T(8,128)S(1)}, f32[384,16]{0,1:T(8,128)}, u32[]{:S(2)}) copy-start(f32[384,16]{0,1:T(8,128)} %param.32) | copy-start | bytes 73732
  194.4 20.7 %all-to-all-start.4 = ((bf16[32,16,512]{2,1,0:T(8,128)(2,1)}), bf16[32,16,512]{2,1,0:T(8,128)(2,1)S(1)}, u32[]{:S(2)}, u32[]{:S(2)}) async-start(bf16[32,16,512]{2,1,0:T(8,128)(2,1)} %pad_maximum_fusion.2), calls=%async_computation.4 | async-start | bytes 1048576 | tf_op jit(solution)/shard_map/all_to_all | solution.py:224
  (28 other events, 319.8 us)

commit v2 on v1

--- a/solution.py
+++ b/solution.py
@@ -59,8 +59,23 @@
     held = share.astype(jnp.bfloat16).reshape(1, 1, share_len, row_count)
     for step in (1, 2, 4):
         held = doubled(held, "z", Z, step, 0)
-    for step in (1, 2):
-        held = doubled(held, "x", X, step, 1)
+    near = [held]
+    for step in (1, 2, 3):
+        near.append(lax.ppermute(held, "x", [(i, i ^ step) for i in range(X)]))
+    index = lax.axis_index("x")
+    low, high = index % 2 == 0, index // 2 == 0
+
+    def pair(first, second):
+        return jnp.where(
+            low,
+            jnp.concatenate([first, second], axis=1),
+            jnp.concatenate([second, first], axis=1),
+        )
+
+    mine, far = pair(near[0], near[1]), pair(near[2], near[3])
+    held = jnp.where(
+        high, jnp.concatenate([mine, far], axis=1), jnp.concatenate([far, mine], axis=1)
+    )
     own = held.reshape(-1, row_count)
     return own, swapped(own)
 
@@ -205,26 +220,29 @@
         flow_part = flow_own + swapped(flow_other) - load_flow
         balance = balance + swapped(balance)
         high = rounded(balance)
-        lanes = row_count // 3
+        lanes = 128
+        strips = row_count // lanes
         tail = jnp.concatenate(
             [
-                high.reshape(3, lanes),
-                (balance - high).reshape(3, lanes),
-                jnp.zeros((share_len - 6, lanes), jnp.float32),
+                high.reshape(strips, lanes),
+                (balance - high).reshape(strips, lanes),
+                jnp.zeros((8 - 2 * strips, lanes), jnp.float32),
             ],
             axis=0,
         )
+        body = flow_part.reshape(chip_count, share_len, row_count)
         sent = jnp.concatenate(
-            [
-                flow_part.reshape(chip_count, share_len, row_count),
-                jnp.broadcast_to(tail[None], (chip_count, share_len, lanes)),
-            ],
-            axis=2,
+            [body[:, :, i * lanes : (i + 1) * lanes] for i in range(strips)]
+            + [jnp.broadcast_to(tail[None], (chip_count, 8, lanes))],
+            axis=1,
         ).astype(jnp.bfloat16)
         received = lax.all_to_all(sent, CHIPS, 0, 0, tiled=True)
         summed = jnp.sum(received.astype(jnp.float32), axis=0)
-        flow_share = summed[:, :row_count]
-        balance = (summed[:3, row_count:] + summed[3:6, row_count:]).reshape(row_count)
+        flow_share = jnp.concatenate(
+            [summed[i * share_len : (i + 1) * share_len] for i in range(strips)], axis=1
+        )
+        tail = summed[strips * share_len :]
+        balance = (tail[:strips] + tail[strips : 2 * strips]).reshape(row_count)
         dual_flow = dual_step(dual_flow, flow_share, SIGMA_FLOW, -limit, limit)
         if iteration == 0:
             dual_own, dual_other = gathered_duals(dual_flow)

time: 218 us -> 212 us (0.972)
  waiting for transfers between devices: 83.5 us -> 81 us
    ppermute x5 -> x3, waiting for transfers between devices: 23.1 us -> 17.3 us  [doubled(): other = lax.ppermute(x, axis, [(i, i ^ step) for i in range(size)])]
    ppermute x0 -> x3, waiting for transfers between devices: none -> 4.15 us  [gathered_early(): near.append(lax.ppermute(held, 'x', [(i, i ^ step) for i in range(X)]))]
    ppermute x0 -> x3, starting transfers between devices: none -> 3.37 us  [gathered_early(): near.append(lax.ppermute(held, 'x', [(i, i ^ step) for i in range(X)]))]
    ppermute x5 -> x3, starting transfers between devices: 12.1 us -> 8.78 us  [doubled(): other = lax.ppermute(x, axis, [(i, i ^ step) for i in range(size)])]
    unnamed x82 -> x96, local copies, waits for them, and re-layouts: 8.43 us -> 7.46 us
  transfers between devices with their start and end apart: 22 -> 23, of which waited for: 12 -> 13; matrix products, arithmetic and copies ran while one was open for 19% -> 19% of each run, Pallas kernels for 0% -> 0%
where the time goes in v2:
time: 212 us; the launch traced here: 211 us
  waiting for transfers between devices  81 us (38%)
  starting transfers between devices  59.6 us (28%)
  matrix products  22.2 us (10%)
  blocking collectives  17.6 us (8%)
  other arithmetic  15.7 us (7%)
  local copies, waits for them, and re-layouts  13.9 us (7%)
    ppermute x6, waiting for transfers between devices, sum_over_lines(): lax.ppermute(low, 'lines', [(i, (i + s) % 4) for i in range(4)])  27.5 us
    all_to_all x2, waiting for transfers between devices, shards(): received = lax.all_to_all(sent, CHIPS, 0, 0, tiled=True)  22.6 us
    all_to_all x1, blocking collectives, sent_to_chips(): return lax.all_to_all(sent, CHIPS, 0, 0, tiled=True)  17.6 us
    ppermute x3, waiting for transfers between devices, doubled(): other = lax.ppermute(x, axis, [(i, i ^ step) for i in range(size)])  17.3 us
    all_to_all x1, starting transfers between devices, shards(): lax.all_to_all(slot_bus.reshape(area_count, slots), AREAS, 0, 0, tiled=True)  13 us
    ppermute x7, starting transfers between devices, swapped(): return lax.ppermute(x, 'core', [(0, 1), (1, 0)])  11.8 us
    all_to_all x2, starting transfers between devices, shards(): received = lax.all_to_all(sent, CHIPS, 0, 0, tiled=True)  10.8 us
    ppermute x3, starting transfers between devices, doubled(): other = lax.ppermute(x, axis, [(i, i ^ step) for i in range(size)])  8.78 us
  transfers between devices with their start and end apart: 23, of which 13 were waited for; matrix products, arithmetic and copies ran while one was open for 19% of the time, Pallas kernels for 0%

profile of v2, /device:TPU:1, one launch (start us, length us, event | category | flops | bytes accessed | tf_op | source)
XLA Modules:
  0.0 211.4 jit_solution(8432896587846036175)
XLA Ops:
  2.6 13.0 %all-to-all-start = ((s32[64,1,8]{2,1,0:T(1,128)}), s32[64,1,8]{2,1,0:T(1,128)S(1)}, u32[]{:S(2)}, u32[]{:S(2)}) async-start(s32[64,1,8]{2,1,0:T(1,128)} %bitcast.11), calls=%async_computation | async-start | bytes 65536 | tf_op jit(solution)/shard_map/all_to_all | solution.py:142
  17.6 7.2 %all-to-all-done = s32[64,1,8]{2,1,0:T(1,128)S(1)} async-done(((s32[64,1,8]{2,1,0:T(1,128)}), s32[64,1,8]{2,1,0:T(1,128)S(1)}, u32[]{:S(2)}, u32[]{:S(2)}) %all-to-all-start) | async-done | bytes 2080 | tf_op jit(solution)/shard_map/all_to_all | solution.py:142
  26.2 2.5 %fusion.2 = bf16[64,8,1024]{2,1,0:T(8,128)(2,1)} fusion(bf16[1024,1280]{1,0:T(8,128)(2,1)S(1)} %copy-done, s32[512]{0:T(512)S(1)} %eq.166), kind=kOutput, calls=%fused_computation.4 | convolution fusion | flops 1343356928 | bytes 3672064 | tf_op jit(solution)/shard_map/dot_general | solution.py:151
  28.8 5.6 %all-to-all-start.1 = ((bf16[64,8,1024]{2,1,0:T(8,128)(2,1)}), bf16[64,8,1024]{2,1,0:T(8,128)(2,1)}, u32[]{:S(2)}, u32[]{:S(2)}) async-start(bf16[64,8,1024]{2,1,0:T(8,128)(2,1)} %fusion.2), calls=%async_computation.1 | async-start | bytes 2097152 | tf_op jit(solution)/shard_map/all_to_all | solution.py:154
  34.3 3.1 %fusion.12 = f32[1024,384]{1,0:T(8,128)S(1)} fusion(bf16[1024,1280]{1,0:T(8,128)(2,1)S(1)} %copy-done, f32[384,1280]{1,0:T(8,128)} %param.18), kind=kOutput, calls=%fused_computation.22 | convolution fusion | flops 1007124480 | bytes 6160384 | tf_op jit(solution)/shard_map/dot_general | solution.py:172
  39.4 1.7 fusion.8
  41.1 2.2 %collective-permute-start.1 = (bf16[2,1,16,384]{3,2,1,0:T(8,128)(2,1)S(1)}, bf16[2,1,16,384]{3,2,1,0:T(8,128)(2,1)S(1)}, u32[]{:S(2)}, u32[]{:S(2)}) collective-permute-start(bf16[2,1,16,384]{3,2,1,0:T(8,128)(2,1)S(1)} %maximum_select_fusion.6), channel_id=1, source_target_pairs={{0,16},{8,24},{16,0},{24,8},{32,48},{40,56},{48,32},{56,40},{1,17}... | collective-permute-start | bytes 73736 | tf_op jit(solution)/shard_map/ppermute | solution.py:50
  43.3 15.6 %collective-permute-done.1 = bf16[2,1,16,384]{3,2,1,0:T(8,128)(2,1)S(1)} collective-permute-done((bf16[2,1,16,384]{3,2,1,0:T(8,128)(2,1)S(1)}, bf16[2,1,16,384]{3,2,1,0:T(8,128)(2,1)S(1)}, u32[]{:S(2)}, u32[]{:S(2)}) %collective-permute-start.1) | collective-permute-done | bytes 24608 | tf_op jit(solution)/shard_map/ppermute | solution.py:50
  58.9 5.2 %collective-permute-start.2 = (bf16[4,1,16,384]{3,2,1,0:T(8,128)(2,1)S(1)}, bf16[4,1,16,384]{3,2,1,0:T(8,128)(2,1)S(1)}, u32[]{:S(2)}, u32[]{:S(2)}) collective-permute-start(bf16[4,1,16,384]{3,2,1,0:T(8,128)(2,1)S(1)} %fusion.72), channel_id=1, source_target_pairs={{0,32},{8,40},{16,48},{24,56},{32,0},{40,8},{48,16},{56,24},{1,33}... | collective-permute-start | bytes 147464 | tf_op jit(solution)/shard_map/ppermute | solution.py:50
  64.1 1.7 collective-permute-done.2
  68.1 1.7 reduce_sum.85
  72.8 2.6 %collective-permute-done.5 = bf16[8,1,16,384]{3,2,1,0:T(8,128)(2,1)S(1)} collective-permute-done((bf16[8,1,16,384]{3,2,1,0:T(8,128)(2,1)S(1)}, bf16[8,1,16,384]{3,2,1,0:T(8,128)(2,1)S(1)}, u32[]{:S(2)}, u32[]{:S(2)}) %collective-permute-start.5) | collective-permute-done | bytes 98336 | tf_op jit(solution)/shard_map/ppermute | solution.py:64
  75.4 1.5 collective-permute-done.4
  77.9 5.1 %collective-permute-start.6 = (bf16[512,384]{1,0:T(8,128)(2,1)}, bf16[512,384]{1,0:T(8,128)(2,1)}, u32[]{:S(2)}, u32[]{:S(2)}) collective-permute-start(bf16[512,384]{1,0:T(8,128)(2,1)} %bitcast.10), channel_id=1, source_target_pairs={{0,1},{1,0},{2,3},{3,2},{4,5},{5,4},{6,7},{7,6},{8,9},{9,8},{10,11... | collective-permute-start | bytes 1179656 | tf_op jit(solution)/shard_map/ppermute | solution.py:26
  83.0 1.7 convolution_convert_fusion
  91.1 2.8 %collective-permute-start.9 = (bf16[384,384]{0,1:T(8,128)(2,1)S(1)}, bf16[384,384]{0,1:T(8,128)(2,1)S(1)}, u32[]{:S(2)}, u32[]{:S(2)}) collective-permute-start(bf16[384,384]{0,1:T(8,128)(2,1)S(1)} %get-tuple-element.61), channel_id=1, source_target_pairs={{0,192},{64,0},{128,64},{192,128},{1,193},{65,1},{129,65},{193,129... | collective-permute-start | bytes 884744 | tf_op jit(solution)/shard_map/ppermute | solution.py:32
  93.9 1.6 collective-permute-start.7
  95.6 10.9 %collective-permute-done.9 = bf16[384,384]{0,1:T(8,128)(2,1)S(1)} collective-permute-done((bf16[384,384]{0,1:T(8,128)(2,1)S(1)}, bf16[384,384]{0,1:T(8,128)(2,1)S(1)}, u32[]{:S(2)}, u32[]{:S(2)}) %collective-permute-start.9) | collective-permute-done | bytes 294944 | tf_op jit(solution)/shard_map/ppermute | solution.py:32
  106.5 3.3 %collective-permute-done.8 = bf16[384,384]{0,1:T(8,128)(2,1)S(1)} collective-permute-done((bf16[384,384]{0,1:T(8,128)(2,1)S(1)}, bf16[384,384]{0,1:T(8,128)(2,1)S(1)}, u32[]{:S(2)}, u32[]{:S(2)}) %collective-permute-start.8) | collective-permute-done | bytes 294944 | tf_op jit(solution)/shard_map/ppermute | solution.py:32
  110.2 1.5 fusion.113
  117.0 6.8 %all-to-all-start.2 = ((bf16[32,56,128]{2,1,0:T(8,128)(2,1)}), bf16[32,56,128]{2,1,0:T(8,128)(2,1)}, u32[]{:S(2)}, u32[]{:S(2)}) async-start(bf16[32,56,128]{2,1,0:T(8,128)(2,1)} %pad_maximum_fusion.1), calls=%async_computation.2 | async-start | bytes 917504 | tf_op jit(solution)/shard_map/all_to_all | solution.py:239
  126.6 12.5 %all-to-all-done.2 = bf16[32,56,128]{2,1,0:T(8,128)(2,1)} async-done(((bf16[32,56,128]{2,1,0:T(8,128)(2,1)}), bf16[32,56,128]{2,1,0:T(8,128)(2,1)}, u32[]{:S(2)}, u32[]{:S(2)}) %all-to-all-start.2) | async-done | bytes 458784 | tf_op jit(solution)/shard_map/all_to_all | solution.py:239
  141.0 17.6 %all_to_all.33 = bf16[32,16,384]{2,1,0:T(8,128)(2,1)} all-to-all(bf16[32,16,384]{2,1,0:T(8,128)(2,1)S(1)} %broadcast_in_dim.88), channel_id=1, replica_groups=mesh['lines'=4,'z'=8,'x'=4,'core'=2] {'z','x'}, dimensions={0} | all-to-all | bytes 786432 | tf_op jit(solution)/shard_map/all_to_all | solution.py:41
  158.7 3.5 %collective-permute-start.13 = (bf16[512,384]{1,0:T(8,128)(2,1)}, bf16[512,384]{1,0:T(8,128)(2,1)}, u32[]{:S(2)}, u32[]{:S(2)}) collective-permute-start(bf16[512,384]{1,0:T(8,128)(2,1)} %bitcast.25), channel_id=1, source_target_pairs={{0,1},{1,0},{2,3},{3,2},{4,5},{5,4},{6,7},{7,6},{8,9},{9,8},{10,11... | collective-permute-start | bytes 1179656 | tf_op jit(solution)/shard_map/ppermute | solution.py:26
  162.8 1.7 copy.98
  170.3 5.9 %collective-permute-done.16 = bf16[384,384]{0,1:T(8,128)(2,1)S(1)} collective-permute-done((bf16[384,384]{0,1:T(8,128)(2,1)S(1)}, bf16[384,384]{0,1:T(8,128)(2,1)S(1)}, u32[]{:S(2)}, u32[]{:S(2)}) %collective-permute-start.16) | collective-permute-done | bytes 294944 | tf_op jit(solution)/shard_map/ppermute | solution.py:32
  176.2 7.4 %collective-permute-done.15 = bf16[384,384]{0,1:T(8,128)(2,1)S(1)} collective-permute-done((bf16[384,384]{0,1:T(8,128)(2,1)S(1)}, bf16[384,384]{0,1:T(8,128)(2,1)S(1)}, u32[]{:S(2)}, u32[]{:S(2)}) %collective-permute-start.15) | collective-permute-done | bytes 294944 | tf_op jit(solution)/shard_map/ppermute | solution.py:32
  187.4 1.7 collective-permute-done.18
  190.6 4.0 %all-to-all-start.4 = ((bf16[32,56,128]{2,1,0:T(8,128)(2,1)}), bf16[32,56,128]{2,1,0:T(8,128)(2,1)S(1)}, u32[]{:S(2)}, u32[]{:S(2)}) async-start(bf16[32,56,128]{2,1,0:T(8,128)(2,1)} %pad_maximum_fusion.2), calls=%async_computation.4 | async-start | bytes 917504 | tf_op jit(solution)/shard_map/all_to_all | solution.py:239
  195.5 1.7 copy.101
  197.3 1.9 fusion.50
  200.0 10.1 %all-to-all-done.4 = bf16[32,56,128]{2,1,0:T(8,128)(2,1)S(1)} async-done(((bf16[32,56,128]{2,1,0:T(8,128)(2,1)}), bf16[32,56,128]{2,1,0:T(8,128)(2,1)S(1)}, u32[]{:S(2)}, u32[]{:S(2)}) %all-to-all-start.4) | async-done | bytes 458784 | tf_op jit(solution)/shard_map/all_to_all | solution.py:239
  (192 shorter events, 44.4 us)
Async XLA Ops:
  0.6 25.6 %copy-start = (bf16[1024,1280]{1,0:T(8,128)(2,1)S(1)}, bf16[1024,1280]{1,0:T(8,128)(2,1)}, u32[]{:S(2)}) copy-start(bf16[1024,1280]{1,0:T(8,128)(2,1)} %param.17) | copy-start | bytes 7864324
  2.6 22.3 %all-to-all-start = ((s32[64,1,8]{2,1,0:T(1,128)}), s32[64,1,8]{2,1,0:T(1,128)S(1)}, u32[]{:S(2)}, u32[]{:S(2)}) async-start(s32[64,1,8]{2,1,0:T(1,128)} %bitcast.11), calls=%async_computation | async-start | bytes 65536 | tf_op jit(solution)/shard_map/all_to_all | solution.py:142
  16.3 24.8 %collective-permute-start = (bf16[1,1,16,384]{3,2,1,0:T(8,128)(2,1)S(1)}, bf16[1,1,16,384]{3,2,1,0:T(8,128)(2,1)S(1)}, u32[]{:S(2)}, u32[]{:S(2)}) collective-permute-start(bf16[1,1,16,384]{3,2,1,0:T(8,128)(2,1)S(1)} %get-tuple-element.52), channel_id=1, source_target_pairs={{0,8},{8,0},{16,24},{24,16},{32,40},{40,32},{48,56},{56,48},{1,9},... | collective-permute-start | bytes 36872 | tf_op jit(solution)/shard_map/ppermute | solution.py:50
  28.8 54.2 %all-to-all-start.1 = ((bf16[64,8,1024]{2,1,0:T(8,128)(2,1)}), bf16[64,8,1024]{2,1,0:T(8,128)(2,1)}, u32[]{:S(2)}, u32[]{:S(2)}) async-start(bf16[64,8,1024]{2,1,0:T(8,128)(2,1)} %fusion.2), calls=%async_computation.1 | async-start | bytes 2097152 | tf_op jit(solution)/shard_map/all_to_all | solution.py:154
  37.4 29.8 %copy-start.30 = (f32[128]{0:T(128)S(1)}, f32[128]{0:T(128)}, u32[]{:S(2)}) copy-start(f32[128]{0:T(128)} %param.27) | copy-start | bytes 1540
  38.7 28.5 %copy-start.11 = (f32[384,256]{1,0:T(8,128)S(1)}, f32[384,256]{1,0:T(8,128)}, u32[]{:S(2)}) copy-start(f32[384,256]{1,0:T(8,128)} %param.25) | copy-start | bytes 1179652
  38.7 31.1 %copy-start.13 = (f32[384,128]{1,0:T(8,128)S(1)}, f32[384,128]{1,0:T(8,128)}, u32[]{:S(2)}) copy-start(f32[384,128]{1,0:T(8,128)} %param.30) | copy-start | bytes 589828
  38.7 74.8 %collective-permute-start.11 = (f32[512,384]{1,0:T(8,128)}, f32[512,384]{1,0:T(8,128)}, u32[]{:S(2)}, u32[]{:S(2)}) collective-permute-start(f32[512,384]{1,0:T(8,128)} %bitcast.20), channel_id=1, source_target_pairs={{0,1},{1,0},{2,3},{3,2},{4,5},{5,4},{6,7},{7,6},{8,9},{9,8},{10,11... | collective-permute-start | bytes 2359304 | tf_op jit(solution)/shard_map/ppermute | solution.py:26
  41.0 29.6 %copy-start.31 = (f32[128]{0:T(128)S(1)}, f32[128]{0:T(128)}, u32[]{:S(2)}) copy-start(f32[128]{0:T(128)} %param.28) | copy-start | bytes 1540
  41.1 17.8 %collective-permute-start.1 = (bf16[2,1,16,384]{3,2,1,0:T(8,128)(2,1)S(1)}, bf16[2,1,16,384]{3,2,1,0:T(8,128)(2,1)S(1)}, u32[]{:S(2)}, u32[]{:S(2)}) collective-permute-start(bf16[2,1,16,384]{3,2,1,0:T(8,128)(2,1)S(1)} %maximum_select_fusion.6), channel_id=1, source_target_pairs={{0,16},{8,24},{16,0},{24,8},{32,48},{40,56},{48,32},{56,40},{1,17}... | collective-permute-start | bytes 73736 | tf_op jit(solution)/shard_map/ppermute | solution.py:50
  58.9 7.0 %collective-permute-start.2 = (bf16[4,1,16,384]{3,2,1,0:T(8,128)(2,1)S(1)}, bf16[4,1,16,384]{3,2,1,0:T(8,128)(2,1)S(1)}, u32[]{:S(2)}, u32[]{:S(2)}) collective-permute-start(bf16[4,1,16,384]{3,2,1,0:T(8,128)(2,1)S(1)} %fusion.72), channel_id=1, source_target_pairs={{0,32},{8,40},{16,48},{24,56},{32,0},{40,8},{48,16},{56,24},{1,33}... | collective-permute-start | bytes 147464 | tf_op jit(solution)/shard_map/ppermute | solution.py:50
  65.9 6.9 %collective-permute-start.3 = (bf16[8,1,16,384]{3,2,1,0:T(8,128)(2,1)S(1)}, bf16[8,1,16,384]{3,2,1,0:T(8,128)(2,1)S(1)}, u32[]{:S(2)}, u32[]{:S(2)}) collective-permute-start(bf16[8,1,16,384]{3,2,1,0:T(8,128)(2,1)S(1)} %maximum_select_fusion.3), channel_id=1, source_target_pairs={{0,2},{2,0},{4,6},{6,4},{1,3},{3,1},{5,7},{7,5},{8,10},{10,8},{12,... | collective-permute-start | bytes 294920 | tf_op jit(solution)/shard_map/ppermute | solution.py:64
  67.2 43.0 %copy-start.37 = (f32[128]{0:T(128)}, f32[128]{0:T(128)S(1)}, u32[]{:S(2)}) copy-start(f32[128]{0:T(128)S(1)} %broadcast_multiply_fusion.2) | copy-start | bytes 1540
  70.6 39.5 %copy-start.39 = (f32[128]{0:T(128)}, f32[128]{0:T(128)S(1)}, u32[]{:S(2)}) copy-start(f32[128]{0:T(128)S(1)} %neg.15) | copy-start | bytes 1540
  70.7 44.5 %copy-start.23 = (bf16[8]{0:T(256)(128)(2,1)}, bf16[8]{0:T(256)(128)(2,1)S(1)}, u32[]{:S(2)}) copy-start(bf16[8]{0:T(256)(128)(2,1)S(1)} %pad.21.clone) | copy-start | bytes 52
  70.7 4.7 %collective-permute-start.5 = (bf16[8,1,16,384]{3,2,1,0:T(8,128)(2,1)S(1)}, bf16[8,1,16,384]{3,2,1,0:T(8,128)(2,1)S(1)}, u32[]{:S(2)}, u32[]{:S(2)}) collective-permute-start(bf16[8,1,16,384]{3,2,1,0:T(8,128)(2,1)S(1)} %maximum_select_fusion.3), channel_id=1, source_target_pairs={{0,6},{2,4},{4,2},{6,0},{1,7},{3,5},{5,3},{7,1},{8,14},{10,12},{12... | collective-permute-start | bytes 294920 | tf_op jit(solution)/shard_map/ppermute | solution.py:64
  72.0 5.0 %collective-permute-start.4 = (bf16[8,1,16,384]{3,2,1,0:T(8,128)(2,1)S(1)}, bf16[8,1,16,384]{3,2,1,0:T(8,128)(2,1)S(1)}, u32[]{:S(2)}, u32[]{:S(2)}) collective-permute-start(bf16[8,1,16,384]{3,2,1,0:T(8,128)(2,1)S(1)} %maximum_select_fusion.3), channel_id=1, source_target_pairs={{0,4},{2,6},{4,0},{6,2},{1,5},{3,7},{5,1},{7,3},{8,12},{10,14},{12... | collective-permute-start | bytes 294920 | tf_op jit(solution)/shard_map/ppermute | solution.py:64
  77.9 11.7 %collective-permute-start.6 = (bf16[512,384]{1,0:T(8,128)(2,1)}, bf16[512,384]{1,0:T(8,128)(2,1)}, u32[]{:S(2)}, u32[]{:S(2)}) collective-permute-start(bf16[512,384]{1,0:T(8,128)(2,1)} %bitcast.10), channel_id=1, source_target_pairs={{0,1},{1,0},{2,3},{3,2},{4,5},{5,4},{6,7},{7,6},{8,9},{9,8},{10,11... | collective-permute-start | bytes 1179656 | tf_op jit(solution)/shard_map/ppermute | solution.py:26
  91.1 15.4 %collective-permute-start.9 = (bf16[384,384]{0,1:T(8,128)(2,1)S(1)}, bf16[384,384]{0,1:T(8,128)(2,1)S(1)}, u32[]{:S(2)}, u32[]{:S(2)}) collective-permute-start(bf16[384,384]{0,1:T(8,128)(2,1)S(1)} %get-tuple-element.61), channel_id=1, source_target_pairs={{0,192},{64,0},{128,64},{192,128},{1,193},{65,1},{129,65},{193,129... | collective-permute-start | bytes 884744 | tf_op jit(solution)/shard_map/ppermute | solution.py:32
  93.9 15.8 %collective-permute-start.8 = (bf16[384,384]{0,1:T(8,128)(2,1)S(1)}, bf16[384,384]{0,1:T(8,128)(2,1)S(1)}, u32[]{:S(2)}, u32[]{:S(2)}) collective-permute-start(bf16[384,384]{0,1:T(8,128)(2,1)S(1)} %get-tuple-element.61), channel_id=1, source_target_pairs={{0,64},{64,128},{128,192},{192,0},{1,65},{65,129},{129,193},{193,1... | collective-permute-start | bytes 884744 | tf_op jit(solution)/shard_map/ppermute | solution.py:32
  93.9 15.8 %collective-permute-start.7 = (bf16[384,384]{0,1:T(8,128)(2,1)S(1)}, bf16[384,384]{0,1:T(8,128)(2,1)S(1)}, u32[]{:S(2)}, u32[]{:S(2)}) collective-permute-start(bf16[384,384]{0,1:T(8,128)(2,1)S(1)} %get-tuple-element.61), channel_id=1, source_target_pairs={{0,128},{64,192},{128,0},{192,64},{1,129},{65,193},{129,1},{193,65... | collective-permute-start | bytes 884744 | tf_op jit(solution)/shard_map/ppermute | solution.py:32
  112.1 3.2 %collective-permute-start.10 = (f32[512,384]{1,0:T(8,128)S(1)}, f32[512,384]{1,0:T(8,128)S(1)}, u32[]{:S(2)}, u32[]{:S(2)}) collective-permute-start(f32[512,384]{1,0:T(8,128)S(1)} %fusion.66), channel_id=1, source_target_pairs={{0,1},{1,0},{2,3},{3,2},{4,5},{5,4},{6,7},{7,6},{8,9},{9,8},{10,11... | collective-permute-start | bytes 2359304 | tf_op jit(solution)/shard_map/ppermute | solution.py:26
  113.4 1.8 collective-permute-start.12
  117.0 22.1 %all-to-all-start.2 = ((bf16[32,56,128]{2,1,0:T(8,128)(2,1)}), bf16[32,56,128]{2,1,0:T(8,128)(2,1)}, u32[]{:S(2)}, u32[]{:S(2)}) async-start(bf16[32,56,128]{2,1,0:T(8,128)(2,1)} %pad_maximum_fusion.1), calls=%async_computation.2 | async-start | bytes 917504 | tf_op jit(solution)/shard_map/all_to_all | solution.py:239
  141.0 28.4 %copy-start.26 = (s32[384]{0:T(512)S(1)}, s32[384]{0:T(512)}, u32[]{:S(2)}) copy-start(s32[384]{0:T(512)} %copy-done.25) | copy-start | bytes 4612
  158.7 7.4 %collective-permute-start.13 = (bf16[512,384]{1,0:T(8,128)(2,1)}, bf16[512,384]{1,0:T(8,128)(2,1)}, u32[]{:S(2)}, u32[]{:S(2)}) collective-permute-start(bf16[512,384]{1,0:T(8,128)(2,1)} %bitcast.25), channel_id=1, source_target_pairs={{0,1},{1,0},{2,3},{3,2},{4,5},{5,4},{6,7},{7,6},{8,9},{9,8},{10,11... | collective-permute-start | bytes 1179656 | tf_op jit(solution)/shard_map/ppermute | solution.py:26
  167.6 8.6 %collective-permute-start.16 = (bf16[384,384]{0,1:T(8,128)(2,1)S(1)}, bf16[384,384]{0,1:T(8,128)(2,1)S(1)}, u32[]{:S(2)}, u32[]{:S(2)}) collective-permute-start(bf16[384,384]{0,1:T(8,128)(2,1)S(1)} %get-tuple-element.64), channel_id=1, source_target_pairs={{0,192},{64,0},{128,64},{192,128},{1,193},{65,1},{129,65},{193,129... | collective-permute-start | bytes 884744 | tf_op jit(solution)/shard_map/ppermute | solution.py:32
  167.7 16.0 %collective-permute-start.15 = (bf16[384,384]{0,1:T(8,128)(2,1)S(1)}, bf16[384,384]{0,1:T(8,128)(2,1)S(1)}, u32[]{:S(2)}, u32[]{:S(2)}) collective-permute-start(bf16[384,384]{0,1:T(8,128)(2,1)S(1)} %get-tuple-element.64), channel_id=1, source_target_pairs={{0,64},{64,128},{128,192},{192,0},{1,65},{65,129},{129,193},{193,1... | collective-permute-start | bytes 884744 | tf_op jit(solution)/shard_map/ppermute | solution.py:32
  169.1 14.5 %collective-permute-start.14 = (bf16[384,384]{0,1:T(8,128)(2,1)S(1)}, bf16[384,384]{0,1:T(8,128)(2,1)S(1)}, u32[]{:S(2)}, u32[]{:S(2)}) collective-permute-start(bf16[384,384]{0,1:T(8,128)(2,1)S(1)} %get-tuple-element.64), channel_id=1, source_target_pairs={{0,128},{64,192},{128,0},{192,64},{1,129},{65,193},{129,1},{193,65... | collective-permute-start | bytes 884744 | tf_op jit(solution)/shard_map/ppermute | solution.py:32
  186.0 3.2 %collective-permute-start.17 = (f32[512,384]{1,0:T(8,128)S(1)}, f32[512,384]{1,0:T(8,128)S(1)}, u32[]{:S(2)}, u32[]{:S(2)}) collective-permute-start(f32[512,384]{1,0:T(8,128)S(1)} %fusion.65), channel_id=1, source_target_pairs={{0,1},{1,0},{2,3},{3,2},{4,5},{5,4},{6,7},{7,6},{8,9},{9,8},{10,11... | collective-permute-start | bytes 2359304 | tf_op jit(solution)/shard_map/ppermute | solution.py:26
  187.3 1.8 collective-permute-start.18
  190.6 19.5 %all-to-all-start.4 = ((bf16[32,56,128]{2,1,0:T(8,128)(2,1)}), bf16[32,56,128]{2,1,0:T(8,128)(2,1)S(1)}, u32[]{:S(2)}, u32[]{:S(2)}) async-start(bf16[32,56,128]{2,1,0:T(8,128)(2,1)} %pad_maximum_fusion.2), calls=%async_computation.4 | async-start | bytes 917504 | tf_op jit(solution)/shard_map/all_to_all | solution.py:239
  (36 other events, 425.4 us)

commit v3 on v2

--- a/solution.py
+++ b/solution.py
@@ -1,6 +1,8 @@
 import jax
 import jax.numpy as jnp
 from jax import lax
+from jax.experimental import pallas as pl
+from jax.experimental.pallas import tpu as pltpu
 from jax.sharding import Mesh
 from jax.sharding import PartitionSpec as P
 
@@ -26,13 +28,100 @@
     return lax.ppermute(x, "core", [(0, 1), (1, 0)])
 
 
-def sum_over_lines(part):
-    low = part.astype(jnp.bfloat16)
-    near = [
-        lax.ppermute(low, "lines", [(i, (i + s) % 4) for i in range(4)]).astype(jnp.float32)
-        for s in (1, 2, 3)
-    ]
-    return (rounded(part) + near[1]) + (near[0] + near[2])
+CONTRACT_MAJOR = (((0,), (0,)), ((), ()))
+CONTRACT_MINOR = (((1,), (1,)), ((), ()))
+
+
+def with_side(x, step):
+    other = lax.ppermute(x.astype(jnp.bfloat16), "lines", [(i, i ^ step) for i in range(4)])
+    return x + other.astype(jnp.float32)
+
+
+def sum_over_lines(halves):
+    first, second = (rounded(half.astype(jnp.float32)) for half in halves)
+    first, second = rounded(with_side(first, 1)), rounded(with_side(second, 3))
+    return jnp.concatenate([with_side(first, 3), with_side(second, 1)], axis=0)
+
+
+def store_price(dual_own, dual_other, weight_own, weight_other, first, second):
+    price = lax.dot_general(
+        dual_own[...], weight_own[...], CONTRACT_MAJOR, preferred_element_type=jnp.float32
+    ) + lax.dot_general(
+        dual_other[...], weight_other[...], CONTRACT_MAJOR, preferred_element_type=jnp.float32
+    )
+    rows = first.shape[0]
+    first[...] = price[:rows].astype(jnp.bfloat16)
+    second[...] = price[rows:].astype(jnp.bfloat16)
+
+
+def weights_body(
+    core,
+    columns,
+    column,
+    stor_own,
+    stor_other,
+    dual_own,
+    dual_other,
+    weight_own,
+    weight_other,
+    first,
+    second,
+    split,
+):
+    slot_count, gen_count = columns.shape[0], column.shape[1]
+    slot = lax.broadcasted_iota(jnp.int32, (slot_count, gen_count), 0)
+    pick = jnp.where(slot == column[...], 1.0, 0.0).astype(jnp.bfloat16)
+    weight = lax.dot_general(
+        columns[...], pick, CONTRACT_MAJOR, preferred_element_type=jnp.float32
+    )
+    split[...] = weight.astype(jnp.bfloat16).reshape(split.shape)
+    share_len = split.shape[1]
+    mine = core[0]
+    for chip in range(split.shape[0] // CORES):
+        rows = slice(chip * share_len, (chip + 1) * share_len)
+        weight_own[rows, :gen_count] = split[CORES * chip + mine]
+        weight_other[rows, :gen_count] = split[CORES * chip + 1 - mine]
+    weight_own[:, gen_count:] = stor_own[...]
+    weight_other[:, gen_count:] = stor_other[...]
+    store_price(dual_own, dual_other, weight_own, weight_other, first, second)
+
+
+def price_body(dual_own, dual_other, weight_own, weight_other, first, second):
+    store_price(dual_own, dual_other, weight_own, weight_other, first, second)
+
+
+def half_prices(row_count, units):
+    half = jax.ShapeDtypeStruct((row_count // 2, units), jnp.bfloat16)
+    return (half, half)
+
+
+def weights_and_prices(core, columns, column, stor_own, stor_other, dual_own, dual_other):
+    half_lines, row_count = dual_own.shape
+    gen_count = column.shape[0]
+    units = gen_count + stor_own.shape[1]
+    weight = jax.ShapeDtypeStruct((half_lines, units), jnp.bfloat16)
+    in_vmem = pl.BlockSpec(memory_space=pltpu.VMEM)
+    share_len = columns.shape[1] // (Z * X * CORES)
+    own, other, first, second = pl.pallas_call(
+        weights_body,
+        out_shape=(weight, weight, *half_prices(row_count, units)),
+        in_specs=[pl.BlockSpec(memory_space=pltpu.SMEM)] + [in_vmem] * 6,
+        out_specs=(in_vmem,) * 4,
+        scratch_shapes=[pltpu.VMEM((Z * X * CORES, share_len, gen_count), jnp.bfloat16)],
+        name="weights",
+    )(core.reshape(1), columns, column.reshape(1, -1), stor_own, stor_other, dual_own, dual_other)
+    return own, other, (first, second)
+
+
+def later_prices(dual_own, dual_other, weight_own, weight_other):
+    in_vmem = pl.BlockSpec(memory_space=pltpu.VMEM)
+    return pl.pallas_call(
+        price_body,
+        out_shape=half_prices(dual_own.shape[1], weight_own.shape[1]),
+        in_specs=[in_vmem] * 4,
+        out_specs=(in_vmem,) * 2,
+        name="prices",
+    )(dual_own, dual_other, weight_own, weight_other)
 
 
 def sent_to_chips(x):
@@ -147,19 +236,13 @@
     bus_ids = jnp.arange(bus_count, dtype=jnp.int32)
     sel_gen = (wanted.reshape(-1)[:, None] == bus_ids[None, :]).astype(jnp.bfloat16)
     sel_stor = (stor_bus[:, None] == bus_ids[None, :]).astype(jnp.bfloat16)
-    contract_minor = (((1,), (1,)), ((), ()))
     sent_columns = lax.dot_general(
-        sel_gen, ptdf, contract_minor, preferred_element_type=jnp.float32
+        sel_gen, ptdf, CONTRACT_MINOR, preferred_element_type=jnp.float32
     ).astype(jnp.bfloat16)
     columns = lax.all_to_all(sent_columns, AREAS, 0, 0, tiled=True)
     weight_stor = lax.dot_general(
-        ptdf, sel_stor, contract_minor, preferred_element_type=jnp.float32
+        ptdf, sel_stor, CONTRACT_MINOR, preferred_element_type=jnp.float32
     ).astype(jnp.bfloat16)
-    pick = (column[:, None] == slot_of[None, :]).astype(jnp.bfloat16)
-    weight_gen = lax.dot_general(
-        columns, pick, (((0,), (1,)), ((), ())), preferred_element_type=jnp.float32
-    ).astype(jnp.bfloat16)
-    weight = jnp.concatenate([weight_gen, weight_stor], axis=1)
 
     def by_core(x):
         split = x.reshape(chip_count, CORES, share_len, x.shape[1])
@@ -167,10 +250,17 @@
         other = lax.dynamic_index_in_dim(split, 1 - core, 1, keepdims=False)
         return own.reshape(-1, x.shape[1]), other.reshape(-1, x.shape[1])
 
-    weight_own, weight_other = by_core(weight)
+    weight_own, weight_other, halves = weights_and_prices(
+        core,
+        columns.reshape(-1, line_count),
+        column,
+        *by_core(weight_stor),
+        dual_own,
+        dual_other,
+    )
     load_own, load_other = by_core(
         lax.dot_general(
-            ptdf, load.astype(jnp.bfloat16), contract_minor, preferred_element_type=jnp.float32
+            ptdf, load.astype(jnp.bfloat16), CONTRACT_MINOR, preferred_element_type=jnp.float32
         )
     )
     load_flow = load_own + swapped(load_other)
@@ -186,17 +276,15 @@
     gen_now, stor_now = (gen_start, stor_start)
     gen_old, stor_old = (gen_start, stor_start)
     price_level, dual_store = (lam_start, omega_start)
-    contract_major = (((0,), (0,)), ((), ()))
     for iteration in range(2):
         if iteration == 0:
             gen_mid, stor_mid = (gen_now, stor_now)
         else:
             gen_mid = gen_now + THETA * (gen_now - gen_old)
             stor_mid = stor_now + THETA * (stor_now - stor_old)
-        price = sum_over_lines(
-            lax.dot_general(dual_own, weight_own, contract_major, preferred_element_type=jnp.float32)
-            + lax.dot_general(dual_other, weight_other, contract_major, preferred_element_type=jnp.float32)
-        )
+        if iteration > 0:
+            halves = later_prices(dual_own, dual_other, weight_own, weight_other)
+        price = sum_over_lines(halves)
         gen_price, stor_price = price[:, :gen_count], price[:, gen_count:]
         gen_grad = 2.0 * gen_quad * gen_mid + gen_lin + price_level[:, None] + gen_price
         gen_next = jnp.clip(gen_mid - TAU * gen_grad, 0.0, gen_max)
@@ -212,10 +300,10 @@
         balance = jnp.sum(gen_bar, axis=1) + jnp.sum(stor_bar, axis=1) - load_total
         bar_low = jnp.concatenate([gen_bar, stor_bar], axis=1).astype(jnp.bfloat16)
         flow_other = lax.dot_general(
-            weight_other, bar_low, contract_minor, preferred_element_type=jnp.float32
+            weight_other, bar_low, CONTRACT_MINOR, preferred_element_type=jnp.float32
         )
         flow_own = lax.dot_general(
-            weight_own, bar_low, contract_minor, preferred_element_type=jnp.float32
+            weight_own, bar_low, CONTRACT_MINOR, preferred_element_type=jnp.float32
         )
         flow_part = flow_own + swapped(flow_other) - load_flow
         balance = balance + swapped(balance)

time: 212 us -> 211 us (level)
  blocking collectives: 17.6 us -> 0 us
  starting transfers between devices: 59.6 us -> 70.5 us
  other arithmetic: 15.7 us -> 25.3 us
  Pallas kernels: 0 us -> 6.52 us
  local copies, waits for them, and re-layouts: 13.9 us -> 7.52 us
  matrix products: 22.2 us -> 16.1 us
    all_to_all x1 -> x0, blocking collectives: 17.6 us -> none  [sent_to_chips(): return lax.all_to_all(sent, CHIPS, 0, 0, tiled=True)]
    ppermute x6 -> x8, waiting for transfers between devices: 27.5 us -> 13.9 us  [with_side(): lax.ppermute(x.astype(jnp.bfloat16), 'lines', [(i, i ^ step) for i in ran...]
    all_to_all x0 -> x1, waiting for transfers between devices: none -> 12.1 us  [sent_to_chips(): return lax.all_to_all(sent, CHIPS, 0, 0, tiled=True)]
    dot_general x12 -> x7, matrix products: 16.5 us -> 8.23 us  [the longest x1 3.08 us: shards(): lax.dot_general(ptdf, load.astype(jnp.bfloat16), CONTRACT_MINOR, preferre...]
    convert_element_type x0 -> x8, other arithmetic: none -> 7.65 us  [with_side(): x.astype(jnp.bfloat16)]
    unnamed x96 -> x76, local copies, waits for them, and re-layouts: 7.46 us -> 0.18 us
    pallas_call x0 -> x2, Pallas kernels: none -> 6.52 us  [the longest x1 3.9 us: weights_and_prices(): pl.pallas_call(weights_body, out_shape=(weight, weight, *half_prices(row_...]
    ppermute x3, waiting for transfers between devices: 17.3 us -> 22.4 us  [doubled(): other = lax.ppermute(x, axis, [(i, i ^ step) for i in range(size)])]
  transfers between devices with their start and end apart: 23 -> 26, of which waited for: 13 -> 18; matrix products, arithmetic and copies ran while one was open for 19% -> 17% of each run, Pallas kernels for 0% -> 2%
where the time goes in v3:
time: 211 us; the launch traced here: 210 us
  waiting for transfers between devices  82.7 us (39%)
  starting transfers between devices  70.5 us (33%)
  other arithmetic  25.3 us (12%)
  matrix products  16.1 us (8%)
  local copies, waits for them, and re-layouts  7.52 us (4%)
  Pallas kernels  6.52 us (3%)
    all_to_all x2, waiting for transfers between devices, shards(): received = lax.all_to_all(sent, CHIPS, 0, 0, tiled=True)  25.8 us
    ppermute x3, waiting for transfers between devices, doubled(): other = lax.ppermute(x, axis, [(i, i ^ step) for i in range(size)])  22.4 us
    ppermute x7, starting transfers between devices, swapped(): return lax.ppermute(x, 'core', [(0, 1), (1, 0)])  13.9 us
    ppermute x8, waiting for transfers between devices, with_side(): lax.ppermute(x.astype(jnp.bfloat16), 'lines', [(i, i ^ step) for i in ran...  13.9 us
    all_to_all x1, starting transfers between devices, shards(): lax.all_to_all(slot_bus.reshape(area_count, slots), AREAS, 0, 0, tiled=True)  13 us
    all_to_all x1, waiting for transfers between devices, sent_to_chips(): return lax.all_to_all(sent, CHIPS, 0, 0, tiled=True)  12.1 us
    all_to_all x2, starting transfers between devices, shards(): received = lax.all_to_all(sent, CHIPS, 0, 0, tiled=True)  10.9 us
    ppermute x3, starting transfers between devices, doubled(): other = lax.ppermute(x, axis, [(i, i ^ step) for i in range(size)])  9.21 us
  transfers between devices with their start and end apart: 26, of which 18 were waited for; matrix products, arithmetic and copies ran while one was open for 17% of the time, Pallas kernels for 2%

profile of v3, /device:TPU:1, one launch (start us, length us, event | category | flops | bytes accessed | tf_op | source)
XLA Modules:
  0.0 210.1 jit_solution(11519964908616175571)
XLA Ops:
  2.6 13.0 %all-to-all-start = ((s32[64,1,8]{2,1,0:T(1,128)}), s32[64,1,8]{2,1,0:T(1,128)S(1)}, u32[]{:S(2)}, u32[]{:S(2)}) async-start(s32[64,1,8]{2,1,0:T(1,128)} %bitcast.1), calls=%async_computation | async-start | bytes 65536 | tf_op jit(solution)/shard_map/all_to_all | solution.py:231
  17.6 3.1 %fusion.11 = f32[1024,384]{1,0:T(8,128)S(1)} fusion(bf16[1024,1280]{1,0:T(8,128)(2,1)S(1)} %copy-done, f32[384,1280]{1,0:T(8,128)} %param.18), kind=kOutput, calls=%fused_computation.18 | convolution fusion | flops 1007124480 | bytes 6160384 | tf_op jit(solution)/shard_map/dot_general | solution.py:262
  22.7 2.2 %all-to-all-done = s32[64,1,8]{2,1,0:T(1,128)S(1)} async-done(((s32[64,1,8]{2,1,0:T(1,128)}), s32[64,1,8]{2,1,0:T(1,128)S(1)}, u32[]{:S(2)}, u32[]{:S(2)}) %all-to-all-start) | async-done | bytes 2080 | tf_op jit(solution)/shard_map/all_to_all | solution.py:231
  26.2 2.5 %fusion.2 = bf16[64,8,1024]{2,1,0:T(8,128)(2,1)} fusion(bf16[1024,1280]{1,0:T(8,128)(2,1)S(1)} %copy-done, s32[512]{0:T(512)S(1)} %eq.148), kind=kOutput, calls=%fused_computation.4 | convolution fusion | flops 1343356928 | bytes 3672064 | tf_op jit(solution)/shard_map/dot_general | solution.py:239
  28.8 7.1 %all-to-all-start.1 = ((bf16[64,8,1024]{2,1,0:T(8,128)(2,1)}), bf16[64,8,1024]{2,1,0:T(8,128)(2,1)}, u32[]{:S(2)}, u32[]{:S(2)}) async-start(bf16[64,8,1024]{2,1,0:T(8,128)(2,1)} %fusion.2), calls=%async_computation.1 | async-start | bytes 2097152 | tf_op jit(solution)/shard_map/all_to_all | solution.py:242
  37.0 2.3 %collective-permute-start.1 = (bf16[2,1,16,384]{3,2,1,0:T(8,128)(2,1)S(1)}, bf16[2,1,16,384]{3,2,1,0:T(8,128)(2,1)S(1)}, u32[]{:S(2)}, u32[]{:S(2)}) collective-permute-start(bf16[2,1,16,384]{3,2,1,0:T(8,128)(2,1)S(1)} %maximum_select_fusion.6), channel_id=1, source_target_pairs={{0,16},{8,24},{16,0},{24,8},{32,48},{40,56},{48,32},{56,40},{1,17}... | collective-permute-start | bytes 73736 | tf_op jit(solution)/shard_map/ppermute | solution.py:139
  39.4 20.9 %collective-permute-done.1 = bf16[2,1,16,384]{3,2,1,0:T(8,128)(2,1)S(1)} collective-permute-done((bf16[2,1,16,384]{3,2,1,0:T(8,128)(2,1)S(1)}, bf16[2,1,16,384]{3,2,1,0:T(8,128)(2,1)S(1)}, u32[]{:S(2)}, u32[]{:S(2)}) %collective-permute-start.1) | collective-permute-done | bytes 24608 | tf_op jit(solution)/shard_map/ppermute | solution.py:139
  60.3 5.5 %collective-permute-start.2 = (bf16[4,1,16,384]{3,2,1,0:T(8,128)(2,1)S(1)}, bf16[4,1,16,384]{3,2,1,0:T(8,128)(2,1)S(1)}, u32[]{:S(2)}, u32[]{:S(2)}) collective-permute-start(bf16[4,1,16,384]{3,2,1,0:T(8,128)(2,1)S(1)} %fusion.84), channel_id=1, source_target_pairs={{0,32},{8,40},{16,48},{24,56},{32,0},{40,8},{48,16},{56,24},{1,33}... | collective-permute-start | bytes 147464 | tf_op jit(solution)/shard_map/ppermute | solution.py:139
  70.9 2.4 %collective-permute-done.5 = bf16[8,1,16,384]{3,2,1,0:T(8,128)(2,1)S(1)} collective-permute-done((bf16[8,1,16,384]{3,2,1,0:T(8,128)(2,1)S(1)}, bf16[8,1,16,384]{3,2,1,0:T(8,128)(2,1)S(1)}, u32[]{:S(2)}, u32[]{:S(2)}) %collective-permute-start.5) | collective-permute-done | bytes 98336 | tf_op jit(solution)/shard_map/ppermute | solution.py:153
  73.3 1.8 collective-permute-done.4
  75.2 4.9 %collective-permute-start.6 = (bf16[512,384]{1,0:T(8,128)(2,1)S(1)}, bf16[512,384]{1,0:T(8,128)(2,1)}, u32[]{:S(2)}, u32[]{:S(2)}) collective-permute-start(bf16[512,384]{1,0:T(8,128)(2,1)S(1)} %bitcast.82), channel_id=1, source_target_pairs={{0,1},{1,0},{2,3},{3,2},{4,5},{5,4},{6,7},{7,6},{8,9},{9,8},{10,11... | collective-permute-start | bytes 1179656 | tf_op jit(solution)/shard_map/ppermute | solution.py:28
  81.0 1.7 reduce_sum.85
  82.8 1.7 constant_dynamic-slice_fusion.2
  84.6 3.9 %weights.1 = (bf16[512,384]{1,0:T(8,128)(2,1)}, bf16[512,384]{1,0:T(8,128)(2,1)}, bf16[192,384]{1,0:T(8,128)(2,1)}, bf16[192,384]{1,0:T(8,128)(2,1)}) custom-call(s32[1]{0:T(128)} %bitcast.core, bf16[512,1024]{1,0:T(8,128)(2,1)} %bitcast.3.columns, s32[1,256]{1,0:T(1,128)} %bitcast.94, bf16[512,128]{1,0:T(8,128)(2,1)} %bitcast.88, ...), custom_call_target="tpu_custom_call" | custom-call | tf_op jit(solution)/shard_map/weights/pallas_call | solution.py:105
  89.5 3.0 %collective-permute-start.9 = (bf16[192,384]{1,0:T(8,128)(2,1)S(1)}, bf16[192,384]{1,0:T(8,128)(2,1)S(1)}, u32[]{:S(2)}, u32[]{:S(2)}) collective-permute-start(bf16[192,384]{1,0:T(8,128)(2,1)S(1)} %fusion.46), channel_id=1, source_target_pairs={{0,192},{64,128},{128,64},{192,0},{1,193},{65,129},{129,65},{193,1... | collective-permute-start | bytes 442376 | tf_op jit(solution)/shard_map/ppermute | solution.py:36
  93.5 2.9 %collective-permute-done.9 = bf16[192,384]{1,0:T(8,128)(2,1)S(1)} collective-permute-done((bf16[192,384]{1,0:T(8,128)(2,1)S(1)}, bf16[192,384]{1,0:T(8,128)(2,1)S(1)}, u32[]{:S(2)}, u32[]{:S(2)}) %collective-permute-start.9) | collective-permute-done | bytes 147488 | tf_op jit(solution)/shard_map/ppermute | solution.py:36
  103.1 1.8 collective-permute-done.8
  108.0 2.4 %collective-permute-start.11 = (f32[512,384]{1,0:T(8,128)S(1)}, f32[512,384]{1,0:T(8,128)S(1)}, u32[]{:S(2)}, u32[]{:S(2)}) collective-permute-start(f32[512,384]{1,0:T(8,128)S(1)} %fusion.78), channel_id=1, source_target_pairs={{0,1},{1,0},{2,3},{3,2},{4,5},{5,4},{6,7},{7,6},{8,9},{9,8},{10,11... | collective-permute-start | bytes 2359304 | tf_op jit(solution)/shard_map/ppermute | solution.py:28
  113.7 6.9 %all-to-all-start.2 = ((bf16[32,56,128]{2,1,0:T(8,128)(2,1)}), bf16[32,56,128]{2,1,0:T(8,128)(2,1)}, u32[]{:S(2)}, u32[]{:S(2)}) async-start(bf16[32,56,128]{2,1,0:T(8,128)(2,1)} %pad_maximum_fusion), calls=%async_computation.2 | async-start | bytes 917504 | tf_op jit(solution)/shard_map/all_to_all | solution.py:327
  123.3 12.7 %all-to-all-done.2 = bf16[32,56,128]{2,1,0:T(8,128)(2,1)} async-done(((bf16[32,56,128]{2,1,0:T(8,128)(2,1)}), bf16[32,56,128]{2,1,0:T(8,128)(2,1)}, u32[]{:S(2)}, u32[]{:S(2)}) %all-to-all-start.2) | async-done | bytes 458784 | tf_op jit(solution)/shard_map/all_to_all | solution.py:327
  138.8 4.8 %all-to-all-start.3 = ((bf16[32,16,384]{2,1,0:T(8,128)(2,1)}), bf16[32,16,384]{2,1,0:T(8,128)(2,1)}, u32[]{:S(2)}, u32[]{:S(2)}) async-start(bf16[32,16,384]{2,1,0:T(8,128)(2,1)} %broadcast_in_dim.142), calls=%async_computation.3 | async-start | bytes 786432 | tf_op jit(solution)/shard_map/all_to_all | solution.py:130
  144.3 12.1 %all-to-all-done.3 = bf16[32,16,384]{2,1,0:T(8,128)(2,1)} async-done(((bf16[32,16,384]{2,1,0:T(8,128)(2,1)}), bf16[32,16,384]{2,1,0:T(8,128)(2,1)}, u32[]{:S(2)}, u32[]{:S(2)}) %all-to-all-start.3) | async-done | bytes 393248 | tf_op jit(solution)/shard_map/all_to_all | solution.py:130
  156.4 3.5 %collective-permute-start.14 = (bf16[512,384]{1,0:T(8,128)(2,1)}, bf16[512,384]{1,0:T(8,128)(2,1)}, u32[]{:S(2)}, u32[]{:S(2)}) collective-permute-start(bf16[512,384]{1,0:T(8,128)(2,1)} %bitcast.27.dual_own), channel_id=1, source_target_pairs={{0,1},{1,0},{2,3},{3,2},{4,5},{5,4},{6,7},{7,6},{8,9},{9,8},{10,11... | collective-permute-start | bytes 1179656 | tf_op jit(solution)/shard_map/ppermute | solution.py:28
  159.9 2.5 %fusion.58 = f32[384,128]{1,0:T(8,128)} fusion(f32[384,128]{1,0:T(8,128)} %param.33, s32[384]{0:T(512)} %copy-done.22, f32[128]{0:T(128)S(1)} %get-tuple-element.52, f32[128]{0:T(128)S(1)} %get-tuple-element.51, pred[384]{0:T(512)(128)(4,1)S(1)} %fusion.95, f32[384,128]{1,0:T(8,128)} %param.30, f32[384,128]{1,0:T(8,128)} %get-tuple-element.53), kind=kOutput, calls=%fused_computation.104 | convolution fusion | flops 227622912 | bytes 789376 | tf_op jit(solution)/shard_map/dot_general | solution.py:180
  162.4 2.6 %prices.1 = (bf16[192,384]{1,0:T(8,128)(2,1)}, bf16[192,384]{1,0:T(8,128)(2,1)}) custom-call(bf16[512,384]{1,0:T(8,128)(2,1)} %bitcast.27.dual_own, bf16[512,384]{1,0:T(8,128)(2,1)} %collective-permute-done.14.dual_other, bf16[512,384]{1,0:T(8,128)(2,1)} %get-tuple-element.13.weight_own, bf16[512,384]{1,0:T(8,128)(2,1)} %get-tuple-element.14.weight_other), custom_call_target="tpu_custom_call" | custom-call | tf_op jit(solution)/shard_map/prices/pallas_call | solution.py:118
  168.7 4.1 %collective-permute-done.17 = bf16[192,384]{1,0:T(8,128)(2,1)S(1)} collective-permute-done((bf16[192,384]{1,0:T(8,128)(2,1)S(1)}, bf16[192,384]{1,0:T(8,128)(2,1)S(1)}, u32[]{:S(2)}, u32[]{:S(2)}) %collective-permute-start.17) | collective-permute-done | bytes 147488 | tf_op jit(solution)/shard_map/ppermute | solution.py:36
  176.4 2.0 collective-permute-done.18
  183.6 2.3 %collective-permute-start.19 = (f32[512,384]{1,0:T(8,128)S(1)}, f32[512,384]{1,0:T(8,128)S(1)}, u32[]{:S(2)}, u32[]{:S(2)}) collective-permute-start(f32[512,384]{1,0:T(8,128)S(1)} %fusion.77), channel_id=1, source_target_pairs={{0,1},{1,0},{2,3},{3,2},{4,5},{5,4},{6,7},{7,6},{8,9},{9,8},{10,11... | collective-permute-start | bytes 2359304 | tf_op jit(solution)/shard_map/ppermute | solution.py:28
  186.2 1.7 collective-permute-done.20
  189.2 4.0 %all-to-all-start.4 = ((bf16[32,56,128]{2,1,0:T(8,128)(2,1)}), bf16[32,56,128]{2,1,0:T(8,128)(2,1)S(1)}, u32[]{:S(2)}, u32[]{:S(2)}) async-start(bf16[32,56,128]{2,1,0:T(8,128)(2,1)} %pad_maximum_fusion.1), calls=%async_computation.4 | async-start | bytes 917504 | tf_op jit(solution)/shard_map/all_to_all | solution.py:327
  193.3 2.5 %fusion.60 = f32[384,128]{1,0:T(8,128)} fusion(f32[384,128]{1,0:T(8,128)} %fusion.58, s32[384]{0:T(512)S(1)} %copy-done.23, f32[128]{0:T(128)S(1)} %get-tuple-element.52, f32[128]{0:T(128)S(1)} %get-tuple-element.51, pred[384]{0:T(512)(128)(4,1)S(1)} %fusion.95, f32[384,128]{1,0:T(8,128)} %get-tuple-element.53, f32[384,128]{1,0:T(8,128)} %get-tuple-element.54), kind=kOutput, calls=%fused_computation.106 | convolution fusion | flops 227622912 | bytes 789376 | tf_op jit(solution)/shard_map/dot_general | solution.py:180
  195.8 13.0 %all-to-all-done.4 = bf16[32,56,128]{2,1,0:T(8,128)(2,1)S(1)} async-done(((bf16[32,56,128]{2,1,0:T(8,128)(2,1)}), bf16[32,56,128]{2,1,0:T(8,128)(2,1)S(1)}, u32[]{:S(2)}, u32[]{:S(2)}) %all-to-all-start.4) | async-done | bytes 458784 | tf_op jit(solution)/shard_map/all_to_all | solution.py:327
  (183 shorter events, 50.8 us)
Async XLA Ops:
  2.6 22.3 %all-to-all-start = ((s32[64,1,8]{2,1,0:T(1,128)}), s32[64,1,8]{2,1,0:T(1,128)S(1)}, u32[]{:S(2)}, u32[]{:S(2)}) async-start(s32[64,1,8]{2,1,0:T(1,128)} %bitcast.1), calls=%async_computation | async-start | bytes 65536 | tf_op jit(solution)/shard_map/all_to_all | solution.py:231
  16.3 20.7 %collective-permute-start = (bf16[1,1,16,384]{3,2,1,0:T(8,128)(2,1)S(1)}, bf16[1,1,16,384]{3,2,1,0:T(8,128)(2,1)S(1)}, u32[]{:S(2)}, u32[]{:S(2)}) collective-permute-start(bf16[1,1,16,384]{3,2,1,0:T(8,128)(2,1)S(1)} %get-tuple-element.44), channel_id=1, source_target_pairs={{0,8},{8,0},{16,24},{24,16},{32,40},{40,32},{48,56},{56,48},{1,9},... | collective-permute-start | bytes 36872 | tf_op jit(solution)/shard_map/ppermute | solution.py:139
  22.0 88.7 %collective-permute-start.12 = (f32[512,384]{1,0:T(8,128)}, f32[512,384]{1,0:T(8,128)}, u32[]{:S(2)}, u32[]{:S(2)}) collective-permute-start(f32[512,384]{1,0:T(8,128)} %bitcast.22), channel_id=1, source_target_pairs={{0,1},{1,0},{2,3},{3,2},{4,5},{5,4},{6,7},{7,6},{8,9},{9,8},{10,11... | collective-permute-start | bytes 2359304 | tf_op jit(solution)/shard_map/ppermute | solution.py:28
  28.8 39.9 %copy-start.29 = (f32[128]{0:T(128)S(1)}, f32[128]{0:T(128)}, u32[]{:S(2)}) copy-start(f32[128]{0:T(128)} %param.27) | copy-start | bytes 1540
  28.8 55.8 %all-to-all-start.1 = ((bf16[64,8,1024]{2,1,0:T(8,128)(2,1)}), bf16[64,8,1024]{2,1,0:T(8,128)(2,1)}, u32[]{:S(2)}, u32[]{:S(2)}) async-start(bf16[64,8,1024]{2,1,0:T(8,128)(2,1)} %fusion.2), calls=%async_computation.1 | async-start | bytes 2097152 | tf_op jit(solution)/shard_map/all_to_all | solution.py:242
  36.9 45.8 %copy-start.30 = (f32[128]{0:T(128)S(1)}, f32[128]{0:T(128)}, u32[]{:S(2)}) copy-start(f32[128]{0:T(128)} %param.28) | copy-start | bytes 1540
  37.0 23.3 %collective-permute-start.1 = (bf16[2,1,16,384]{3,2,1,0:T(8,128)(2,1)S(1)}, bf16[2,1,16,384]{3,2,1,0:T(8,128)(2,1)S(1)}, u32[]{:S(2)}, u32[]{:S(2)}) collective-permute-start(bf16[2,1,16,384]{3,2,1,0:T(8,128)(2,1)S(1)} %maximum_select_fusion.6), channel_id=1, source_target_pairs={{0,16},{8,24},{16,0},{24,8},{32,48},{40,56},{48,32},{56,40},{1,17}... | collective-permute-start | bytes 73736 | tf_op jit(solution)/shard_map/ppermute | solution.py:139
  39.3 45.2 %copy-start.24 = (f32[256]{0:T(256)S(1)}, f32[256]{0:T(256)}, u32[]{:S(2)}) copy-start(f32[256]{0:T(256)} %param.22) | copy-start | bytes 3076
  60.3 7.0 %collective-permute-start.2 = (bf16[4,1,16,384]{3,2,1,0:T(8,128)(2,1)S(1)}, bf16[4,1,16,384]{3,2,1,0:T(8,128)(2,1)S(1)}, u32[]{:S(2)}, u32[]{:S(2)}) collective-permute-start(bf16[4,1,16,384]{3,2,1,0:T(8,128)(2,1)S(1)} %fusion.84), channel_id=1, source_target_pairs={{0,32},{8,40},{16,48},{24,56},{32,0},{40,8},{48,16},{56,24},{1,33}... | collective-permute-start | bytes 147464 | tf_op jit(solution)/shard_map/ppermute | solution.py:139
  67.3 3.6 %collective-permute-start.3 = (bf16[8,1,16,384]{3,2,1,0:T(8,128)(2,1)S(1)}, bf16[8,1,16,384]{3,2,1,0:T(8,128)(2,1)S(1)}, u32[]{:S(2)}, u32[]{:S(2)}) collective-permute-start(bf16[8,1,16,384]{3,2,1,0:T(8,128)(2,1)S(1)} %maximum_select_fusion.3), channel_id=1, source_target_pairs={{0,2},{2,0},{4,6},{6,4},{1,3},{3,1},{5,7},{7,5},{8,10},{10,8},{12,... | collective-permute-start | bytes 294920 | tf_op jit(solution)/shard_map/ppermute | solution.py:153
  68.6 37.5 %copy-start.32 = (f32[128]{0:T(128)}, f32[128]{0:T(128)S(1)}, u32[]{:S(2)}) copy-start(f32[128]{0:T(128)S(1)} %broadcast_multiply_fusion.2) | copy-start | bytes 1540
  68.6 4.7 %collective-permute-start.5 = (bf16[8,1,16,384]{3,2,1,0:T(8,128)(2,1)S(1)}, bf16[8,1,16,384]{3,2,1,0:T(8,128)(2,1)S(1)}, u32[]{:S(2)}, u32[]{:S(2)}) collective-permute-start(bf16[8,1,16,384]{3,2,1,0:T(8,128)(2,1)S(1)} %maximum_select_fusion.3), channel_id=1, source_target_pairs={{0,6},{2,4},{4,2},{6,0},{1,7},{3,5},{5,3},{7,1},{8,14},{10,12},{12... | collective-permute-start | bytes 294920 | tf_op jit(solution)/shard_map/ppermute | solution.py:153
  70.0 5.1 %collective-permute-start.4 = (bf16[8,1,16,384]{3,2,1,0:T(8,128)(2,1)S(1)}, bf16[8,1,16,384]{3,2,1,0:T(8,128)(2,1)S(1)}, u32[]{:S(2)}, u32[]{:S(2)}) collective-permute-start(bf16[8,1,16,384]{3,2,1,0:T(8,128)(2,1)S(1)} %maximum_select_fusion.3), channel_id=1, source_target_pairs={{0,4},{2,6},{4,0},{6,2},{1,5},{3,7},{5,1},{7,3},{8,12},{10,14},{12... | collective-permute-start | bytes 294920 | tf_op jit(solution)/shard_map/ppermute | solution.py:153
  75.2 9.4 %collective-permute-start.6 = (bf16[512,384]{1,0:T(8,128)(2,1)S(1)}, bf16[512,384]{1,0:T(8,128)(2,1)}, u32[]{:S(2)}, u32[]{:S(2)}) collective-permute-start(bf16[512,384]{1,0:T(8,128)(2,1)S(1)} %bitcast.82), channel_id=1, source_target_pairs={{0,1},{1,0},{2,3},{3,2},{4,5},{5,4},{6,7},{7,6},{8,9},{9,8},{10,11... | collective-permute-start | bytes 1179656 | tf_op jit(solution)/shard_map/ppermute | solution.py:28
  80.2 25.9 %copy-start.22 = (s32[384]{0:T(512)}, s32[384]{0:T(512)S(1)}, u32[]{:S(2)}) copy-start(s32[384]{0:T(512)S(1)} %add_select_fusion) | copy-start | bytes 4612
  82.8 29.5 %copy-start.20 = (bf16[8]{0:T(256)(128)(2,1)}, bf16[8]{0:T(256)(128)(2,1)S(1)}, u32[]{:S(2)}) copy-start(bf16[8]{0:T(256)(128)(2,1)S(1)} %pad.23.clone) | copy-start | bytes 52
  89.5 7.0 %collective-permute-start.9 = (bf16[192,384]{1,0:T(8,128)(2,1)S(1)}, bf16[192,384]{1,0:T(8,128)(2,1)S(1)}, u32[]{:S(2)}, u32[]{:S(2)}) collective-permute-start(bf16[192,384]{1,0:T(8,128)(2,1)S(1)} %fusion.46), channel_id=1, source_target_pairs={{0,192},{64,128},{128,64},{192,0},{1,193},{65,129},{129,65},{193,1... | collective-permute-start | bytes 442376 | tf_op jit(solution)/shard_map/ppermute | solution.py:36
  93.4 5.2 %collective-permute-start.7 = (bf16[192,384]{1,0:T(8,128)(2,1)S(1)}, bf16[192,384]{1,0:T(8,128)(2,1)S(1)}, u32[]{:S(2)}, u32[]{:S(2)}) collective-permute-start(bf16[192,384]{1,0:T(8,128)(2,1)S(1)} %fusion.47), channel_id=1, source_target_pairs={{0,64},{64,0},{128,192},{192,128},{1,65},{65,1},{129,193},{193,129... | collective-permute-start | bytes 442376 | tf_op jit(solution)/shard_map/ppermute | solution.py:36
  97.4 4.7 %collective-permute-start.10 = (bf16[192,384]{1,0:T(8,128)(2,1)S(1)}, bf16[192,384]{1,0:T(8,128)(2,1)S(1)}, u32[]{:S(2)}, u32[]{:S(2)}) collective-permute-start(bf16[192,384]{1,0:T(8,128)(2,1)S(1)} %fusion.54), channel_id=1, source_target_pairs={{0,64},{64,0},{128,192},{192,128},{1,65},{65,1},{129,193},{193,129... | collective-permute-start | bytes 442376 | tf_op jit(solution)/shard_map/ppermute | solution.py:36
  99.6 5.3 %collective-permute-start.8 = (bf16[192,384]{1,0:T(8,128)(2,1)S(1)}, bf16[192,384]{1,0:T(8,128)(2,1)S(1)}, u32[]{:S(2)}, u32[]{:S(2)}) collective-permute-start(bf16[192,384]{1,0:T(8,128)(2,1)S(1)} %fusion.53), channel_id=1, source_target_pairs={{0,192},{64,128},{128,64},{192,0},{1,193},{65,129},{129,65},{193,1... | collective-permute-start | bytes 442376 | tf_op jit(solution)/shard_map/ppermute | solution.py:36
  108.0 4.4 %collective-permute-start.11 = (f32[512,384]{1,0:T(8,128)S(1)}, f32[512,384]{1,0:T(8,128)S(1)}, u32[]{:S(2)}, u32[]{:S(2)}) collective-permute-start(f32[512,384]{1,0:T(8,128)S(1)} %fusion.78), channel_id=1, source_target_pairs={{0,1},{1,0},{2,3},{3,2},{4,5},{5,4},{6,7},{7,6},{8,9},{9,8},{10,11... | collective-permute-start | bytes 2359304 | tf_op jit(solution)/shard_map/ppermute | solution.py:28
  110.5 1.8 collective-permute-start.13
  113.7 22.4 %all-to-all-start.2 = ((bf16[32,56,128]{2,1,0:T(8,128)(2,1)}), bf16[32,56,128]{2,1,0:T(8,128)(2,1)}, u32[]{:S(2)}, u32[]{:S(2)}) async-start(bf16[32,56,128]{2,1,0:T(8,128)(2,1)} %pad_maximum_fusion), calls=%async_computation.2 | async-start | bytes 917504 | tf_op jit(solution)/shard_map/all_to_all | solution.py:327
  138.8 17.6 %all-to-all-start.3 = ((bf16[32,16,384]{2,1,0:T(8,128)(2,1)}), bf16[32,16,384]{2,1,0:T(8,128)(2,1)}, u32[]{:S(2)}, u32[]{:S(2)}) async-start(bf16[32,16,384]{2,1,0:T(8,128)(2,1)} %broadcast_in_dim.142), calls=%async_computation.3 | async-start | bytes 786432 | tf_op jit(solution)/shard_map/all_to_all | solution.py:130
  156.4 6.0 %collective-permute-start.14 = (bf16[512,384]{1,0:T(8,128)(2,1)}, bf16[512,384]{1,0:T(8,128)(2,1)}, u32[]{:S(2)}, u32[]{:S(2)}) collective-permute-start(bf16[512,384]{1,0:T(8,128)(2,1)} %bitcast.27.dual_own), channel_id=1, source_target_pairs={{0,1},{1,0},{2,3},{3,2},{4,5},{5,4},{6,7},{7,6},{8,9},{9,8},{10,11... | collective-permute-start | bytes 1179656 | tf_op jit(solution)/shard_map/ppermute | solution.py:28
  166.1 6.7 %collective-permute-start.17 = (bf16[192,384]{1,0:T(8,128)(2,1)S(1)}, bf16[192,384]{1,0:T(8,128)(2,1)S(1)}, u32[]{:S(2)}, u32[]{:S(2)}) collective-permute-start(bf16[192,384]{1,0:T(8,128)(2,1)S(1)} %fusion.32), channel_id=1, source_target_pairs={{0,192},{64,128},{128,64},{192,0},{1,193},{65,129},{129,65},{193,1... | collective-permute-start | bytes 442376 | tf_op jit(solution)/shard_map/ppermute | solution.py:36
  168.6 5.2 %collective-permute-start.15 = (bf16[192,384]{1,0:T(8,128)(2,1)S(1)}, bf16[192,384]{1,0:T(8,128)(2,1)S(1)}, u32[]{:S(2)}, u32[]{:S(2)}) collective-permute-start(bf16[192,384]{1,0:T(8,128)(2,1)S(1)} %fusion.33), channel_id=1, source_target_pairs={{0,64},{64,0},{128,192},{192,128},{1,65},{65,1},{129,193},{193,129... | collective-permute-start | bytes 442376 | tf_op jit(solution)/shard_map/ppermute | solution.py:36
  173.8 4.6 %collective-permute-start.18 = (bf16[192,384]{1,0:T(8,128)(2,1)S(1)}, bf16[192,384]{1,0:T(8,128)(2,1)S(1)}, u32[]{:S(2)}, u32[]{:S(2)}) collective-permute-start(bf16[192,384]{1,0:T(8,128)(2,1)S(1)} %fusion.56), channel_id=1, source_target_pairs={{0,64},{64,0},{128,192},{192,128},{1,65},{65,1},{129,193},{193,129... | collective-permute-start | bytes 442376 | tf_op jit(solution)/shard_map/ppermute | solution.py:36
  174.9 5.6 %collective-permute-start.16 = (bf16[192,384]{1,0:T(8,128)(2,1)S(1)}, bf16[192,384]{1,0:T(8,128)(2,1)S(1)}, u32[]{:S(2)}, u32[]{:S(2)}) collective-permute-start(bf16[192,384]{1,0:T(8,128)(2,1)S(1)} %fusion.55), channel_id=1, source_target_pairs={{0,192},{64,128},{128,64},{192,0},{1,193},{65,129},{129,65},{193,1... | collective-permute-start | bytes 442376 | tf_op jit(solution)/shard_map/ppermute | solution.py:36
  183.6 4.3 %collective-permute-start.19 = (f32[512,384]{1,0:T(8,128)S(1)}, f32[512,384]{1,0:T(8,128)S(1)}, u32[]{:S(2)}, u32[]{:S(2)}) collective-permute-start(f32[512,384]{1,0:T(8,128)S(1)} %fusion.77), channel_id=1, source_target_pairs={{0,1},{1,0},{2,3},{3,2},{4,5},{5,4},{6,7},{7,6},{8,9},{9,8},{10,11... | collective-permute-start | bytes 2359304 | tf_op jit(solution)/shard_map/ppermute | solution.py:28
  186.0 1.8 collective-permute-start.20
  189.2 19.5 %all-to-all-start.4 = ((bf16[32,56,128]{2,1,0:T(8,128)(2,1)}), bf16[32,56,128]{2,1,0:T(8,128)(2,1)S(1)}, u32[]{:S(2)}, u32[]{:S(2)}) async-start(bf16[32,56,128]{2,1,0:T(8,128)(2,1)} %pad_maximum_fusion.1), calls=%async_computation.4 | async-start | bytes 917504 | tf_op jit(solution)/shard_map/all_to_all | solution.py:327
  (32 other events, 473.8 us)

commit v4 on v3

--- a/solution.py
+++ b/solution.py
@@ -32,15 +32,18 @@
 CONTRACT_MINOR = (((1,), (1,)), ((), ()))
 
 
+def from_side(x, step):
+    return lax.ppermute(x, "lines", [(i, i ^ step) for i in range(4)])
+
+
 def with_side(x, step):
-    other = lax.ppermute(x.astype(jnp.bfloat16), "lines", [(i, i ^ step) for i in range(4)])
-    return x + other.astype(jnp.float32)
-
-
-def sum_over_lines(halves):
-    first, second = (rounded(half.astype(jnp.float32)) for half in halves)
-    first, second = rounded(with_side(first, 1)), rounded(with_side(second, 3))
-    return jnp.concatenate([with_side(first, 3), with_side(second, 1)], axis=0)
+    other = from_side(x, step)
+    return (x.astype(jnp.float32) + other.astype(jnp.float32)).astype(jnp.bfloat16)
+
+
+def summed_pairs(halves):
+    first, second = with_side(halves[0], 1), with_side(halves[1], 3)
+    return first, from_side(first, 3), second, from_side(second, 1)
 
 
 def store_price(dual_own, dual_other, weight_own, weight_other, first, second):
@@ -90,8 +93,12 @@
     store_price(dual_own, dual_other, weight_own, weight_other, first, second)
 
 
+def in_fast(*arrays):
+    return tuple(pltpu.with_memory_space_constraint(x, pltpu.VMEM) for x in arrays)
+
+
 def half_prices(row_count, units):
-    half = jax.ShapeDtypeStruct((row_count // 2, units), jnp.bfloat16)
+    half = pltpu.VMEM((row_count // 2, units), jnp.bfloat16)
     return (half, half)
 
 
@@ -99,7 +106,7 @@
     half_lines, row_count = dual_own.shape
     gen_count = column.shape[0]
     units = gen_count + stor_own.shape[1]
-    weight = jax.ShapeDtypeStruct((half_lines, units), jnp.bfloat16)
+    weight = pltpu.VMEM((half_lines, units), jnp.bfloat16)
     in_vmem = pl.BlockSpec(memory_space=pltpu.VMEM)
     share_len = columns.shape[1] // (Z * X * CORES)
     own, other, first, second = pl.pallas_call(
@@ -109,7 +116,12 @@
         out_specs=(in_vmem,) * 4,
         scratch_shapes=[pltpu.VMEM((Z * X * CORES, share_len, gen_count), jnp.bfloat16)],
         name="weights",
-    )(core.reshape(1), columns, column.reshape(1, -1), stor_own, stor_other, dual_own, dual_other)
+    )(
+        core.reshape(1),
+        *in_fast(columns),
+        column.reshape(1, -1),
+        *in_fast(stor_own, stor_other, dual_own, dual_other),
+    )
     return own, other, (first, second)
 
 
@@ -121,7 +133,85 @@
         in_specs=[in_vmem] * 4,
         out_specs=(in_vmem,) * 2,
         name="prices",
-    )(dual_own, dual_other, weight_own, weight_other)
+    )(*in_fast(dual_own, dual_other, weight_own, weight_other))
+
+
+def update_body(*refs):
+    (
+        first,
+        first_far,
+        second,
+        second_far,
+        level,
+        gen_quad,
+        gen_lin,
+        gen_max,
+        stor_quad,
+        stor_rate,
+        back,
+        gen_now,
+        stor_now,
+        *old,
+        bar_low,
+        gen_next,
+        stor_next,
+        total,
+    ) = refs
+    row_count, gen_count = gen_now.shape
+    half = row_count // 2
+    bars = []
+    for i, (near, far) in enumerate(((first, first_far), (second, second_far))):
+        rows = slice(i * half, (i + 1) * half)
+        price = near[...].astype(jnp.float32) + far[...].astype(jnp.float32)
+        gen, stor = gen_now[rows], stor_now[rows]
+        gen_mid, stor_mid = gen, stor
+        if old:
+            gen_mid = gen + THETA * (gen - old[0][rows])
+            stor_mid = stor + THETA * (stor - old[1][rows])
+        gen_grad = 2.0 * gen_quad[...] * gen_mid + gen_lin[...] + level[rows] + price[:, :gen_count]
+        moved = jnp.clip(gen_mid - TAU * gen_grad, 0.0, gen_max[...])
+        stor_grad = 2.0 * stor_quad[...] * stor_mid + level[rows] + price[:, gen_count:] + back[rows]
+        rate = stor_rate[...]
+        shifted = jnp.clip(stor_mid - TAU * stor_grad, -rate, rate)
+        gen_next[rows] = moved
+        stor_next[rows] = shifted
+        bar = jnp.concatenate([2.0 * moved - gen, 2.0 * shifted - stor], axis=1)
+        bar_low[rows] = bar.astype(jnp.bfloat16)
+        bars.append(bar)
+    total[...] = lax.dot_general(
+        jnp.ones((8, bars[0].shape[1]), jnp.float32),
+        jnp.concatenate(bars, axis=0),
+        CONTRACT_MINOR,
+        precision=lax.Precision.HIGHEST,
+        preferred_element_type=jnp.float32,
+    )
+
+
+def updated(pairs, level, gen_params, stor_params, back, gen_now, stor_now, old):
+    row_count, gen_count = gen_now.shape
+    stor_count = stor_now.shape[1]
+    operands = (
+        *in_fast(*pairs, level[:, None]),
+        *(value[None, :] for value in gen_params),
+        *(value[None, :] for value in stor_params),
+        *in_fast(back),
+        gen_now,
+        stor_now,
+        *old,
+    )
+    in_vmem = pl.BlockSpec(memory_space=pltpu.VMEM)
+    return pl.pallas_call(
+        update_body,
+        out_shape=(
+            pltpu.VMEM((row_count, gen_count + stor_count), jnp.bfloat16),
+            pltpu.VMEM((row_count, gen_count), jnp.float32),
+            pltpu.VMEM((row_count, stor_count), jnp.float32),
+            pltpu.VMEM((8, row_count), jnp.float32),
+        ),
+        in_specs=[in_vmem] * len(operands),
+        out_specs=(in_vmem,) * 4,
+        name="update",
+    )(*operands)
 
 
 def sent_to_chips(x):
@@ -258,11 +348,10 @@
         dual_own,
         dual_other,
     )
-    load_own, load_other = by_core(
-        lax.dot_general(
-            ptdf, load.astype(jnp.bfloat16), CONTRACT_MINOR, preferred_element_type=jnp.float32
-        )
-    )
+    load_part = lax.dot_general(
+        ptdf, load.astype(jnp.bfloat16), CONTRACT_MINOR, preferred_element_type=jnp.float32
+    )
+    load_own, load_other = by_core(load_part)
     load_flow = load_own + swapped(load_other)
     load_total = jnp.sum(load, axis=1)
 
@@ -277,28 +366,21 @@
     gen_old, stor_old = (gen_start, stor_start)
     price_level, dual_store = (lam_start, omega_start)
     for iteration in range(2):
-        if iteration == 0:
-            gen_mid, stor_mid = (gen_now, stor_now)
-        else:
-            gen_mid = gen_now + THETA * (gen_now - gen_old)
-            stor_mid = stor_now + THETA * (stor_now - stor_old)
         if iteration > 0:
             halves = later_prices(dual_own, dual_other, weight_own, weight_other)
-        price = sum_over_lines(halves)
-        gen_price, stor_price = price[:, :gen_count], price[:, gen_count:]
-        gen_grad = 2.0 * gen_quad * gen_mid + gen_lin + price_level[:, None] + gen_price
-        gen_next = jnp.clip(gen_mid - TAU * gen_grad, 0.0, gen_max)
-        stor_grad = (
-            2.0 * stor_quad * stor_mid
-            + price_level[:, None]
-            + stor_price
-            + summed_hours(dual_store, True)
-        )
-        stor_next = jnp.clip(stor_mid - TAU * stor_grad, -stor_rate, stor_rate)
-        gen_bar = 2.0 * gen_next - gen_now
+        back = summed_hours(dual_store, True)
+        bar_low, gen_next, stor_next, total = updated(
+            summed_pairs(halves),
+            price_level,
+            (gen_quad, gen_lin, gen_max),
+            (stor_quad, stor_rate),
+            back,
+            gen_now,
+            stor_now,
+            (gen_old, stor_old) if iteration > 0 else (),
+        )
+        balance = total[0] - load_total
         stor_bar = 2.0 * stor_next - stor_now
-        balance = jnp.sum(gen_bar, axis=1) + jnp.sum(stor_bar, axis=1) - load_total
-        bar_low = jnp.concatenate([gen_bar, stor_bar], axis=1).astype(jnp.bfloat16)
         flow_other = lax.dot_general(
             weight_other, bar_low, CONTRACT_MINOR, preferred_element_type=jnp.float32
         )

time: 211 us -> 208 us (0.986)
  blocking collectives: 0 us -> 39.8 us
  starting transfers between devices: 70.5 us -> 48.3 us
  other arithmetic: 25.3 us -> 10.2 us
  waiting for transfers between devices: 82.7 us -> 72.2 us
  local copies, waits for them, and re-layouts: 7.52 us -> 10.6 us
    all_to_all x0 -> x2, blocking collectives: none -> 39.8 us  [the longest x1 22.2 us: shards(): lax.all_to_all(slot_bus.reshape(area_count, slots), AREAS, 0, 0, tiled=True)]
    all_to_all x2 -> x0, starting transfers between devices: 17.8 us -> none  [the longest x1 13 us: shards(): lax.all_to_all(slot_bus.reshape(area_count, slots), AREAS, 0, 0, tiled=True)]
    all_to_all x2 -> x0, waiting for transfers between devices: 14.3 us -> none  [the longest x1 12.1 us: sent_to_chips(): return lax.all_to_all(sent, CHIPS, 0, 0, tiled=True)]
    convert_element_type x8 -> x4, other arithmetic: 7.65 us -> 0.16 us  [with_side(): (x.astype(jnp.float32) + other.astype(jnp.float32)).astype(jnp.bfloat16)]
    unnamed x76 -> x42, local copies, waits for them, and re-layouts: 0.18 us -> 5.18 us
    dot_general x4, matrix products: 7.84 us -> 3.51 us  [summed_hours(): jnp.dot(hour_sums(values.shape[0], later), values, precision=lax.Precisio...]
    pallas_call x0 -> x2, Pallas kernels: none -> 4.24 us  [updated(): pl.pallas_call(update_body, out_shape=(pltpu.VMEM((row_count, gen_count +...]
    ppermute x3, waiting for transfers between devices: 22.4 us -> 26.3 us  [doubled(): other = lax.ppermute(x, axis, [(i, i ^ step) for i in range(size)])]
  transfers between devices with their start and end apart: 26 -> 24, of which waited for: 18 -> 16; matrix products, arithmetic and copies ran while one was open for 17% -> 11% of each run, Pallas kernels for 2% -> 1%
where the time goes in v4:
time: 208 us; the launch traced here: 207 us
  waiting for transfers between devices  72.2 us (35%)
  starting transfers between devices  48.3 us (23%)
  blocking collectives  39.8 us (19%)
  matrix products  17.6 us (8%)
  local copies, waits for them, and re-layouts  10.6 us (5%)
  other arithmetic  10.2 us (5%)
  Pallas kernels  7.12 us (3%)
    ppermute x3, waiting for transfers between devices, doubled(): other = lax.ppermute(x, axis, [(i, i ^ step) for i in range(size)])  26.3 us
    all_to_all x2, waiting for transfers between devices, shards(): received = lax.all_to_all(sent, CHIPS, 0, 0, tiled=True)  25.7 us
    all_to_all x1, blocking collectives, shards(): lax.all_to_all(slot_bus.reshape(area_count, slots), AREAS, 0, 0, tiled=True)  22.2 us
    all_to_all x1, blocking collectives, sent_to_chips(): return lax.all_to_all(sent, CHIPS, 0, 0, tiled=True)  17.6 us
    ppermute x7, starting transfers between devices, swapped(): return lax.ppermute(x, 'core', [(0, 1), (1, 0)])  14.7 us
    ppermute x8, waiting for transfers between devices, from_side(): return lax.ppermute(x, 'lines', [(i, i ^ step) for i in range(4)])  13.3 us
    all_to_all x2, starting transfers between devices, shards(): received = lax.all_to_all(sent, CHIPS, 0, 0, tiled=True)  10.4 us
    ppermute x8, starting transfers between devices, from_side(): return lax.ppermute(x, 'lines', [(i, i ^ step) for i in range(4)])  8.69 us
  transfers between devices with their start and end apart: 24, of which 16 were waited for; matrix products, arithmetic and copies ran while one was open for 11% of the time, Pallas kernels for 1%

profile of v4, /device:TPU:1, one launch (start us, length us, event | category | flops | bytes accessed | tf_op | source)
XLA Modules:
  0.0 207.0 jit_solution(13916748704599984120)
XLA Ops:
  1.8 22.2 %all_to_all.32 = s32[64,1,8]{2,1,0:T(1,128)S(1)} all-to-all(s32[64,1,8]{2,1,0:T(1,128)S(1)} %bitcast.106), channel_id=1, replica_groups=mesh['lines'=4,'z'=8,'x'=4,'core'=2] {'z','x','core'}, dimensions={0} | all-to-all | bytes 4096 | tf_op jit(solution)/shard_map/all_to_all | solution.py:321
  25.4 4.3 %fusion.2 = bf16[64,8,1024]{2,1,0:T(8,128)(2,1)} fusion(bf16[1024,1280]{1,0:T(8,128)(2,1)} %param.17, s32[512]{0:T(512)S(1)} %eq.148), kind=kOutput, calls=%fused_computation.4 | convolution fusion | flops 1343356928 | bytes 3672064 | tf_op jit(solution)/shard_map/dot_general | solution.py:329
  29.7 4.8 %all-to-all-start.1 = ((bf16[64,8,1024]{2,1,0:T(8,128)(2,1)}), bf16[64,8,1024]{2,1,0:T(8,128)(2,1)S(1)}, u32[]{:S(2)}, u32[]{:S(2)}) async-start(bf16[64,8,1024]{2,1,0:T(8,128)(2,1)} %fusion.2), calls=%async_computation.1 | async-start | bytes 2097152 | tf_op jit(solution)/shard_map/all_to_all | solution.py:332
  36.0 2.7 %fusion.8 = bf16[1024,128]{0,1:T(8,128)(2,1)S(1)} fusion(bf16[1024,1280]{1,0:T(8,128)(2,1)} %param.17, s32[128]{0:T(128)S(1)} %copy-done.15), kind=kOutput, calls=%fused_computation.13 | convolution fusion | flops 335839232 | bytes 2884096 | tf_op jit(solution)/shard_map/dot_general | solution.py:333
  39.0 19.9 %collective-permute-done = bf16[1,1,16,384]{3,2,1,0:T(8,128)(2,1)S(1)} collective-permute-done((bf16[1,1,16,384]{3,2,1,0:T(8,128)(2,1)S(1)}, bf16[1,1,16,384]{3,2,1,0:T(8,128)(2,1)S(1)}, u32[]{:S(2)}, u32[]{:S(2)}) %collective-permute-start) | collective-permute-done | bytes 12320 | tf_op jit(solution)/shard_map/ppermute | solution.py:229
  59.4 4.0 %collective-permute-done.1 = bf16[2,1,16,384]{3,2,1,0:T(8,128)(2,1)S(1)} collective-permute-done((bf16[2,1,16,384]{3,2,1,0:T(8,128)(2,1)S(1)}, bf16[2,1,16,384]{3,2,1,0:T(8,128)(2,1)S(1)}, u32[]{:S(2)}, u32[]{:S(2)}) %collective-permute-start.1) | collective-permute-done | bytes 24608 | tf_op jit(solution)/shard_map/ppermute | solution.py:229
  63.4 4.5 %collective-permute-start.2 = (bf16[4,1,16,384]{3,2,1,0:T(8,128)(2,1)S(1)}, bf16[4,1,16,384]{3,2,1,0:T(8,128)(2,1)S(1)}, u32[]{:S(2)}, u32[]{:S(2)}) collective-permute-start(bf16[4,1,16,384]{3,2,1,0:T(8,128)(2,1)S(1)} %fusion.52), channel_id=1, source_target_pairs={{0,32},{8,40},{16,48},{24,56},{32,0},{40,8},{48,16},{56,24},{1,33}... | collective-permute-start | bytes 147464 | tf_op jit(solution)/shard_map/ppermute | solution.py:229
  67.9 2.5 %collective-permute-done.2 = bf16[4,1,16,384]{3,2,1,0:T(8,128)(2,1)S(1)} collective-permute-done((bf16[4,1,16,384]{3,2,1,0:T(8,128)(2,1)S(1)}, bf16[4,1,16,384]{3,2,1,0:T(8,128)(2,1)S(1)}, u32[]{:S(2)}, u32[]{:S(2)}) %collective-permute-start.2) | collective-permute-done | bytes 49184 | tf_op jit(solution)/shard_map/ppermute | solution.py:229
  71.7 1.9 collective-permute-start.5
  74.4 2.0 collective-permute-done.5
  76.4 2.2 %collective-permute-done.4 = bf16[8,1,16,384]{3,2,1,0:T(8,128)(2,1)S(1)} collective-permute-done((bf16[8,1,16,384]{3,2,1,0:T(8,128)(2,1)S(1)}, bf16[8,1,16,384]{3,2,1,0:T(8,128)(2,1)S(1)}, u32[]{:S(2)}, u32[]{:S(2)}) %collective-permute-start.4) | collective-permute-done | bytes 98336 | tf_op jit(solution)/shard_map/ppermute | solution.py:243
  78.7 5.3 %collective-permute-start.6 = (bf16[512,384]{1,0:T(8,128)(2,1)S(1)}, bf16[512,384]{1,0:T(8,128)(2,1)S(1)}, u32[]{:S(2)}, u32[]{:S(2)}) collective-permute-start(bf16[512,384]{1,0:T(8,128)(2,1)S(1)} %bitcast.91), channel_id=1, source_target_pairs={{0,1},{1,0},{2,3},{3,2},{4,5},{5,4},{6,7},{7,6},{8,9},{9,8},{10,11... | collective-permute-start | bytes 1179656 | tf_op jit(solution)/shard_map/ppermute | solution.py:28
  84.0 4.3 %fusion.11 = f32[1024,384]{1,0:T(8,128)} fusion(bf16[1024,1280]{1,0:T(8,128)(2,1)S(1)} %copy-done.10, f32[384,1280]{1,0:T(8,128)} %param.18), kind=kOutput, calls=%fused_computation.18 | convolution fusion | flops 1007124480 | bytes 6160384 | tf_op jit(solution)/shard_map/dot_general | solution.py:351
  91.9 2.3 %weights.1 = (bf16[512,384]{1,0:T(8,128)(2,1)S(1)}, bf16[512,384]{1,0:T(8,128)(2,1)S(1)}, bf16[192,384]{1,0:T(8,128)(2,1)S(1)}, bf16[192,384]{1,0:T(8,128)(2,1)S(1)}) custom-call(s32[1]{0:T(128)} %bitcast.1.core, bf16[512,1024]{1,0:T(8,128)(2,1)S(1)} %bitcast.90, s32[1,256]{1,0:T(1,128)} %bitcast.107, bf16[512,128]{1,0:T(8,128)(2,1)S(1)} %bitcast.96, ...), custom_call_target="tpu_custom_call" | custom-call | tf_op jit(solution)/shard_map/weights/pallas_call | solution.py:112
  95.6 2.7 %constant_dynamic-slice_fusion.1 = (f32[32,1,16,384]{3,2,1,0:T(8,128)}, f32[32,1,16,384]{3,2,1,0:T(8,128)}) fusion(f32[32,2,16,384]{3,2,1,0:T(8,128)} %bitcast.97, s32[]{:T(128)S(6)} %select_n.237, s32[]{:T(128)S(6)} %select_n.238), kind=kLoop, calls=%fused_computation.134 | loop fusion | bytes 3145736 | tf_op jit(solution)/shard_map/jit(dynamic_index_in_dim)/dynamic_slice | solution.py:339
  100.5 2.0 collective-permute-start.9
  103.4 3.6 %collective-permute-done.9 = bf16[192,384]{1,0:T(8,128)(2,1)S(1)} collective-permute-done((bf16[192,384]{1,0:T(8,128)(2,1)S(1)}, bf16[192,384]{1,0:T(8,128)(2,1)S(1)}, u32[]{:S(2)}, u32[]{:S(2)}) %collective-permute-start.9) | collective-permute-done | bytes 147488 | tf_op jit(solution)/shard_map/ppermute | solution.py:36
  107.9 2.3 %collective-permute-done.8.refs_1_ = bf16[192,384]{1,0:T(8,128)(2,1)S(1)} collective-permute-done((bf16[192,384]{1,0:T(8,128)(2,1)S(1)}, bf16[192,384]{1,0:T(8,128)(2,1)S(1)}, u32[]{:S(2)}, u32[]{:S(2)}) %collective-permute-start.8) | collective-permute-done | bytes 147488 | tf_op jit(solution)/shard_map/ppermute | solution.py:36
  111.2 2.0 update.2
  113.6 2.9 %collective-permute-start.11 = (f32[512,384]{1,0:T(8,128)S(1)}, f32[512,384]{1,0:T(8,128)S(1)}, u32[]{:S(2)}, u32[]{:S(2)}) collective-permute-start(f32[512,384]{1,0:T(8,128)S(1)} %fusion.91), channel_id=1, source_target_pairs={{0,1},{1,0},{2,3},{3,2},{4,5},{5,4},{6,7},{7,6},{8,9},{9,8},{10,11... | collective-permute-start | bytes 2359304 | tf_op jit(solution)/shard_map/ppermute | solution.py:28
  119.9 6.4 %all-to-all-start.2 = ((bf16[32,56,128]{2,1,0:T(8,128)(2,1)}), bf16[32,56,128]{2,1,0:T(8,128)(2,1)S(1)}, u32[]{:S(2)}, u32[]{:S(2)}) async-start(bf16[32,56,128]{2,1,0:T(8,128)(2,1)} %pad_maximum_fusion), calls=%async_computation.2 | async-start | bytes 917504 | tf_op jit(solution)/shard_map/all_to_all | solution.py:409
  128.5 13.0 %all-to-all-done.2 = bf16[32,56,128]{2,1,0:T(8,128)(2,1)S(1)} async-done(((bf16[32,56,128]{2,1,0:T(8,128)(2,1)}), bf16[32,56,128]{2,1,0:T(8,128)(2,1)S(1)}, u32[]{:S(2)}, u32[]{:S(2)}) %all-to-all-start.2) | async-done | bytes 458784 | tf_op jit(solution)/shard_map/all_to_all | solution.py:409
  141.7 17.6 %all_to_all.33 = bf16[32,16,384]{2,1,0:T(8,128)(2,1)S(1)} all-to-all(bf16[32,16,384]{2,1,0:T(8,128)(2,1)S(1)} %broadcast_in_dim.155), channel_id=1, replica_groups=mesh['lines'=4,'z'=8,'x'=4,'core'=2] {'z','x'}, dimensions={0} | all-to-all | bytes 786432 | tf_op jit(solution)/shard_map/all_to_all | solution.py:220
  159.3 3.5 %collective-permute-start.14 = (bf16[512,384]{1,0:T(8,128)(2,1)S(1)}, bf16[512,384]{1,0:T(8,128)(2,1)S(1)}, u32[]{:S(2)}, u32[]{:S(2)}) collective-permute-start(bf16[512,384]{1,0:T(8,128)(2,1)S(1)} %bitcast.93), channel_id=1, source_target_pairs={{0,1},{1,0},{2,3},{3,2},{4,5},{5,4},{6,7},{7,6},{8,9},{9,8},{10,11... | collective-permute-start | bytes 1179656 | tf_op jit(solution)/shard_map/ppermute | solution.py:28
  165.6 2.0 collective-permute-start.17
  167.6 2.3 %collective-permute-done.15 = bf16[192,384]{1,0:T(8,128)(2,1)S(1)} collective-permute-done((bf16[192,384]{1,0:T(8,128)(2,1)S(1)}, bf16[192,384]{1,0:T(8,128)(2,1)S(1)}, u32[]{:S(2)}, u32[]{:S(2)}) %collective-permute-start.15) | collective-permute-done | bytes 147488 | tf_op jit(solution)/shard_map/ppermute | solution.py:36
  169.9 2.0 collective-permute-start.16
  172.4 2.8 %collective-permute-done.16.refs_1_ = bf16[192,384]{1,0:T(8,128)(2,1)S(1)} collective-permute-done((bf16[192,384]{1,0:T(8,128)(2,1)S(1)}, bf16[192,384]{1,0:T(8,128)(2,1)S(1)}, u32[]{:S(2)}, u32[]{:S(2)}) %collective-permute-start.16) | collective-permute-done | bytes 147488 | tf_op jit(solution)/shard_map/ppermute | solution.py:36
  176.6 2.2 %update.3 = (bf16[384,384]{1,0:T(8,128)(2,1)S(1)}, f32[384,256]{1,0:T(8,128)S(1)}, f32[384,128]{1,0:T(8,128)S(1)}, f32[8,384]{1,0:T(8,128)S(1)}) custom-call(bf16[192,384]{1,0:T(8,128)(2,1)S(1)} %add_convert_fusion.1.refs_0_, bf16[192,384]{1,0:T(8,128)(2,1)S(1)} %collective-permute-done.16.refs_1_, bf16[192,384]{1,0:T(8,128)(2,1)S(1)} %add_convert_fusion.refs_2_, ...), custom_call_target="tpu_custom_call" | custom-call | tf_op jit(solution)/shard_map/update/pallas_call | solution.py:203
  179.2 2.4 %collective-permute-start.19 = (f32[512,384]{1,0:T(8,128)S(1)}, f32[512,384]{1,0:T(8,128)S(1)}, u32[]{:S(2)}, u32[]{:S(2)}) collective-permute-start(f32[512,384]{1,0:T(8,128)S(1)} %fusion.92), channel_id=1, source_target_pairs={{0,1},{1,0},{2,3},{3,2},{4,5},{5,4},{6,7},{7,6},{8,9},{9,8},{10,11... | collective-permute-start | bytes 2359304 | tf_op jit(solution)/shard_map/ppermute | solution.py:28
  186.2 4.0 %all-to-all-start.4 = ((bf16[32,56,128]{2,1,0:T(8,128)(2,1)}), bf16[32,56,128]{2,1,0:T(8,128)(2,1)S(1)}, u32[]{:S(2)}, u32[]{:S(2)}) async-start(bf16[32,56,128]{2,1,0:T(8,128)(2,1)} %pad_maximum_fusion.1), calls=%async_computation.4 | async-start | bytes 917504 | tf_op jit(solution)/shard_map/all_to_all | solution.py:409
  193.0 12.7 %all-to-all-done.4 = bf16[32,56,128]{2,1,0:T(8,128)(2,1)S(1)} async-done(((bf16[32,56,128]{2,1,0:T(8,128)(2,1)}), bf16[32,56,128]{2,1,0:T(8,128)(2,1)S(1)}, u32[]{:S(2)}, u32[]{:S(2)}) %all-to-all-start.4) | async-done | bytes 458784 | tf_op jit(solution)/shard_map/all_to_all | solution.py:409
  (138 shorter events, 36.8 us)
Async XLA Ops:
  0.6 126.5 %copy-start = (f32[32768]{0:T(1024)S(1)}, f32[32768]{0:T(1024)}, u32[]{:S(2)}) copy-start(f32[32768]{0:T(1024)} %param.19) | copy-start | bytes 393220
  1.6 28.1 %copy-start.13 = (s32[256]{0:T(256)}, s32[256]{0:T(256)S(1)}, u32[]{:S(2)}) copy-start(s32[256]{0:T(256)S(1)} %multiply_add_fusion) | copy-start | bytes 3076
  25.4 10.6 %copy-start.15 = (s32[128]{0:T(128)S(1)}, s32[128]{0:T(128)}, u32[]{:S(2)}) copy-start(s32[128]{0:T(128)} %param.26) | copy-start | bytes 1540
  29.7 59.4 %all-to-all-start.1 = ((bf16[64,8,1024]{2,1,0:T(8,128)(2,1)}), bf16[64,8,1024]{2,1,0:T(8,128)(2,1)S(1)}, u32[]{:S(2)}, u32[]{:S(2)}) async-start(bf16[64,8,1024]{2,1,0:T(8,128)(2,1)} %fusion.2), calls=%async_computation.1 | async-start | bytes 2097152 | tf_op jit(solution)/shard_map/all_to_all | solution.py:332
  34.5 24.5 %collective-permute-start = (bf16[1,1,16,384]{3,2,1,0:T(8,128)(2,1)S(1)}, bf16[1,1,16,384]{3,2,1,0:T(8,128)(2,1)S(1)}, u32[]{:S(2)}, u32[]{:S(2)}) collective-permute-start(bf16[1,1,16,384]{3,2,1,0:T(8,128)(2,1)S(1)} %get-tuple-element.52), channel_id=1, source_target_pairs={{0,8},{8,0},{16,24},{24,16},{32,40},{40,32},{48,56},{56,48},{1,9},... | collective-permute-start | bytes 36872 | tf_op jit(solution)/shard_map/ppermute | solution.py:229
  39.0 45.0 %copy-start.10 = (bf16[1024,1280]{1,0:T(8,128)(2,1)S(1)}, bf16[1024,1280]{1,0:T(8,128)(2,1)}, u32[]{:S(2)}) copy-start(bf16[1024,1280]{1,0:T(8,128)(2,1)} %param.17) | copy-start | bytes 7864324
  58.9 4.4 %collective-permute-start.1 = (bf16[2,1,16,384]{3,2,1,0:T(8,128)(2,1)S(1)}, bf16[2,1,16,384]{3,2,1,0:T(8,128)(2,1)S(1)}, u32[]{:S(2)}, u32[]{:S(2)}) collective-permute-start(bf16[2,1,16,384]{3,2,1,0:T(8,128)(2,1)S(1)} %maximum_select_fusion.6), channel_id=1, source_target_pairs={{0,16},{8,24},{16,0},{24,8},{32,48},{40,56},{48,32},{56,40},{1,17}... | collective-permute-start | bytes 73736 | tf_op jit(solution)/shard_map/ppermute | solution.py:229
  63.4 6.9 %collective-permute-start.2 = (bf16[4,1,16,384]{3,2,1,0:T(8,128)(2,1)S(1)}, bf16[4,1,16,384]{3,2,1,0:T(8,128)(2,1)S(1)}, u32[]{:S(2)}, u32[]{:S(2)}) collective-permute-start(bf16[4,1,16,384]{3,2,1,0:T(8,128)(2,1)S(1)} %fusion.52), channel_id=1, source_target_pairs={{0,32},{8,40},{16,48},{24,56},{32,0},{40,8},{48,16},{56,24},{1,33}... | collective-permute-start | bytes 147464 | tf_op jit(solution)/shard_map/ppermute | solution.py:229
  70.3 4.0 %collective-permute-start.3 = (bf16[8,1,16,384]{3,2,1,0:T(8,128)(2,1)S(1)}, bf16[8,1,16,384]{3,2,1,0:T(8,128)(2,1)S(1)}, u32[]{:S(2)}, u32[]{:S(2)}) collective-permute-start(bf16[8,1,16,384]{3,2,1,0:T(8,128)(2,1)S(1)} %maximum_select_fusion.3), channel_id=1, source_target_pairs={{0,2},{2,0},{4,6},{6,4},{1,3},{3,1},{5,7},{7,5},{8,10},{10,8},{12,... | collective-permute-start | bytes 294920 | tf_op jit(solution)/shard_map/ppermute | solution.py:243
  71.7 4.7 %collective-permute-start.5 = (bf16[8,1,16,384]{3,2,1,0:T(8,128)(2,1)S(1)}, bf16[8,1,16,384]{3,2,1,0:T(8,128)(2,1)S(1)}, u32[]{:S(2)}, u32[]{:S(2)}) collective-permute-start(bf16[8,1,16,384]{3,2,1,0:T(8,128)(2,1)S(1)} %maximum_select_fusion.3), channel_id=1, source_target_pairs={{0,6},{2,4},{4,2},{6,0},{1,7},{3,5},{5,3},{7,1},{8,14},{10,12},{12... | collective-permute-start | bytes 294920 | tf_op jit(solution)/shard_map/ppermute | solution.py:243
  73.6 5.0 %collective-permute-start.4 = (bf16[8,1,16,384]{3,2,1,0:T(8,128)(2,1)S(1)}, bf16[8,1,16,384]{3,2,1,0:T(8,128)(2,1)S(1)}, u32[]{:S(2)}, u32[]{:S(2)}) collective-permute-start(bf16[8,1,16,384]{3,2,1,0:T(8,128)(2,1)S(1)} %maximum_select_fusion.3), channel_id=1, source_target_pairs={{0,4},{2,6},{4,0},{6,2},{1,5},{3,7},{5,1},{7,3},{8,12},{10,14},{12... | collective-permute-start | bytes 294920 | tf_op jit(solution)/shard_map/ppermute | solution.py:243
  78.7 9.6 %collective-permute-start.6 = (bf16[512,384]{1,0:T(8,128)(2,1)S(1)}, bf16[512,384]{1,0:T(8,128)(2,1)S(1)}, u32[]{:S(2)}, u32[]{:S(2)}) collective-permute-start(bf16[512,384]{1,0:T(8,128)(2,1)S(1)} %bitcast.91), channel_id=1, source_target_pairs={{0,1},{1,0},{2,3},{3,2},{4,5},{5,4},{6,7},{7,6},{8,9},{9,8},{10,11... | collective-permute-start | bytes 1179656 | tf_op jit(solution)/shard_map/ppermute | solution.py:28
  94.2 8.3 %collective-permute-start.7 = (bf16[192,384]{1,0:T(8,128)(2,1)S(1)}, bf16[192,384]{1,0:T(8,128)(2,1)S(1)}, u32[]{:S(2)}, u32[]{:S(2)}) collective-permute-start(bf16[192,384]{1,0:T(8,128)(2,1)S(1)} %get-tuple-element.20), channel_id=1, source_target_pairs={{0,64},{64,0},{128,192},{192,128},{1,65},{65,1},{129,193},{193,129... | collective-permute-start | bytes 442376 | tf_op jit(solution)/shard_map/ppermute | solution.py:36
  95.6 11.6 %copy-start.16 = (f32[384,128]{1,0:T(8,128)S(1)}, f32[384,128]{1,0:T(8,128)}, u32[]{:S(2)}) copy-start(f32[384,128]{1,0:T(8,128)} %param.33) | copy-start | bytes 589828
  98.3 18.4 %collective-permute-start.12 = (f32[512,384]{1,0:T(8,128)}, f32[512,384]{1,0:T(8,128)}, u32[]{:S(2)}, u32[]{:S(2)}) collective-permute-start(f32[512,384]{1,0:T(8,128)} %bitcast.27), channel_id=1, source_target_pairs={{0,1},{1,0},{2,3},{3,2},{4,5},{5,4},{6,7},{7,6},{8,9},{9,8},{10,11... | collective-permute-start | bytes 2359304 | tf_op jit(solution)/shard_map/ppermute | solution.py:28
  100.5 6.5 %collective-permute-start.9 = (bf16[192,384]{1,0:T(8,128)(2,1)S(1)}, bf16[192,384]{1,0:T(8,128)(2,1)S(1)}, u32[]{:S(2)}, u32[]{:S(2)}) collective-permute-start(bf16[192,384]{1,0:T(8,128)(2,1)S(1)} %get-tuple-element.21), channel_id=1, source_target_pairs={{0,192},{64,128},{128,64},{192,0},{1,193},{65,129},{129,65},{193,1... | collective-permute-start | bytes 442376 | tf_op jit(solution)/shard_map/ppermute | solution.py:36
  102.6 7.6 %collective-permute-start.8 = (bf16[192,384]{1,0:T(8,128)(2,1)S(1)}, bf16[192,384]{1,0:T(8,128)(2,1)S(1)}, u32[]{:S(2)}, u32[]{:S(2)}) collective-permute-start(bf16[192,384]{1,0:T(8,128)(2,1)S(1)} %add_convert_fusion.3.refs_0_), channel_id=1, source_target_pairs={{0,192},{64,128},{128,64},{192,0},{1,193},{65,129},{129,65},{193,1... | collective-permute-start | bytes 442376 | tf_op jit(solution)/shard_map/ppermute | solution.py:36
  107.1 4.1 %collective-permute-start.10 = (bf16[192,384]{1,0:T(8,128)(2,1)S(1)}, bf16[192,384]{1,0:T(8,128)(2,1)S(1)}, u32[]{:S(2)}, u32[]{:S(2)}) collective-permute-start(bf16[192,384]{1,0:T(8,128)(2,1)S(1)} %add_convert_fusion.2.refs_2_), channel_id=1, source_target_pairs={{0,64},{64,0},{128,192},{192,128},{1,65},{65,1},{129,193},{193,129... | collective-permute-start | bytes 442376 | tf_op jit(solution)/shard_map/ppermute | solution.py:36
  113.2 49.6 %copy-start.7 = (f32[384,128]{1,0:T(8,128)}, f32[384,128]{1,0:T(8,128)S(1)}, u32[]{:S(2)}) copy-start(f32[384,128]{1,0:T(8,128)S(1)} %get-tuple-element.27.refs_12_) | copy-start | bytes 589828
  113.6 4.9 %collective-permute-start.11 = (f32[512,384]{1,0:T(8,128)S(1)}, f32[512,384]{1,0:T(8,128)S(1)}, u32[]{:S(2)}, u32[]{:S(2)}) collective-permute-start(f32[512,384]{1,0:T(8,128)S(1)} %fusion.91), channel_id=1, source_target_pairs={{0,1},{1,0},{2,3},{3,2},{4,5},{5,4},{6,7},{7,6},{8,9},{9,8},{10,11... | collective-permute-start | bytes 2359304 | tf_op jit(solution)/shard_map/ppermute | solution.py:28
  116.6 1.9 collective-permute-start.13
  119.0 43.8 %copy-start.17 = (f32[128]{0:T(128)S(1)}, f32[128]{0:T(128)}, u32[]{:S(2)}) copy-start(f32[128]{0:T(128)} %param.29) | copy-start | bytes 1540
  119.0 43.8 %copy-start.11 = (f32[384,128]{1,0:T(8,128)S(1)}, f32[384,128]{1,0:T(8,128)}, u32[]{:S(2)}) copy-start(f32[384,128]{1,0:T(8,128)} %refs_14_.1) | copy-start | bytes 589828
  119.9 21.6 %all-to-all-start.2 = ((bf16[32,56,128]{2,1,0:T(8,128)(2,1)}), bf16[32,56,128]{2,1,0:T(8,128)(2,1)S(1)}, u32[]{:S(2)}, u32[]{:S(2)}) async-start(bf16[32,56,128]{2,1,0:T(8,128)(2,1)} %pad_maximum_fusion), calls=%async_computation.2 | async-start | bytes 917504 | tf_op jit(solution)/shard_map/all_to_all | solution.py:409
  159.3 4.8 %collective-permute-start.14 = (bf16[512,384]{1,0:T(8,128)(2,1)S(1)}, bf16[512,384]{1,0:T(8,128)(2,1)S(1)}, u32[]{:S(2)}, u32[]{:S(2)}) collective-permute-start(bf16[512,384]{1,0:T(8,128)(2,1)S(1)} %bitcast.93), channel_id=1, source_target_pairs={{0,1},{1,0},{2,3},{3,2},{4,5},{5,4},{6,7},{7,6},{8,9},{9,8},{10,11... | collective-permute-start | bytes 1179656 | tf_op jit(solution)/shard_map/ppermute | solution.py:28
  164.8 5.1 %collective-permute-start.15 = (bf16[192,384]{1,0:T(8,128)(2,1)S(1)}, bf16[192,384]{1,0:T(8,128)(2,1)S(1)}, u32[]{:S(2)}, u32[]{:S(2)}) collective-permute-start(bf16[192,384]{1,0:T(8,128)(2,1)S(1)} %get-tuple-element.25), channel_id=1, source_target_pairs={{0,64},{64,0},{128,192},{192,128},{1,65},{65,1},{129,193},{193,129... | collective-permute-start | bytes 442376 | tf_op jit(solution)/shard_map/ppermute | solution.py:36
  165.6 6.3 %collective-permute-start.17 = (bf16[192,384]{1,0:T(8,128)(2,1)S(1)}, bf16[192,384]{1,0:T(8,128)(2,1)S(1)}, u32[]{:S(2)}, u32[]{:S(2)}) collective-permute-start(bf16[192,384]{1,0:T(8,128)(2,1)S(1)} %get-tuple-element.26), channel_id=1, source_target_pairs={{0,192},{64,128},{128,64},{192,0},{1,193},{65,129},{129,65},{193,1... | collective-permute-start | bytes 442376 | tf_op jit(solution)/shard_map/ppermute | solution.py:36
  169.9 5.3 %collective-permute-start.16 = (bf16[192,384]{1,0:T(8,128)(2,1)S(1)}, bf16[192,384]{1,0:T(8,128)(2,1)S(1)}, u32[]{:S(2)}, u32[]{:S(2)}) collective-permute-start(bf16[192,384]{1,0:T(8,128)(2,1)S(1)} %add_convert_fusion.1.refs_0_), channel_id=1, source_target_pairs={{0,192},{64,128},{128,64},{192,0},{1,193},{65,129},{129,65},{193,1... | collective-permute-start | bytes 442376 | tf_op jit(solution)/shard_map/ppermute | solution.py:36
  172.0 4.6 %collective-permute-start.18 = (bf16[192,384]{1,0:T(8,128)(2,1)S(1)}, bf16[192,384]{1,0:T(8,128)(2,1)S(1)}, u32[]{:S(2)}, u32[]{:S(2)}) collective-permute-start(bf16[192,384]{1,0:T(8,128)(2,1)S(1)} %add_convert_fusion.refs_2_), channel_id=1, source_target_pairs={{0,64},{64,0},{128,192},{192,128},{1,65},{65,1},{129,193},{193,129... | collective-permute-start | bytes 442376 | tf_op jit(solution)/shard_map/ppermute | solution.py:36
  179.2 4.4 %collective-permute-start.19 = (f32[512,384]{1,0:T(8,128)S(1)}, f32[512,384]{1,0:T(8,128)S(1)}, u32[]{:S(2)}, u32[]{:S(2)}) collective-permute-start(f32[512,384]{1,0:T(8,128)S(1)} %fusion.92), channel_id=1, source_target_pairs={{0,1},{1,0},{2,3},{3,2},{4,5},{5,4},{6,7},{7,6},{8,9},{9,8},{10,11... | collective-permute-start | bytes 2359304 | tf_op jit(solution)/shard_map/ppermute | solution.py:28
  181.7 1.9 collective-permute-start.20
  186.2 19.5 %all-to-all-start.4 = ((bf16[32,56,128]{2,1,0:T(8,128)(2,1)}), bf16[32,56,128]{2,1,0:T(8,128)(2,1)S(1)}, u32[]{:S(2)}, u32[]{:S(2)}) async-start(bf16[32,56,128]{2,1,0:T(8,128)(2,1)} %pad_maximum_fusion.1), calls=%async_computation.4 | async-start | bytes 917504 | tf_op jit(solution)/shard_map/all_to_all | solution.py:409
  (12 other events, 53.6 us)

commit v5 on v4

--- a/solution.py
+++ b/solution.py
@@ -16,6 +16,7 @@
 KAPPA = 1.0
 THETA = 0.5
 
+VMEM_LIMIT = 16 * 1024 * 1024
 AREAS = ("z", "x", "core")
 CHIPS = ("z", "x")
 
@@ -97,6 +98,10 @@
     return tuple(pltpu.with_memory_space_constraint(x, pltpu.VMEM) for x in arrays)
 
 
+def in_main(*arrays):
+    return tuple(pltpu.with_memory_space_constraint(x, pltpu.HBM) for x in arrays)
+
+
 def half_prices(row_count, units):
     half = pltpu.VMEM((row_count // 2, units), jnp.bfloat16)
     return (half, half)
@@ -116,6 +121,7 @@
         out_specs=(in_vmem,) * 4,
         scratch_shapes=[pltpu.VMEM((Z * X * CORES, share_len, gen_count), jnp.bfloat16)],
         name="weights",
+        compiler_params=pltpu.CompilerParams(vmem_limit_bytes=VMEM_LIMIT),
     )(
         core.reshape(1),
         *in_fast(columns),
@@ -133,6 +139,7 @@
         in_specs=[in_vmem] * 4,
         out_specs=(in_vmem,) * 2,
         name="prices",
+        compiler_params=pltpu.CompilerParams(vmem_limit_bytes=VMEM_LIMIT),
     )(*in_fast(dual_own, dual_other, weight_own, weight_other))
 
 
@@ -192,12 +199,14 @@
     stor_count = stor_now.shape[1]
     operands = (
         *in_fast(*pairs, level[:, None]),
-        *(value[None, :] for value in gen_params),
-        *(value[None, :] for value in stor_params),
-        *in_fast(back),
-        gen_now,
-        stor_now,
-        *old,
+        *in_main(
+            *(value[None, :] for value in gen_params),
+            *(value[None, :] for value in stor_params),
+            back,
+            gen_now,
+            stor_now,
+            *old,
+        ),
     )
     in_vmem = pl.BlockSpec(memory_space=pltpu.VMEM)
     return pl.pallas_call(
@@ -211,6 +220,7 @@
         in_specs=[in_vmem] * len(operands),
         out_specs=(in_vmem,) * 4,
         name="update",
+        compiler_params=pltpu.CompilerParams(vmem_limit_bytes=VMEM_LIMIT),
     )(*operands)
 
 
@@ -235,9 +245,10 @@
 
 def gathered_early(share):
     share_len, row_count = share.shape
-    held = share.astype(jnp.bfloat16).reshape(1, 1, share_len, row_count)
-    for step in (1, 2, 4):
-        held = doubled(held, "z", Z, step, 0)
+    held = share.astype(jnp.bfloat16).reshape(1, 1, 1, share_len, row_count)
+    for dim, step in enumerate((4, 2, 1)):
+        held = doubled(held, "z", Z, step, dim)
+    held = held.reshape(Z, 1, share_len, row_count)
     near = [held]
     for step in (1, 2, 3):
         near.append(lax.ppermute(held, "x", [(i, i ^ step) for i in range(X)]))
@@ -355,6 +366,7 @@
     load_flow = load_own + swapped(load_other)
     load_total = jnp.sum(load, axis=1)
 
+    weight_far = swapped(weight_other)
     limit = jnp.take(ratings, lax.dynamic_slice_in_dim(line_index, area * share_len, share_len))[:, None]
     hour_of = jnp.arange(row_count, dtype=jnp.int32) % HOURS
     last_hour = (hour_of == HOURS - 1)[:, None]
@@ -381,13 +393,13 @@
         )
         balance = total[0] - load_total
         stor_bar = 2.0 * stor_next - stor_now
-        flow_other = lax.dot_general(
-            weight_other, bar_low, CONTRACT_MINOR, preferred_element_type=jnp.float32
-        )
-        flow_own = lax.dot_general(
-            weight_own, bar_low, CONTRACT_MINOR, preferred_element_type=jnp.float32
-        )
-        flow_part = flow_own + swapped(flow_other) - load_flow
+        flow_part = (
+            lax.dot_general(weight_own, bar_low, CONTRACT_MINOR, preferred_element_type=jnp.float32)
+            + lax.dot_general(
+                weight_far, swapped(bar_low), CONTRACT_MINOR, preferred_element_type=jnp.float32
+            )
+            - load_flow
+        )
         balance = balance + swapped(balance)
         high = rounded(balance)
         lanes = 128

time: 208 us -> 211 us (1.014)
  other arithmetic: 10.2 us -> 15.4 us
  waiting for transfers between devices: 72.2 us -> 67.3 us
  starting transfers between devices: 48.3 us -> 51.2 us
    dot_general x4, matrix products: 3.51 us -> 7.86 us  [summed_hours(): jnp.dot(hour_sums(values.shape[0], later), values, precision=lax.Precisio...]
    ppermute x8, waiting for transfers between devices: 13.3 us -> 10.3 us  [from_side(): return lax.ppermute(x, 'lines', [(i, i ^ step) for i in range(4)])]
    unnamed x42 -> x56, local copies, waits for them, and re-layouts: 5.18 us -> 4.2 us
    ppermute x7 -> x8, starting transfers between devices: 14.7 us -> 14.5 us  [swapped(): return lax.ppermute(x, 'core', [(0, 1), (1, 0)])]
  transfers between devices with their start and end apart: 24 -> 25, of which waited for: 16 -> 17; matrix products, arithmetic and copies ran while one was open for 11% -> 12% of each run, Pallas kernels for 1% -> 1%
where the time goes in v5:
time: 211 us; the launch traced here: 210 us
  waiting for transfers between devices  67.3 us (32%)
  starting transfers between devices  51.2 us (24%)
  blocking collectives  40.4 us (19%)
  matrix products  17.3 us (8%)
  other arithmetic  15.4 us (7%)
  local copies, waits for them, and re-layouts  8.72 us (4%)
  Pallas kernels  8.63 us (4%)
    ppermute x3, waiting for transfers between devices, doubled(): other = lax.ppermute(x, axis, [(i, i ^ step) for i in range(size)])  25.1 us
    all_to_all x2, waiting for transfers between devices, shards(): received = lax.all_to_all(sent, CHIPS, 0, 0, tiled=True)  24.6 us
    all_to_all x1, blocking collectives, shards(): lax.all_to_all(slot_bus.reshape(area_count, slots), AREAS, 0, 0, tiled=True)  22.2 us
    all_to_all x1, blocking collectives, sent_to_chips(): return lax.all_to_all(sent, CHIPS, 0, 0, tiled=True)  18.2 us
    ppermute x8, starting transfers between devices, swapped(): return lax.ppermute(x, 'core', [(0, 1), (1, 0)])  14.5 us
    ppermute x8, waiting for transfers between devices, from_side(): return lax.ppermute(x, 'lines', [(i, i ^ step) for i in range(4)])  10.3 us
    ppermute x8, starting transfers between devices, from_side(): return lax.ppermute(x, 'lines', [(i, i ^ step) for i in range(4)])  9.89 us
    all_to_all x2, starting transfers between devices, shards(): received = lax.all_to_all(sent, CHIPS, 0, 0, tiled=True)  9.2 us
  transfers between devices with their start and end apart: 25, of which 17 were waited for; matrix products, arithmetic and copies ran while one was open for 12% of the time, Pallas kernels for 1%

profile of v5, /device:TPU:1, one launch (start us, length us, event | category | flops | bytes accessed | tf_op | source)
XLA Modules:
  0.0 210.1 jit_solution(7279083975594296598)
XLA Ops:
  1.9 22.2 %all_to_all.32 = s32[64,1,8]{2,1,0:T(1,128)S(1)} all-to-all(s32[64,1,8]{2,1,0:T(1,128)S(1)} %bitcast.101), channel_id=1, replica_groups=mesh['lines'=4,'z'=8,'x'=4,'core'=2] {'z','x','core'}, dimensions={0} | all-to-all | bytes 4096 | tf_op jit(solution)/shard_map/all_to_all | solution.py:332
  25.5 2.6 %fusion.2 = bf16[64,8,1024]{2,1,0:T(8,128)(2,1)} fusion(bf16[1024,1280]{1,0:T(8,128)(2,1)S(1)} %copy-done, s32[512]{0:T(512)S(1)} %eq.148), kind=kOutput, calls=%fused_computation.4 | convolution fusion | flops 1343356928 | bytes 3672064 | tf_op jit(solution)/shard_map/dot_general | solution.py:340
  28.0 5.6 %all-to-all-start.1 = ((bf16[64,8,1024]{2,1,0:T(8,128)(2,1)}), bf16[64,8,1024]{2,1,0:T(8,128)(2,1)}, u32[]{:S(2)}, u32[]{:S(2)}) async-start(bf16[64,8,1024]{2,1,0:T(8,128)(2,1)} %fusion.2), calls=%async_computation.1 | async-start | bytes 2097152 | tf_op jit(solution)/shard_map/all_to_all | solution.py:343
  33.6 5.6 %collective-permute-start = (bf16[1,1,1,16,384]{4,3,2,1,0:T(8,128)(2,1)S(1)}, bf16[1,1,1,16,384]{4,3,2,1,0:T(8,128)(2,1)S(1)}, u32[]{:S(2)}, u32[]{:S(2)}) collective-permute-start(bf16[1,1,1,16,384]{4,3,2,1,0:T(8,128)(2,1)S(1)} %get-tuple-element.52), channel_id=1, source_target_pairs={{0,32},{8,40},{16,48},{24,56},{32,0},{40,8},{48,16},{56,24},{1,33}... | collective-permute-start | bytes 36872 | tf_op jit(solution)/shard_map/ppermute | solution.py:239
  39.2 21.9 %collective-permute-done = bf16[1,1,1,16,384]{4,3,2,1,0:T(8,128)(2,1)S(1)} collective-permute-done((bf16[1,1,1,16,384]{4,3,2,1,0:T(8,128)(2,1)S(1)}, bf16[1,1,1,16,384]{4,3,2,1,0:T(8,128)(2,1)S(1)}, u32[]{:S(2)}, u32[]{:S(2)}) %collective-permute-start) | collective-permute-done | bytes 12320 | tf_op jit(solution)/shard_map/ppermute | solution.py:239
  61.7 3.0 %collective-permute-done.1 = bf16[2,1,1,16,384]{4,3,2,1,0:T(8,128)(2,1)S(1)} collective-permute-done((bf16[2,1,1,16,384]{4,3,2,1,0:T(8,128)(2,1)S(1)}, bf16[2,1,1,16,384]{4,3,2,1,0:T(8,128)(2,1)S(1)}, u32[]{:S(2)}, u32[]{:S(2)}) %collective-permute-start.1) | collective-permute-done | bytes 24608 | tf_op jit(solution)/shard_map/ppermute | solution.py:239
  64.7 2.2 %collective-permute-start.2 = (bf16[2,2,1,16,384]{4,3,2,1,0:T(8,128)(2,1)S(1)}, bf16[2,2,1,16,384]{4,3,2,1,0:T(8,128)(2,1)S(1)}, u32[]{:S(2)}, u32[]{:S(2)}) collective-permute-start(bf16[2,2,1,16,384]{4,3,2,1,0:T(8,128)(2,1)S(1)} %maximum_select_fusion.4), channel_id=1, source_target_pairs={{0,8},{8,0},{16,24},{24,16},{32,40},{40,32},{48,56},{56,48},{1,9},... | collective-permute-start | bytes 147464 | tf_op jit(solution)/shard_map/ppermute | solution.py:239
  70.1 2.1 %collective-permute-start.5 = (bf16[8,1,16,384]{3,2,1,0:T(8,128)(2,1)S(1)}, bf16[8,1,16,384]{3,2,1,0:T(8,128)(2,1)S(1)}, u32[]{:S(2)}, u32[]{:S(2)}) collective-permute-start(bf16[8,1,16,384]{3,2,1,0:T(8,128)(2,1)S(1)} %bitcast.98), channel_id=1, source_target_pairs={{0,6},{2,4},{4,2},{6,0},{1,7},{3,5},{5,3},{7,1},{8,14},{10,12},{12... | collective-permute-start | bytes 294920 | tf_op jit(solution)/shard_map/ppermute | solution.py:254
  72.8 1.9 collective-permute-done.5
  74.7 2.4 %collective-permute-done.4 = bf16[8,1,16,384]{3,2,1,0:T(8,128)(2,1)S(1)} collective-permute-done((bf16[8,1,16,384]{3,2,1,0:T(8,128)(2,1)S(1)}, bf16[8,1,16,384]{3,2,1,0:T(8,128)(2,1)S(1)}, u32[]{:S(2)}, u32[]{:S(2)}) %collective-permute-start.4) | collective-permute-done | bytes 98336 | tf_op jit(solution)/shard_map/ppermute | solution.py:254
  77.3 6.0 %collective-permute-start.6 = (bf16[512,384]{1,0:T(8,128)(2,1)S(1)}, bf16[512,384]{1,0:T(8,128)(2,1)S(1)}, u32[]{:S(2)}, u32[]{:S(2)}) collective-permute-start(bf16[512,384]{1,0:T(8,128)(2,1)S(1)} %bitcast.86), channel_id=1, source_target_pairs={{0,1},{1,0},{2,3},{3,2},{4,5},{5,4},{6,7},{7,6},{8,9},{9,8},{10,11... | collective-permute-start | bytes 1179656 | tf_op jit(solution)/shard_map/ppermute | solution.py:29
  83.3 4.3 %fusion.11 = f32[1024,384]{1,0:T(8,128)} fusion(bf16[1024,1280]{1,0:T(8,128)(2,1)S(1)} %copy-done, f32[384,1280]{1,0:T(8,128)} %param.18), kind=kOutput, calls=%fused_computation.18 | convolution fusion | flops 1007124480 | bytes 6160384 | tf_op jit(solution)/shard_map/dot_general | solution.py:362
  90.2 3.6 %weights.1 = (bf16[512,384]{1,0:T(8,128)(2,1)S(1)}, bf16[512,384]{1,0:T(8,128)(2,1)S(1)}, bf16[192,384]{1,0:T(8,128)(2,1)}, bf16[192,384]{1,0:T(8,128)(2,1)S(1)}) custom-call(s32[1]{0:T(128)} %bitcast.1.core, bf16[512,1024]{1,0:T(8,128)(2,1)} %bitcast.4.columns, s32[1,256]{1,0:T(1,128)S(1)} %bitcast.92, bf16[512,128]{1,0:T(8,128)(2,1)S(1)} %bitcast.91, ...), custom_call_target="tpu_custom_call" | custom-call | tf_op jit(solution)/shard_map/weights/pallas_call | solution.py:117
  98.6 2.0 collective-permute-start.9
  103.2 2.1 %collective-permute-done.9 = bf16[192,384]{1,0:T(8,128)(2,1)S(1)} collective-permute-done((bf16[192,384]{1,0:T(8,128)(2,1)}, bf16[192,384]{1,0:T(8,128)(2,1)S(1)}, u32[]{:S(2)}, u32[]{:S(2)}) %collective-permute-start.9) | collective-permute-done | bytes 147488 | tf_op jit(solution)/shard_map/ppermute | solution.py:37
  106.4 2.3 %fusion.17.refs_10_ = f32[384,128]{1,0:T(8,128)} fusion(f32[384,128]{1,0:T(8,128)} %param.33, s32[384]{0:T(512)S(1)} %add_select_fusion), kind=kOutput, calls=%fused_computation.27 | convolution fusion | flops 227082240 | bytes 394752 | tf_op jit(solution)/shard_map/dot_general | solution.py:281
  110.3 2.1 %update.2 = (bf16[384,384]{1,0:T(8,128)(2,1)S(1)}, f32[384,256]{1,0:T(8,128)S(1)}, f32[384,128]{1,0:T(8,128)S(1)}, f32[8,384]{1,0:T(8,128)S(1)}) custom-call(bf16[192,384]{1,0:T(8,128)(2,1)S(1)} %add_convert_fusion.3.refs_0_, bf16[192,384]{1,0:T(8,128)(2,1)S(1)} %collective-permute-done.8.refs_1_, bf16[192,384]{1,0:T(8,128)(2,1)S(1)} %add_convert_fusion.2.refs_2_, ...), custom_call_target="tpu_custom_call" | custom-call | tf_op jit(solution)/shard_map/update/pallas_call | solution.py:212
  112.5 2.7 %collective-permute-start.14 = (f32[384]{0:T(512)S(1)}, f32[384]{0:T(512)S(1)}, u32[]{:S(2)}, u32[]{:S(2)}) collective-permute-start(f32[384]{0:T(512)S(1)} %sub.100), channel_id=1, source_target_pairs={{0,1},{1,0},{2,3},{3,2},{4,5},{5,4},{6,7},{7,6},{8,9},{9,8},{10,11... | collective-permute-start | bytes 4616 | tf_op jit(solution)/shard_map/ppermute | solution.py:29
  120.5 4.6 %all-to-all-start.2 = ((bf16[32,56,128]{2,1,0:T(8,128)(2,1)}), bf16[32,56,128]{2,1,0:T(8,128)(2,1)}, u32[]{:S(2)}, u32[]{:S(2)}) async-start(bf16[32,56,128]{2,1,0:T(8,128)(2,1)} %pad_maximum_fusion), calls=%async_computation.2 | async-start | bytes 917504 | tf_op jit(solution)/shard_map/all_to_all | solution.py:421
  127.9 12.8 %all-to-all-done.2 = bf16[32,56,128]{2,1,0:T(8,128)(2,1)} async-done(((bf16[32,56,128]{2,1,0:T(8,128)(2,1)}), bf16[32,56,128]{2,1,0:T(8,128)(2,1)}, u32[]{:S(2)}, u32[]{:S(2)}) %all-to-all-start.2) | async-done | bytes 458784 | tf_op jit(solution)/shard_map/all_to_all | solution.py:421
  142.6 18.2 %all_to_all.33 = bf16[32,16,384]{2,1,0:T(8,128)(2,1)S(1)} all-to-all(bf16[32,16,384]{2,1,0:T(8,128)(2,1)S(1)} %broadcast_in_dim.155), channel_id=1, replica_groups=mesh['lines'=4,'z'=8,'x'=4,'core'=2] {'z','x'}, dimensions={0} | all-to-all | bytes 786432 | tf_op jit(solution)/shard_map/all_to_all | solution.py:230
  160.8 3.0 %collective-permute-start.15 = (bf16[512,384]{1,0:T(8,128)(2,1)S(1)}, bf16[512,384]{1,0:T(8,128)(2,1)S(1)}, u32[]{:S(2)}, u32[]{:S(2)}) collective-permute-start(bf16[512,384]{1,0:T(8,128)(2,1)S(1)} %bitcast.88), channel_id=1, source_target_pairs={{0,1},{1,0},{2,3},{3,2},{4,5},{5,4},{6,7},{7,6},{8,9},{9,8},{10,11... | collective-permute-start | bytes 1179656 | tf_op jit(solution)/shard_map/ppermute | solution.py:29
  164.5 1.8 fusion.38
  168.5 2.2 %collective-permute-start.18 = (bf16[192,384]{1,0:T(8,128)(2,1)S(1)}, bf16[192,384]{1,0:T(8,128)(2,1)S(1)}, u32[]{:S(2)}, u32[]{:S(2)}) collective-permute-start(bf16[192,384]{1,0:T(8,128)(2,1)S(1)} %get-tuple-element.26), channel_id=1, source_target_pairs={{0,192},{64,128},{128,64},{192,0},{1,193},{65,129},{129,65},{193,1... | collective-permute-start | bytes 442376 | tf_op jit(solution)/shard_map/ppermute | solution.py:37
  170.7 1.8 collective-permute-done.16
  172.5 2.2 %collective-permute-start.17 = (bf16[192,384]{1,0:T(8,128)(2,1)S(1)}, bf16[192,384]{1,0:T(8,128)(2,1)S(1)}, u32[]{:S(2)}, u32[]{:S(2)}) collective-permute-start(bf16[192,384]{1,0:T(8,128)(2,1)S(1)} %add_convert_fusion.1.refs_0_), channel_id=1, source_target_pairs={{0,192},{64,128},{128,64},{192,0},{1,193},{65,129},{129,65},{193,1... | collective-permute-start | bytes 442376 | tf_op jit(solution)/shard_map/ppermute | solution.py:37
  175.7 2.7 %collective-permute-done.17.refs_1_ = bf16[192,384]{1,0:T(8,128)(2,1)S(1)} collective-permute-done((bf16[192,384]{1,0:T(8,128)(2,1)S(1)}, bf16[192,384]{1,0:T(8,128)(2,1)S(1)}, u32[]{:S(2)}, u32[]{:S(2)}) %collective-permute-start.17) | collective-permute-done | bytes 147488 | tf_op jit(solution)/shard_map/ppermute | solution.py:37
  180.0 2.4 %update.3 = (bf16[384,384]{1,0:T(8,128)(2,1)S(1)}, f32[384,256]{1,0:T(8,128)S(1)}, f32[384,128]{1,0:T(8,128)S(1)}, f32[8,384]{1,0:T(8,128)S(1)}) custom-call(bf16[192,384]{1,0:T(8,128)(2,1)S(1)} %add_convert_fusion.1.refs_0_, bf16[192,384]{1,0:T(8,128)(2,1)S(1)} %collective-permute-done.17.refs_1_, bf16[192,384]{1,0:T(8,128)(2,1)S(1)} %add_convert_fusion.refs_2_, ...), custom_call_target="tpu_custom_call" | custom-call | tf_op jit(solution)/shard_map/update/pallas_call | solution.py:212
  182.4 1.8 collective-permute-start.21
  187.6 4.6 %all-to-all-start.4 = ((bf16[32,56,128]{2,1,0:T(8,128)(2,1)}), bf16[32,56,128]{2,1,0:T(8,128)(2,1)}, u32[]{:S(2)}, u32[]{:S(2)}) async-start(bf16[32,56,128]{2,1,0:T(8,128)(2,1)} %pad_maximum_fusion.1), calls=%async_computation.4 | async-start | bytes 917504 | tf_op jit(solution)/shard_map/all_to_all | solution.py:421
  193.6 2.3 %fusion.40 = f32[384,128]{1,0:T(8,128)} fusion(f32[384,128]{1,0:T(8,128)} %copy-done.26, s32[384]{0:T(512)S(1)} %copy-done.24, f32[384,128]{1,0:T(8,128)S(1)} %copy-done.11, f32[384,128]{1,0:T(8,128)S(1)} %get-tuple-element.62, f32[128]{0:T(128)S(1)} %get-tuple-element.60, f32[128]{0:T(128)S(1)} %get-tuple-element.59, pred[384]{0:T(512)(128)(4,1)S(1)} %fusion.62), kind=kOutput, calls=%fused_computation.70 | convolution fusion | flops 227622912 | bytes 789376 | tf_op jit(solution)/shard_map/dot_general | solution.py:281
  195.9 11.8 %all-to-all-done.4 = bf16[32,56,128]{2,1,0:T(8,128)(2,1)} async-done(((bf16[32,56,128]{2,1,0:T(8,128)(2,1)}), bf16[32,56,128]{2,1,0:T(8,128)(2,1)}, u32[]{:S(2)}, u32[]{:S(2)}) %all-to-all-start.4) | async-done | bytes 458784 | tf_op jit(solution)/shard_map/all_to_all | solution.py:421
  (151 shorter events, 42.2 us)
Async XLA Ops:
  0.6 24.8 %copy-start = (bf16[1024,1280]{1,0:T(8,128)(2,1)S(1)}, bf16[1024,1280]{1,0:T(8,128)(2,1)}, u32[]{:S(2)}) copy-start(bf16[1024,1280]{1,0:T(8,128)(2,1)} %param.17) | copy-start | bytes 7864324
  25.5 41.5 %copy-start.25 = (s32[128]{0:T(128)S(1)}, s32[128]{0:T(128)}, u32[]{:S(2)}) copy-start(s32[128]{0:T(128)} %param.26) | copy-start | bytes 1540
  28.0 60.3 %all-to-all-start.1 = ((bf16[64,8,1024]{2,1,0:T(8,128)(2,1)}), bf16[64,8,1024]{2,1,0:T(8,128)(2,1)}, u32[]{:S(2)}, u32[]{:S(2)}) async-start(bf16[64,8,1024]{2,1,0:T(8,128)(2,1)} %fusion.2), calls=%async_computation.1 | async-start | bytes 2097152 | tf_op jit(solution)/shard_map/all_to_all | solution.py:343
  33.6 27.4 %collective-permute-start = (bf16[1,1,1,16,384]{4,3,2,1,0:T(8,128)(2,1)S(1)}, bf16[1,1,1,16,384]{4,3,2,1,0:T(8,128)(2,1)S(1)}, u32[]{:S(2)}, u32[]{:S(2)}) collective-permute-start(bf16[1,1,1,16,384]{4,3,2,1,0:T(8,128)(2,1)S(1)} %get-tuple-element.52), channel_id=1, source_target_pairs={{0,32},{8,40},{16,48},{24,56},{32,0},{40,8},{48,16},{56,24},{1,33}... | collective-permute-start | bytes 36872 | tf_op jit(solution)/shard_map/ppermute | solution.py:239
  61.1 3.7 %collective-permute-start.1 = (bf16[2,1,1,16,384]{4,3,2,1,0:T(8,128)(2,1)S(1)}, bf16[2,1,1,16,384]{4,3,2,1,0:T(8,128)(2,1)S(1)}, u32[]{:S(2)}, u32[]{:S(2)}) collective-permute-start(bf16[2,1,1,16,384]{4,3,2,1,0:T(8,128)(2,1)S(1)} %maximum_select_fusion.6), channel_id=1, source_target_pairs={{0,16},{8,24},{16,0},{24,8},{32,48},{40,56},{48,32},{56,40},{1,17}... | collective-permute-start | bytes 73736 | tf_op jit(solution)/shard_map/ppermute | solution.py:239
  64.7 3.7 %collective-permute-start.2 = (bf16[2,2,1,16,384]{4,3,2,1,0:T(8,128)(2,1)S(1)}, bf16[2,2,1,16,384]{4,3,2,1,0:T(8,128)(2,1)S(1)}, u32[]{:S(2)}, u32[]{:S(2)}) collective-permute-start(bf16[2,2,1,16,384]{4,3,2,1,0:T(8,128)(2,1)S(1)} %maximum_select_fusion.4), channel_id=1, source_target_pairs={{0,8},{8,0},{16,24},{24,16},{32,40},{40,32},{48,56},{56,48},{1,9},... | collective-permute-start | bytes 147464 | tf_op jit(solution)/shard_map/ppermute | solution.py:239
  68.5 4.3 %collective-permute-start.3 = (bf16[8,1,16,384]{3,2,1,0:T(8,128)(2,1)S(1)}, bf16[8,1,16,384]{3,2,1,0:T(8,128)(2,1)S(1)}, u32[]{:S(2)}, u32[]{:S(2)}) collective-permute-start(bf16[8,1,16,384]{3,2,1,0:T(8,128)(2,1)S(1)} %bitcast.97), channel_id=1, source_target_pairs={{0,2},{2,0},{4,6},{6,4},{1,3},{3,1},{5,7},{7,5},{8,10},{10,8},{12,... | collective-permute-start | bytes 294920 | tf_op jit(solution)/shard_map/ppermute | solution.py:254
  70.1 4.7 %collective-permute-start.5 = (bf16[8,1,16,384]{3,2,1,0:T(8,128)(2,1)S(1)}, bf16[8,1,16,384]{3,2,1,0:T(8,128)(2,1)S(1)}, u32[]{:S(2)}, u32[]{:S(2)}) collective-permute-start(bf16[8,1,16,384]{3,2,1,0:T(8,128)(2,1)S(1)} %bitcast.98), channel_id=1, source_target_pairs={{0,6},{2,4},{4,2},{6,0},{1,7},{3,5},{5,3},{7,1},{8,14},{10,12},{12... | collective-permute-start | bytes 294920 | tf_op jit(solution)/shard_map/ppermute | solution.py:254
  72.2 5.0 %collective-permute-start.4 = (bf16[8,1,16,384]{3,2,1,0:T(8,128)(2,1)S(1)}, bf16[8,1,16,384]{3,2,1,0:T(8,128)(2,1)S(1)}, u32[]{:S(2)}, u32[]{:S(2)}) collective-permute-start(bf16[8,1,16,384]{3,2,1,0:T(8,128)(2,1)S(1)} %bitcast.99), channel_id=1, source_target_pairs={{0,4},{2,6},{4,0},{6,2},{1,5},{3,7},{5,1},{7,3},{8,12},{10,14},{12... | collective-permute-start | bytes 294920 | tf_op jit(solution)/shard_map/ppermute | solution.py:254
  77.3 10.3 %collective-permute-start.6 = (bf16[512,384]{1,0:T(8,128)(2,1)S(1)}, bf16[512,384]{1,0:T(8,128)(2,1)S(1)}, u32[]{:S(2)}, u32[]{:S(2)}) collective-permute-start(bf16[512,384]{1,0:T(8,128)(2,1)S(1)} %bitcast.86), channel_id=1, source_target_pairs={{0,1},{1,0},{2,3},{3,2},{4,5},{5,4},{6,7},{7,6},{8,9},{9,8},{10,11... | collective-permute-start | bytes 1179656 | tf_op jit(solution)/shard_map/ppermute | solution.py:29
  93.8 72.5 %copy-start.1 = (bf16[512,384]{1,0:T(8,128)(2,1)}, bf16[512,384]{1,0:T(8,128)(2,1)S(1)}, u32[]{:S(2)}) copy-start(bf16[512,384]{1,0:T(8,128)(2,1)S(1)} %get-tuple-element.19.weight_own) | copy-start | bytes 1179652
  93.8 6.8 %collective-permute-start.7 = (bf16[192,384]{1,0:T(8,128)(2,1)}, bf16[192,384]{1,0:T(8,128)(2,1)S(1)}, u32[]{:S(2)}, u32[]{:S(2)}) collective-permute-start(bf16[192,384]{1,0:T(8,128)(2,1)} %get-tuple-element.20), channel_id=1, source_target_pairs={{0,64},{64,0},{128,192},{192,128},{1,65},{65,1},{129,193},{193,129... | collective-permute-start | bytes 442376 | tf_op jit(solution)/shard_map/ppermute | solution.py:37
  96.4 18.9 %collective-permute-start.13 = (f32[512,384]{1,0:T(8,128)}, f32[512,384]{1,0:T(8,128)}, u32[]{:S(2)}, u32[]{:S(2)}) collective-permute-start(f32[512,384]{1,0:T(8,128)} %bitcast.28), channel_id=1, source_target_pairs={{0,1},{1,0},{2,3},{3,2},{4,5},{5,4},{6,7},{7,6},{8,9},{9,8},{10,11... | collective-permute-start | bytes 2359304 | tf_op jit(solution)/shard_map/ppermute | solution.py:29
  98.6 6.7 %collective-permute-start.9 = (bf16[192,384]{1,0:T(8,128)(2,1)}, bf16[192,384]{1,0:T(8,128)(2,1)S(1)}, u32[]{:S(2)}, u32[]{:S(2)}) collective-permute-start(bf16[192,384]{1,0:T(8,128)(2,1)} %copy-done.12), channel_id=1, source_target_pairs={{0,192},{64,128},{128,64},{192,0},{1,193},{65,129},{129,65},{193,1... | collective-permute-start | bytes 442376 | tf_op jit(solution)/shard_map/ppermute | solution.py:37
  101.6 7.1 %collective-permute-start.8 = (bf16[192,384]{1,0:T(8,128)(2,1)S(1)}, bf16[192,384]{1,0:T(8,128)(2,1)S(1)}, u32[]{:S(2)}, u32[]{:S(2)}) collective-permute-start(bf16[192,384]{1,0:T(8,128)(2,1)S(1)} %add_convert_fusion.3.refs_0_), channel_id=1, source_target_pairs={{0,192},{64,128},{128,64},{192,0},{1,193},{65,129},{129,65},{193,1... | collective-permute-start | bytes 442376 | tf_op jit(solution)/shard_map/ppermute | solution.py:37
  106.3 4.1 %collective-permute-start.10 = (bf16[192,384]{1,0:T(8,128)(2,1)S(1)}, bf16[192,384]{1,0:T(8,128)(2,1)S(1)}, u32[]{:S(2)}, u32[]{:S(2)}) collective-permute-start(bf16[192,384]{1,0:T(8,128)(2,1)S(1)} %add_convert_fusion.2.refs_2_), channel_id=1, source_target_pairs={{0,64},{64,0},{128,192},{192,128},{1,65},{65,1},{129,193},{193,129... | collective-permute-start | bytes 442376 | tf_op jit(solution)/shard_map/ppermute | solution.py:37
  112.5 4.6 %collective-permute-start.14 = (f32[384]{0:T(512)S(1)}, f32[384]{0:T(512)S(1)}, u32[]{:S(2)}, u32[]{:S(2)}) collective-permute-start(f32[384]{0:T(512)S(1)} %sub.100), channel_id=1, source_target_pairs={{0,1},{1,0},{2,3},{3,2},{4,5},{5,4},{6,7},{7,6},{8,9},{9,8},{10,11... | collective-permute-start | bytes 4616 | tf_op jit(solution)/shard_map/ppermute | solution.py:29
  116.5 1.8 collective-permute-start.11
  116.7 2.1 collective-permute-start.12
  119.7 46.7 %copy-start.8 = (bf16[512,384]{1,0:T(8,128)(2,1)S(1)}, bf16[512,384]{1,0:T(8,128)(2,1)}, u32[]{:S(2)}) copy-start(bf16[512,384]{1,0:T(8,128)(2,1)} %copy-done.6) | copy-start | bytes 1179652
  120.5 20.1 %all-to-all-start.2 = ((bf16[32,56,128]{2,1,0:T(8,128)(2,1)}), bf16[32,56,128]{2,1,0:T(8,128)(2,1)}, u32[]{:S(2)}, u32[]{:S(2)}) async-start(bf16[32,56,128]{2,1,0:T(8,128)(2,1)} %pad_maximum_fusion), calls=%async_computation.2 | async-start | bytes 917504 | tf_op jit(solution)/shard_map/all_to_all | solution.py:421
  127.1 40.0 %copy-start.24 = (s32[384]{0:T(512)S(1)}, s32[384]{0:T(512)}, u32[]{:S(2)}) copy-start(s32[384]{0:T(512)} %copy-done.23) | copy-start | bytes 4612
  160.8 5.5 %collective-permute-start.15 = (bf16[512,384]{1,0:T(8,128)(2,1)S(1)}, bf16[512,384]{1,0:T(8,128)(2,1)S(1)}, u32[]{:S(2)}, u32[]{:S(2)}) collective-permute-start(bf16[512,384]{1,0:T(8,128)(2,1)S(1)} %bitcast.88), channel_id=1, source_target_pairs={{0,1},{1,0},{2,3},{3,2},{4,5},{5,4},{6,7},{7,6},{8,9},{9,8},{10,11... | collective-permute-start | bytes 1179656 | tf_op jit(solution)/shard_map/ppermute | solution.py:29
  166.3 19.5 %copy-start.19 = (bf16[512,384]{1,0:T(8,128)(2,1)S(1)}, bf16[512,384]{1,0:T(8,128)(2,1)}, u32[]{:S(2)}) copy-start(bf16[512,384]{1,0:T(8,128)(2,1)} %copy-done.18) | copy-start | bytes 1179652
  167.0 5.5 %collective-permute-start.16 = (bf16[192,384]{1,0:T(8,128)(2,1)S(1)}, bf16[192,384]{1,0:T(8,128)(2,1)S(1)}, u32[]{:S(2)}, u32[]{:S(2)}) collective-permute-start(bf16[192,384]{1,0:T(8,128)(2,1)S(1)} %get-tuple-element.25), channel_id=1, source_target_pairs={{0,64},{64,0},{128,192},{192,128},{1,65},{65,1},{129,193},{193,129... | collective-permute-start | bytes 442376 | tf_op jit(solution)/shard_map/ppermute | solution.py:37
  168.5 6.6 %collective-permute-start.18 = (bf16[192,384]{1,0:T(8,128)(2,1)S(1)}, bf16[192,384]{1,0:T(8,128)(2,1)S(1)}, u32[]{:S(2)}, u32[]{:S(2)}) collective-permute-start(bf16[192,384]{1,0:T(8,128)(2,1)S(1)} %get-tuple-element.26), channel_id=1, source_target_pairs={{0,192},{64,128},{128,64},{192,0},{1,193},{65,129},{129,65},{193,1... | collective-permute-start | bytes 442376 | tf_op jit(solution)/shard_map/ppermute | solution.py:37
  172.5 5.8 %collective-permute-start.17 = (bf16[192,384]{1,0:T(8,128)(2,1)S(1)}, bf16[192,384]{1,0:T(8,128)(2,1)S(1)}, u32[]{:S(2)}, u32[]{:S(2)}) collective-permute-start(bf16[192,384]{1,0:T(8,128)(2,1)S(1)} %add_convert_fusion.1.refs_0_), channel_id=1, source_target_pairs={{0,192},{64,128},{128,64},{192,0},{1,193},{65,129},{129,65},{193,1... | collective-permute-start | bytes 442376 | tf_op jit(solution)/shard_map/ppermute | solution.py:37
  175.2 4.9 %collective-permute-start.19 = (bf16[192,384]{1,0:T(8,128)(2,1)S(1)}, bf16[192,384]{1,0:T(8,128)(2,1)S(1)}, u32[]{:S(2)}, u32[]{:S(2)}) collective-permute-start(bf16[192,384]{1,0:T(8,128)(2,1)S(1)} %add_convert_fusion.refs_2_), channel_id=1, source_target_pairs={{0,64},{64,0},{128,192},{192,128},{1,65},{65,1},{129,193},{193,129... | collective-permute-start | bytes 442376 | tf_op jit(solution)/shard_map/ppermute | solution.py:37
  182.4 2.6 %collective-permute-start.21 = (f32[384]{0:T(512)S(1)}, f32[384]{0:T(512)S(1)}, u32[]{:S(2)}, u32[]{:S(2)}) collective-permute-start(f32[384]{0:T(512)S(1)} %sub.106), channel_id=1, source_target_pairs={{0,1},{1,0},{2,3},{3,2},{4,5},{5,4},{6,7},{7,6},{8,9},{9,8},{10,11... | collective-permute-start | bytes 4616 | tf_op jit(solution)/shard_map/ppermute | solution.py:29
  184.2 1.6 collective-permute-start.20
  186.7 22.7 %copy-start.21 = (f32[384,16]{0,1:T(8,128)S(1)}, f32[384,16]{0,1:T(8,128)}, u32[]{:S(2)}) copy-start(f32[384,16]{0,1:T(8,128)} %param.32) | copy-start | bytes 73732
  187.6 20.1 %all-to-all-start.4 = ((bf16[32,56,128]{2,1,0:T(8,128)(2,1)}), bf16[32,56,128]{2,1,0:T(8,128)(2,1)}, u32[]{:S(2)}, u32[]{:S(2)}) async-start(bf16[32,56,128]{2,1,0:T(8,128)(2,1)} %pad_maximum_fusion.1), calls=%async_computation.4 | async-start | bytes 917504 | tf_op jit(solution)/shard_map/all_to_all | solution.py:421
  (20 other events, 152.9 us)

commit v6 on v5

--- a/solution.py
+++ b/solution.py
@@ -126,7 +126,7 @@
         core.reshape(1),
         *in_fast(columns),
         column.reshape(1, -1),
-        *in_fast(stor_own, stor_other, dual_own, dual_other),
+        *in_main(stor_own, stor_other, dual_own, dual_other),
     )
     return own, other, (first, second)
 
@@ -140,7 +140,41 @@
         out_specs=(in_vmem,) * 2,
         name="prices",
         compiler_params=pltpu.CompilerParams(vmem_limit_bytes=VMEM_LIMIT),
-    )(*in_fast(dual_own, dual_other, weight_own, weight_other))
+    )(*in_fast(dual_own, dual_other), *in_main(weight_own, weight_other))
+
+
+def dual_body(received, dual, limit, tail, dual_next, *sent):
+    total = jnp.sum(received[...].astype(jnp.float32), axis=0)
+    share_len = dual.shape[0]
+    strips = dual.shape[1] // total.shape[1]
+    flow = jnp.concatenate(
+        [total[i * share_len : (i + 1) * share_len] for i in range(strips)], axis=1
+    )
+    tail[...] = total[strips * share_len :]
+    bound = limit[...]
+    moved = dual_step(dual[...], flow, SIGMA_FLOW, -bound, bound)
+    dual_next[...] = moved
+    for out in sent:
+        out[...] = jnp.broadcast_to(moved.astype(jnp.bfloat16)[None], out.shape)
+
+
+def dual_updated(received, dual, limit, spread):
+    chips, _, lanes = received.shape
+    in_vmem = pl.BlockSpec(memory_space=pltpu.VMEM)
+    out_shape = (
+        jax.ShapeDtypeStruct((8, lanes), jnp.float32),
+        jax.ShapeDtypeStruct(dual.shape, jnp.float32),
+    )
+    if spread:
+        out_shape += (pltpu.HBM((chips, *dual.shape), jnp.bfloat16),)
+    return pl.pallas_call(
+        dual_body,
+        out_shape=out_shape,
+        in_specs=[in_vmem] * 3,
+        out_specs=(in_vmem,) * len(out_shape),
+        name="duals",
+        compiler_params=pltpu.CompilerParams(vmem_limit_bytes=VMEM_LIMIT),
+    )(received, dual, limit)
 
 
 def update_body(*refs):
@@ -224,14 +258,8 @@
     )(*operands)
 
 
-def sent_to_chips(x):
-    size = Z * X
-    sent = jnp.broadcast_to(x[None], (size, *x.shape))
-    return lax.all_to_all(sent, CHIPS, 0, 0, tiled=True)
-
-
-def gathered_duals(share):
-    own = sent_to_chips(share.astype(jnp.bfloat16)).reshape(-1, share.shape[1])
+def gathered_duals(sent):
+    own = lax.all_to_all(sent, CHIPS, 0, 0, tiled=True).reshape(-1, sent.shape[2])
     return own, swapped(own)
 
 
@@ -419,15 +447,10 @@
             axis=1,
         ).astype(jnp.bfloat16)
         received = lax.all_to_all(sent, CHIPS, 0, 0, tiled=True)
-        summed = jnp.sum(received.astype(jnp.float32), axis=0)
-        flow_share = jnp.concatenate(
-            [summed[i * share_len : (i + 1) * share_len] for i in range(strips)], axis=1
-        )
-        tail = summed[strips * share_len :]
+        tail, dual_flow, *spread = dual_updated(received, dual_flow, limit, iteration == 0)
         balance = (tail[:strips] + tail[strips : 2 * strips]).reshape(row_count)
-        dual_flow = dual_step(dual_flow, flow_share, SIGMA_FLOW, -limit, limit)
         if iteration == 0:
-            dual_own, dual_other = gathered_duals(dual_flow)
+            dual_own, dual_other = gathered_duals(spread[0])
         price_level = price_level + KAPPA / total_units * balance
         dual_store = dual_step(
             dual_store, summed_hours(stor_bar, False), SIGMA_STORE, low_bound, high_bound

time: 211 us -> 205 us (0.972)
  other arithmetic: 15.4 us -> 10.1 us
  Pallas kernels: 8.63 us -> 12 us
  local copies, waits for them, and re-layouts: 8.72 us -> 6.44 us
    pallas_call x0 -> x2, Pallas kernels: none -> 2.57 us  [dual_updated(): pl.pallas_call(dual_body, out_shape=out_shape, in_specs=[in_vmem] * 3, ou...]
    reduce_sum x2 -> x0, other arithmetic: 2.2 us -> none  [shards(): summed = jnp.sum(received.astype(jnp.float32), axis=0)]
  transfers between devices with their start and end apart: 25 -> 25, of which waited for: 17 -> 17; matrix products, arithmetic and copies ran while one was open for 12% -> 11% of each run, Pallas kernels for 1% -> 1%
where the time goes in v6:
time: 205 us; the launch traced here: 204 us
  waiting for transfers between devices  66.2 us (32%)
  starting transfers between devices  51.5 us (25%)
  blocking collectives  40.6 us (20%)
  matrix products  15.7 us (8%)
  Pallas kernels  12 us (6%)
  other arithmetic  10.1 us (5%)
  local copies, waits for them, and re-layouts  6.44 us (3%)
    ppermute x3, waiting for transfers between devices, doubled(): other = lax.ppermute(x, axis, [(i, i ^ step) for i in range(size)])  25.1 us
    all_to_all x2, waiting for transfers between devices, shards(): received = lax.all_to_all(sent, CHIPS, 0, 0, tiled=True)  25 us
    all_to_all x1, blocking collectives, shards(): lax.all_to_all(slot_bus.reshape(area_count, slots), AREAS, 0, 0, tiled=True)  22.2 us
    all_to_all x1, blocking collectives, gathered_duals(): lax.all_to_all(sent, CHIPS, 0, 0, tiled=True).reshape(-1, sent.shape[2])  18.4 us
    ppermute x8, starting transfers between devices, swapped(): return lax.ppermute(x, 'core', [(0, 1), (1, 0)])  14.6 us
    ppermute x8, starting transfers between devices, from_side(): return lax.ppermute(x, 'lines', [(i, i ^ step) for i in range(4)])  10.8 us
    ppermute x8, waiting for transfers between devices, from_side(): return lax.ppermute(x, 'lines', [(i, i ^ step) for i in range(4)])  8.8 us
    all_to_all x2, starting transfers between devices, shards(): received = lax.all_to_all(sent, CHIPS, 0, 0, tiled=True)  8.48 us
  transfers between devices with their start and end apart: 25, of which 17 were waited for; matrix products, arithmetic and copies ran while one was open for 11% of the time, Pallas kernels for 1%

profile of v6, /device:TPU:1, one launch (start us, length us, event | category | flops | bytes accessed | tf_op | source)
XLA Modules:
  0.0 203.7 jit_solution(8908082192898826326)
XLA Ops:
  1.9 22.2 %all_to_all.32 = s32[64,1,8]{2,1,0:T(1,128)S(1)} all-to-all(s32[64,1,8]{2,1,0:T(1,128)S(1)} %bitcast.83), channel_id=1, replica_groups=mesh['lines'=4,'z'=8,'x'=4,'core'=2] {'z','x','core'}, dimensions={0} | all-to-all | bytes 4096 | tf_op jit(solution)/shard_map/all_to_all | solution.py:360
  25.5 2.6 %fusion.2 = bf16[64,8,1024]{2,1,0:T(8,128)(2,1)} fusion(bf16[1024,1280]{1,0:T(8,128)(2,1)S(1)} %copy-done, s32[512]{0:T(512)S(1)} %eq.148), kind=kOutput, calls=%fused_computation.4 | convolution fusion | flops 1343356928 | bytes 3672064 | tf_op jit(solution)/shard_map/dot_general | solution.py:368
  28.1 5.6 %all-to-all-start.1 = ((bf16[64,8,1024]{2,1,0:T(8,128)(2,1)}), bf16[64,8,1024]{2,1,0:T(8,128)(2,1)}, u32[]{:S(2)}, u32[]{:S(2)}) async-start(bf16[64,8,1024]{2,1,0:T(8,128)(2,1)} %fusion.2), calls=%async_computation.1 | async-start | bytes 2097152 | tf_op jit(solution)/shard_map/all_to_all | solution.py:371
  33.7 5.6 %collective-permute-start = (bf16[1,1,1,16,384]{4,3,2,1,0:T(8,128)(2,1)S(1)}, bf16[1,1,1,16,384]{4,3,2,1,0:T(8,128)(2,1)S(1)}, u32[]{:S(2)}, u32[]{:S(2)}) collective-permute-start(bf16[1,1,1,16,384]{4,3,2,1,0:T(8,128)(2,1)S(1)} %get-tuple-element.54), channel_id=1, source_target_pairs={{0,32},{8,40},{16,48},{24,56},{32,0},{40,8},{48,16},{56,24},{1,33}... | collective-permute-start | bytes 36872 | tf_op jit(solution)/shard_map/ppermute | solution.py:267
  39.2 21.9 %collective-permute-done = bf16[1,1,1,16,384]{4,3,2,1,0:T(8,128)(2,1)S(1)} collective-permute-done((bf16[1,1,1,16,384]{4,3,2,1,0:T(8,128)(2,1)S(1)}, bf16[1,1,1,16,384]{4,3,2,1,0:T(8,128)(2,1)S(1)}, u32[]{:S(2)}, u32[]{:S(2)}) %collective-permute-start) | collective-permute-done | bytes 12320 | tf_op jit(solution)/shard_map/ppermute | solution.py:267
  61.7 3.0 %collective-permute-done.1 = bf16[2,1,1,16,384]{4,3,2,1,0:T(8,128)(2,1)S(1)} collective-permute-done((bf16[2,1,1,16,384]{4,3,2,1,0:T(8,128)(2,1)S(1)}, bf16[2,1,1,16,384]{4,3,2,1,0:T(8,128)(2,1)S(1)}, u32[]{:S(2)}, u32[]{:S(2)}) %collective-permute-start.1) | collective-permute-done | bytes 24608 | tf_op jit(solution)/shard_map/ppermute | solution.py:267
  64.8 2.2 %collective-permute-start.2 = (bf16[2,2,1,16,384]{4,3,2,1,0:T(8,128)(2,1)S(1)}, bf16[2,2,1,16,384]{4,3,2,1,0:T(8,128)(2,1)S(1)}, u32[]{:S(2)}, u32[]{:S(2)}) collective-permute-start(bf16[2,2,1,16,384]{4,3,2,1,0:T(8,128)(2,1)S(1)} %maximum_select_fusion.4), channel_id=1, source_target_pairs={{0,8},{8,0},{16,24},{24,16},{32,40},{40,32},{48,56},{56,48},{1,9},... | collective-permute-start | bytes 147464 | tf_op jit(solution)/shard_map/ppermute | solution.py:267
  70.1 2.1 %collective-permute-start.5 = (bf16[8,1,16,384]{3,2,0,1:T(8,128)(2,1)S(1)}, bf16[8,1,16,384]{3,2,0,1:T(8,128)(2,1)S(1)}, u32[]{:S(2)}, u32[]{:S(2)}) collective-permute-start(bf16[8,1,16,384]{3,2,0,1:T(8,128)(2,1)S(1)} %bitcast.80), channel_id=1, source_target_pairs={{0,6},{2,4},{4,2},{6,0},{1,7},{3,5},{5,3},{7,1},{8,14},{10,12},{12... | collective-permute-start | bytes 294920 | tf_op jit(solution)/shard_map/ppermute | solution.py:282
  72.9 1.9 collective-permute-done.5
  74.8 2.4 %collective-permute-done.4 = bf16[8,1,16,384]{3,2,0,1:T(8,128)(2,1)S(1)} collective-permute-done((bf16[8,1,16,384]{3,2,0,1:T(8,128)(2,1)S(1)}, bf16[8,1,16,384]{3,2,0,1:T(8,128)(2,1)S(1)}, u32[]{:S(2)}, u32[]{:S(2)}) %collective-permute-start.4) | collective-permute-done | bytes 98336 | tf_op jit(solution)/shard_map/ppermute | solution.py:282
  77.4 6.0 %collective-permute-start.6 = (bf16[512,384]{1,0:T(8,128)(2,1)S(1)}, bf16[512,384]{1,0:T(8,128)(2,1)S(1)}, u32[]{:S(2)}, u32[]{:S(2)}) collective-permute-start(bf16[512,384]{1,0:T(8,128)(2,1)S(1)} %bitcast.72), channel_id=1, source_target_pairs={{0,1},{1,0},{2,3},{3,2},{4,5},{5,4},{6,7},{7,6},{8,9},{9,8},{10,11... | collective-permute-start | bytes 1179656 | tf_op jit(solution)/shard_map/ppermute | solution.py:29
  83.4 2.7 %fusion.11 = f32[1024,384]{1,0:T(8,128)} fusion(bf16[1024,1280]{1,0:T(8,128)(2,1)S(1)} %copy-done, f32[384,1280]{1,0:T(8,128)S(1)} %copy-done.13), kind=kOutput, calls=%fused_computation.18 | convolution fusion | flops 1007124480 | bytes 6160384 | tf_op jit(solution)/shard_map/dot_general | solution.py:390
  86.9 3.1 %weights.1 = (bf16[512,384]{1,0:T(8,128)(2,1)S(1)}, bf16[512,384]{1,0:T(8,128)(2,1)S(1)}, bf16[192,384]{1,0:T(8,128)(2,1)S(1)}, bf16[192,384]{1,0:T(8,128)(2,1)S(1)}) custom-call(s32[1]{0:T(128)} %bitcast.core, bf16[512,1024]{1,0:T(8,128)(2,1)} %bitcast.3.columns, s32[1,256]{1,0:T(1,128)S(1)} %bitcast.70, bf16[512,128]{1,0:T(8,128)(2,1)} %bitcast.78, ...), custom_call_target="tpu_custom_call" | custom-call | tf_op jit(solution)/shard_map/weights/pallas_call | solution.py:117
  93.2 1.7 reduce_sum.29
  95.0 2.0 collective-permute-start.9
  99.5 2.0 collective-permute-done.9
  101.6 2.3 %fusion.17.refs_10_ = f32[384,128]{1,0:T(8,128)} fusion(f32[384,128]{1,0:T(8,128)} %param.33, s32[384]{0:T(512)S(1)} %add_select_fusion), kind=kOutput, calls=%fused_computation.25 | convolution fusion | flops 227082240 | bytes 394752 | tf_op jit(solution)/shard_map/dot_general | solution.py:309
  105.6 2.1 %update.2 = (bf16[384,384]{1,0:T(8,128)(2,1)S(1)}, f32[384,256]{1,0:T(8,128)S(1)}, f32[384,128]{1,0:T(8,128)S(1)}, f32[8,384]{1,0:T(8,128)S(1)}) custom-call(bf16[192,384]{1,0:T(8,128)(2,1)S(1)} %add_convert_fusion.3.refs_0_, bf16[192,384]{1,0:T(8,128)(2,1)S(1)} %collective-permute-done.8.refs_1_, bf16[192,384]{1,0:T(8,128)(2,1)S(1)} %add_convert_fusion.2.refs_2_, ...), custom_call_target="tpu_custom_call" | custom-call | tf_op jit(solution)/shard_map/update/pallas_call | solution.py:246
  107.8 2.5 %collective-permute-start.14 = (f32[384]{0:T(512)S(1)}, f32[384]{0:T(512)S(1)}, u32[]{:S(2)}, u32[]{:S(2)}) collective-permute-start(f32[384]{0:T(512)S(1)} %sub.94), channel_id=1, source_target_pairs={{0,1},{1,0},{2,3},{3,2},{4,5},{5,4},{6,7},{7,6},{8,9},{9,8},{10,11... | collective-permute-start | bytes 4616 | tf_op jit(solution)/shard_map/ppermute | solution.py:29
  115.5 3.9 %all-to-all-start.2 = ((bf16[32,56,128]{2,1,0:T(8,128)(2,1)}), bf16[32,56,128]{2,1,0:T(8,128)(2,1)S(1)}, u32[]{:S(2)}, u32[]{:S(2)}) async-start(bf16[32,56,128]{2,1,0:T(8,128)(2,1)} %pad_maximum_fusion), calls=%async_computation.2 | async-start | bytes 917504 | tf_op jit(solution)/shard_map/all_to_all | solution.py:449
  121.7 13.2 %all-to-all-done.2.received = bf16[32,56,128]{2,1,0:T(8,128)(2,1)S(1)} async-done(((bf16[32,56,128]{2,1,0:T(8,128)(2,1)}), bf16[32,56,128]{2,1,0:T(8,128)(2,1)S(1)}, u32[]{:S(2)}, u32[]{:S(2)}) %all-to-all-start.2) | async-done | bytes 458784 | tf_op jit(solution)/shard_map/all_to_all | solution.py:449
  135.8 18.4 %all_to_all.33 = bf16[32,16,384]{2,1,0:T(8,128)(2,1)S(1)} all-to-all(bf16[32,16,384]{2,1,0:T(8,128)(2,1)} %get-tuple-element.30), channel_id=1, replica_groups=mesh['lines'=4,'z'=8,'x'=4,'core'=2] {'z','x'}, dimensions={0} | all-to-all | bytes 786432 | tf_op jit(solution)/shard_map/all_to_all | solution.py:262
  154.2 3.0 %collective-permute-start.15 = (bf16[512,384]{1,0:T(8,128)(2,1)S(1)}, bf16[512,384]{1,0:T(8,128)(2,1)S(1)}, u32[]{:S(2)}, u32[]{:S(2)}) collective-permute-start(bf16[512,384]{1,0:T(8,128)(2,1)S(1)} %bitcast.67), channel_id=1, source_target_pairs={{0,1},{1,0},{2,3},{3,2},{4,5},{5,4},{6,7},{7,6},{8,9},{9,8},{10,11... | collective-permute-start | bytes 1179656 | tf_op jit(solution)/shard_map/ppermute | solution.py:29
  159.0 1.8 prices.1
  162.3 2.4 %collective-permute-start.18 = (bf16[192,384]{1,0:T(8,128)(2,1)S(1)}, bf16[192,384]{1,0:T(8,128)(2,1)S(1)}, u32[]{:S(2)}, u32[]{:S(2)}) collective-permute-start(bf16[192,384]{1,0:T(8,128)(2,1)S(1)} %get-tuple-element.32), channel_id=1, source_target_pairs={{0,192},{64,128},{128,64},{192,0},{1,193},{65,129},{129,65},{193,1... | collective-permute-start | bytes 442376 | tf_op jit(solution)/shard_map/ppermute | solution.py:37
  166.3 2.4 %collective-permute-start.17 = (bf16[192,384]{1,0:T(8,128)(2,1)S(1)}, bf16[192,384]{1,0:T(8,128)(2,1)S(1)}, u32[]{:S(2)}, u32[]{:S(2)}) collective-permute-start(bf16[192,384]{1,0:T(8,128)(2,1)S(1)} %add_convert_fusion.1.refs_0_), channel_id=1, source_target_pairs={{0,192},{64,128},{128,64},{192,0},{1,193},{65,129},{129,65},{193,1... | collective-permute-start | bytes 442376 | tf_op jit(solution)/shard_map/ppermute | solution.py:37
  169.9 2.2 %collective-permute-done.17.refs_1_ = bf16[192,384]{1,0:T(8,128)(2,1)S(1)} collective-permute-done((bf16[192,384]{1,0:T(8,128)(2,1)S(1)}, bf16[192,384]{1,0:T(8,128)(2,1)S(1)}, u32[]{:S(2)}, u32[]{:S(2)}) %collective-permute-start.17) | collective-permute-done | bytes 147488 | tf_op jit(solution)/shard_map/ppermute | solution.py:37
  173.4 2.4 %update.3 = (bf16[384,384]{1,0:T(8,128)(2,1)S(1)}, f32[384,256]{1,0:T(8,128)S(1)}, f32[384,128]{1,0:T(8,128)S(1)}, f32[8,384]{1,0:T(8,128)S(1)}) custom-call(bf16[192,384]{1,0:T(8,128)(2,1)S(1)} %add_convert_fusion.1.refs_0_, bf16[192,384]{1,0:T(8,128)(2,1)S(1)} %collective-permute-done.17.refs_1_, bf16[192,384]{1,0:T(8,128)(2,1)S(1)} %add_convert_fusion.refs_2_, ...), custom_call_target="tpu_custom_call" | custom-call | tf_op jit(solution)/shard_map/update/pallas_call | solution.py:246
  175.8 2.1 %collective-permute-start.21 = (f32[384]{0:T(512)S(1)}, f32[384]{0:T(512)S(1)}, u32[]{:S(2)}, u32[]{:S(2)}) collective-permute-start(f32[384]{0:T(512)S(1)} %sub.99), channel_id=1, source_target_pairs={{0,1},{1,0},{2,3},{3,2},{4,5},{5,4},{6,7},{7,6},{8,9},{9,8},{10,11... | collective-permute-start | bytes 4616 | tf_op jit(solution)/shard_map/ppermute | solution.py:29
  181.3 4.6 %all-to-all-start.4 = ((bf16[32,56,128]{2,1,0:T(8,128)(2,1)}), bf16[32,56,128]{2,1,0:T(8,128)(2,1)}, u32[]{:S(2)}, u32[]{:S(2)}) async-start(bf16[32,56,128]{2,1,0:T(8,128)(2,1)} %pad_maximum_fusion.1), calls=%async_computation.4 | async-start | bytes 917504 | tf_op jit(solution)/shard_map/all_to_all | solution.py:449
  187.3 2.3 %fusion.40 = f32[384,128]{1,0:T(8,128)} fusion(f32[384,128]{1,0:T(8,128)} %copy-done.22, s32[384]{0:T(512)S(1)} %add_select_fusion, f32[384,128]{1,0:T(8,128)S(1)} %copy-done.7, f32[384,128]{1,0:T(8,128)S(1)} %get-tuple-element.64, f32[128]{0:T(128)S(1)} %get-tuple-element.62, f32[128]{0:T(128)S(1)} %get-tuple-element.61, pred[384]{0:T(512)(128)(4,1)S(1)} %fusion.58), kind=kOutput, calls=%fused_computation.68 | convolution fusion | flops 227622912 | bytes 789376 | tf_op jit(solution)/shard_map/dot_general | solution.py:309
  189.6 11.8 %all-to-all-done.4.received = bf16[32,56,128]{2,1,0:T(8,128)(2,1)} async-done(((bf16[32,56,128]{2,1,0:T(8,128)(2,1)}), bf16[32,56,128]{2,1,0:T(8,128)(2,1)}, u32[]{:S(2)}, u32[]{:S(2)}) %all-to-all-start.4) | async-done | bytes 458784 | tf_op jit(solution)/shard_map/all_to_all | solution.py:449
  (140 shorter events, 38.0 us)
Async XLA Ops:
  0.6 24.8 %copy-start = (bf16[1024,1280]{1,0:T(8,128)(2,1)S(1)}, bf16[1024,1280]{1,0:T(8,128)(2,1)}, u32[]{:S(2)}) copy-start(bf16[1024,1280]{1,0:T(8,128)(2,1)} %param.17) | copy-start | bytes 7864324
  25.5 41.5 %copy-start.20 = (s32[128]{0:T(128)S(1)}, s32[128]{0:T(128)}, u32[]{:S(2)}) copy-start(s32[128]{0:T(128)} %param.26) | copy-start | bytes 1540
  28.1 58.1 %all-to-all-start.1 = ((bf16[64,8,1024]{2,1,0:T(8,128)(2,1)}), bf16[64,8,1024]{2,1,0:T(8,128)(2,1)}, u32[]{:S(2)}, u32[]{:S(2)}) async-start(bf16[64,8,1024]{2,1,0:T(8,128)(2,1)} %fusion.2), calls=%async_computation.1 | async-start | bytes 2097152 | tf_op jit(solution)/shard_map/all_to_all | solution.py:371
  33.7 27.4 %collective-permute-start = (bf16[1,1,1,16,384]{4,3,2,1,0:T(8,128)(2,1)S(1)}, bf16[1,1,1,16,384]{4,3,2,1,0:T(8,128)(2,1)S(1)}, u32[]{:S(2)}, u32[]{:S(2)}) collective-permute-start(bf16[1,1,1,16,384]{4,3,2,1,0:T(8,128)(2,1)S(1)} %get-tuple-element.54), channel_id=1, source_target_pairs={{0,32},{8,40},{16,48},{24,56},{32,0},{40,8},{48,16},{56,24},{1,33}... | collective-permute-start | bytes 36872 | tf_op jit(solution)/shard_map/ppermute | solution.py:267
  61.1 3.7 %collective-permute-start.1 = (bf16[2,1,1,16,384]{4,3,2,1,0:T(8,128)(2,1)S(1)}, bf16[2,1,1,16,384]{4,3,2,1,0:T(8,128)(2,1)S(1)}, u32[]{:S(2)}, u32[]{:S(2)}) collective-permute-start(bf16[2,1,1,16,384]{4,3,2,1,0:T(8,128)(2,1)S(1)} %maximum_select_fusion.6), channel_id=1, source_target_pairs={{0,16},{8,24},{16,0},{24,8},{32,48},{40,56},{48,32},{56,40},{1,17}... | collective-permute-start | bytes 73736 | tf_op jit(solution)/shard_map/ppermute | solution.py:267
  64.8 3.7 %collective-permute-start.2 = (bf16[2,2,1,16,384]{4,3,2,1,0:T(8,128)(2,1)S(1)}, bf16[2,2,1,16,384]{4,3,2,1,0:T(8,128)(2,1)S(1)}, u32[]{:S(2)}, u32[]{:S(2)}) collective-permute-start(bf16[2,2,1,16,384]{4,3,2,1,0:T(8,128)(2,1)S(1)} %maximum_select_fusion.4), channel_id=1, source_target_pairs={{0,8},{8,0},{16,24},{24,16},{32,40},{40,32},{48,56},{56,48},{1,9},... | collective-permute-start | bytes 147464 | tf_op jit(solution)/shard_map/ppermute | solution.py:267
  68.5 4.4 %collective-permute-start.3 = (bf16[8,1,16,384]{3,2,0,1:T(8,128)(2,1)S(1)}, bf16[8,1,16,384]{3,2,0,1:T(8,128)(2,1)S(1)}, u32[]{:S(2)}, u32[]{:S(2)}) collective-permute-start(bf16[8,1,16,384]{3,2,0,1:T(8,128)(2,1)S(1)} %bitcast.79), channel_id=1, source_target_pairs={{0,2},{2,0},{4,6},{6,4},{1,3},{3,1},{5,7},{7,5},{8,10},{10,8},{12,... | collective-permute-start | bytes 294920 | tf_op jit(solution)/shard_map/ppermute | solution.py:282
  70.1 4.7 %collective-permute-start.5 = (bf16[8,1,16,384]{3,2,0,1:T(8,128)(2,1)S(1)}, bf16[8,1,16,384]{3,2,0,1:T(8,128)(2,1)S(1)}, u32[]{:S(2)}, u32[]{:S(2)}) collective-permute-start(bf16[8,1,16,384]{3,2,0,1:T(8,128)(2,1)S(1)} %bitcast.80), channel_id=1, source_target_pairs={{0,6},{2,4},{4,2},{6,0},{1,7},{3,5},{5,3},{7,1},{8,14},{10,12},{12... | collective-permute-start | bytes 294920 | tf_op jit(solution)/shard_map/ppermute | solution.py:282
  72.3 5.0 %collective-permute-start.4 = (bf16[8,1,16,384]{3,2,0,1:T(8,128)(2,1)S(1)}, bf16[8,1,16,384]{3,2,0,1:T(8,128)(2,1)S(1)}, u32[]{:S(2)}, u32[]{:S(2)}) collective-permute-start(bf16[8,1,16,384]{3,2,0,1:T(8,128)(2,1)S(1)} %bitcast.81), channel_id=1, source_target_pairs={{0,4},{2,6},{4,0},{6,2},{1,5},{3,7},{5,1},{7,3},{8,12},{10,14},{12... | collective-permute-start | bytes 294920 | tf_op jit(solution)/shard_map/ppermute | solution.py:282
  77.4 8.8 %collective-permute-start.6 = (bf16[512,384]{1,0:T(8,128)(2,1)S(1)}, bf16[512,384]{1,0:T(8,128)(2,1)S(1)}, u32[]{:S(2)}, u32[]{:S(2)}) collective-permute-start(bf16[512,384]{1,0:T(8,128)(2,1)S(1)} %bitcast.72), channel_id=1, source_target_pairs={{0,1},{1,0},{2,3},{3,2},{4,5},{5,4},{6,7},{7,6},{8,9},{9,8},{10,11... | collective-permute-start | bytes 1179656 | tf_op jit(solution)/shard_map/ppermute | solution.py:29
  90.1 24.1 %copy-start.1 = (bf16[512,384]{1,0:T(8,128)(2,1)}, bf16[512,384]{1,0:T(8,128)(2,1)S(1)}, u32[]{:S(2)}) copy-start(bf16[512,384]{1,0:T(8,128)(2,1)S(1)} %get-tuple-element.24.weight_own) | copy-start | bytes 1179652
  90.1 6.9 %collective-permute-start.7 = (bf16[192,384]{1,0:T(8,128)(2,1)S(1)}, bf16[192,384]{1,0:T(8,128)(2,1)}, u32[]{:S(2)}, u32[]{:S(2)}) collective-permute-start(bf16[192,384]{1,0:T(8,128)(2,1)S(1)} %get-tuple-element.25), channel_id=1, source_target_pairs={{0,64},{64,0},{128,192},{192,128},{1,65},{65,1},{129,193},{193,129... | collective-permute-start | bytes 442376 | tf_op jit(solution)/shard_map/ppermute | solution.py:37
  92.8 17.5 %collective-permute-start.13 = (f32[512,384]{1,0:T(8,128)}, f32[512,384]{1,0:T(8,128)}, u32[]{:S(2)}, u32[]{:S(2)}) collective-permute-start(f32[512,384]{1,0:T(8,128)} %bitcast.23), channel_id=1, source_target_pairs={{0,1},{1,0},{2,3},{3,2},{4,5},{5,4},{6,7},{7,6},{8,9},{9,8},{10,11... | collective-permute-start | bytes 2359304 | tf_op jit(solution)/shard_map/ppermute | solution.py:29
  95.0 6.5 %collective-permute-start.9 = (bf16[192,384]{1,0:T(8,128)(2,1)S(1)}, bf16[192,384]{1,0:T(8,128)(2,1)S(1)}, u32[]{:S(2)}, u32[]{:S(2)}) collective-permute-start(bf16[192,384]{1,0:T(8,128)(2,1)S(1)} %get-tuple-element.26), channel_id=1, source_target_pairs={{0,192},{64,128},{128,64},{192,0},{1,193},{65,129},{129,65},{193,1... | collective-permute-start | bytes 442376 | tf_op jit(solution)/shard_map/ppermute | solution.py:37
  97.9 6.6 %collective-permute-start.8 = (bf16[192,384]{1,0:T(8,128)(2,1)S(1)}, bf16[192,384]{1,0:T(8,128)(2,1)S(1)}, u32[]{:S(2)}, u32[]{:S(2)}) collective-permute-start(bf16[192,384]{1,0:T(8,128)(2,1)S(1)} %add_convert_fusion.3.refs_0_), channel_id=1, source_target_pairs={{0,192},{64,128},{128,64},{192,0},{1,193},{65,129},{129,65},{193,1... | collective-permute-start | bytes 442376 | tf_op jit(solution)/shard_map/ppermute | solution.py:37
  101.5 4.1 %collective-permute-start.10 = (bf16[192,384]{1,0:T(8,128)(2,1)S(1)}, bf16[192,384]{1,0:T(8,128)(2,1)S(1)}, u32[]{:S(2)}, u32[]{:S(2)}) collective-permute-start(bf16[192,384]{1,0:T(8,128)(2,1)S(1)} %add_convert_fusion.2.refs_2_), channel_id=1, source_target_pairs={{0,64},{64,0},{128,192},{192,128},{1,65},{65,1},{129,193},{193,129... | collective-permute-start | bytes 442376 | tf_op jit(solution)/shard_map/ppermute | solution.py:37
  107.7 49.5 %copy-start.6 = (f32[384,128]{1,0:T(8,128)}, f32[384,128]{1,0:T(8,128)S(1)}, u32[]{:S(2)}) copy-start(f32[384,128]{1,0:T(8,128)S(1)} %get-tuple-element.34.refs_12_) | copy-start | bytes 589828
  107.8 4.3 %collective-permute-start.14 = (f32[384]{0:T(512)S(1)}, f32[384]{0:T(512)S(1)}, u32[]{:S(2)}, u32[]{:S(2)}) collective-permute-start(f32[384]{0:T(512)S(1)} %sub.94), channel_id=1, source_target_pairs={{0,1},{1,0},{2,3},{3,2},{4,5},{5,4},{6,7},{7,6},{8,9},{9,8},{10,11... | collective-permute-start | bytes 4616 | tf_op jit(solution)/shard_map/ppermute | solution.py:29
  111.5 1.8 collective-permute-start.11
  111.7 2.1 %collective-permute-start.12 = (bf16[384,384]{1,0:T(8,128)(2,1)S(1)}, bf16[384,384]{1,0:T(8,128)(2,1)S(1)}, u32[]{:S(2)}, u32[]{:S(2)}) collective-permute-start(bf16[384,384]{1,0:T(8,128)(2,1)S(1)} %get-tuple-element.27), channel_id=1, source_target_pairs={{0,1},{1,0},{2,3},{3,2},{4,5},{5,4},{6,7},{7,6},{8,9},{9,8},{10,11... | collective-permute-start | bytes 884744 | tf_op jit(solution)/shard_map/ppermute | solution.py:29
  114.6 42.6 %copy-start.21 = (f32[128]{0:T(128)S(1)}, f32[128]{0:T(128)}, u32[]{:S(2)}) copy-start(f32[128]{0:T(128)} %param.29) | copy-start | bytes 1540
  115.5 19.4 %all-to-all-start.2 = ((bf16[32,56,128]{2,1,0:T(8,128)(2,1)}), bf16[32,56,128]{2,1,0:T(8,128)(2,1)S(1)}, u32[]{:S(2)}, u32[]{:S(2)}) async-start(bf16[32,56,128]{2,1,0:T(8,128)(2,1)} %pad_maximum_fusion), calls=%async_computation.2 | async-start | bytes 917504 | tf_op jit(solution)/shard_map/all_to_all | solution.py:449
  154.2 4.7 %collective-permute-start.15 = (bf16[512,384]{1,0:T(8,128)(2,1)S(1)}, bf16[512,384]{1,0:T(8,128)(2,1)S(1)}, u32[]{:S(2)}, u32[]{:S(2)}) collective-permute-start(bf16[512,384]{1,0:T(8,128)(2,1)S(1)} %bitcast.67), channel_id=1, source_target_pairs={{0,1},{1,0},{2,3},{3,2},{4,5},{5,4},{6,7},{7,6},{8,9},{9,8},{10,11... | collective-permute-start | bytes 1179656 | tf_op jit(solution)/shard_map/ppermute | solution.py:29
  158.9 20.5 %copy-start.17 = (bf16[512,384]{1,0:T(8,128)(2,1)S(1)}, bf16[512,384]{1,0:T(8,128)(2,1)}, u32[]{:S(2)}) copy-start(bf16[512,384]{1,0:T(8,128)(2,1)} %copy-done.16) | copy-start | bytes 1179652
  160.8 19.1 %copy-start.2 = (bf16[512,384]{1,0:T(8,128)(2,1)S(1)}, bf16[512,384]{1,0:T(8,128)(2,1)}, u32[]{:S(2)}) copy-start(bf16[512,384]{1,0:T(8,128)(2,1)} %copy-done.1) | copy-start | bytes 1179652
  160.8 5.5 %collective-permute-start.16 = (bf16[192,384]{1,0:T(8,128)(2,1)S(1)}, bf16[192,384]{1,0:T(8,128)(2,1)S(1)}, u32[]{:S(2)}, u32[]{:S(2)}) collective-permute-start(bf16[192,384]{1,0:T(8,128)(2,1)S(1)} %get-tuple-element.31), channel_id=1, source_target_pairs={{0,64},{64,0},{128,192},{192,128},{1,65},{65,1},{129,193},{193,129... | collective-permute-start | bytes 442376 | tf_op jit(solution)/shard_map/ppermute | solution.py:37
  162.3 6.5 %collective-permute-start.18 = (bf16[192,384]{1,0:T(8,128)(2,1)S(1)}, bf16[192,384]{1,0:T(8,128)(2,1)S(1)}, u32[]{:S(2)}, u32[]{:S(2)}) collective-permute-start(bf16[192,384]{1,0:T(8,128)(2,1)S(1)} %get-tuple-element.32), channel_id=1, source_target_pairs={{0,192},{64,128},{128,64},{192,0},{1,193},{65,129},{129,65},{193,1... | collective-permute-start | bytes 442376 | tf_op jit(solution)/shard_map/ppermute | solution.py:37
  166.3 5.8 %collective-permute-start.17 = (bf16[192,384]{1,0:T(8,128)(2,1)S(1)}, bf16[192,384]{1,0:T(8,128)(2,1)S(1)}, u32[]{:S(2)}, u32[]{:S(2)}) collective-permute-start(bf16[192,384]{1,0:T(8,128)(2,1)S(1)} %add_convert_fusion.1.refs_0_), channel_id=1, source_target_pairs={{0,192},{64,128},{128,64},{192,0},{1,193},{65,129},{129,65},{193,1... | collective-permute-start | bytes 442376 | tf_op jit(solution)/shard_map/ppermute | solution.py:37
  168.8 4.6 %collective-permute-start.19 = (bf16[192,384]{1,0:T(8,128)(2,1)S(1)}, bf16[192,384]{1,0:T(8,128)(2,1)S(1)}, u32[]{:S(2)}, u32[]{:S(2)}) collective-permute-start(bf16[192,384]{1,0:T(8,128)(2,1)S(1)} %add_convert_fusion.refs_2_), channel_id=1, source_target_pairs={{0,64},{64,0},{128,192},{192,128},{1,65},{65,1},{129,193},{193,129... | collective-permute-start | bytes 442376 | tf_op jit(solution)/shard_map/ppermute | solution.py:37
  175.8 2.9 %collective-permute-start.21 = (f32[384]{0:T(512)S(1)}, f32[384]{0:T(512)S(1)}, u32[]{:S(2)}, u32[]{:S(2)}) collective-permute-start(f32[384]{0:T(512)S(1)} %sub.99), channel_id=1, source_target_pairs={{0,1},{1,0},{2,3},{3,2},{4,5},{5,4},{6,7},{7,6},{8,9},{9,8},{10,11... | collective-permute-start | bytes 4616 | tf_op jit(solution)/shard_map/ppermute | solution.py:29
  177.9 1.6 collective-permute-start.20
  181.3 20.1 %all-to-all-start.4 = ((bf16[32,56,128]{2,1,0:T(8,128)(2,1)}), bf16[32,56,128]{2,1,0:T(8,128)(2,1)}, u32[]{:S(2)}, u32[]{:S(2)}) async-start(bf16[32,56,128]{2,1,0:T(8,128)(2,1)} %pad_maximum_fusion.1), calls=%async_computation.4 | async-start | bytes 917504 | tf_op jit(solution)/shard_map/all_to_all | solution.py:449
  (16 other events, 130.3 us)

commit v7 on v6

--- a/solution.py
+++ b/solution.py
@@ -43,7 +43,8 @@
 
 
 def summed_pairs(halves):
-    first, second = with_side(halves[0], 1), with_side(halves[1], 3)
+    first = with_side(halves[0], 1)
+    second = with_side(halves[1], 3)
     return first, from_side(first, 3), second, from_side(second, 1)
 
 
@@ -174,49 +175,54 @@
         out_specs=(in_vmem,) * len(out_shape),
         name="duals",
         compiler_params=pltpu.CompilerParams(vmem_limit_bytes=VMEM_LIMIT),
-    )(received, dual, limit)
-
-
-def update_body(*refs):
-    (
-        first,
-        first_far,
-        second,
-        second_far,
-        level,
-        gen_quad,
-        gen_lin,
-        gen_max,
-        stor_quad,
-        stor_rate,
-        back,
-        gen_now,
-        stor_now,
-        *old,
-        bar_low,
-        gen_next,
-        stor_next,
-        total,
-    ) = refs
+    )(*in_fast(received), dual, limit)
+
+
+def base_body(level, gen_quad, gen_lin, stor_quad, back, gen_now, stor_now, *refs):
+    *old, gen_base, stor_base, gen_held, stor_held = refs
+    gen, stor = gen_now[...], stor_now[...]
+    gen_mid, stor_mid = gen, stor
+    if old:
+        gen_mid = gen + THETA * (gen - old[0][...])
+        stor_mid = stor + THETA * (stor - old[1][...])
+    gen_cost = 2.0 * gen_quad[...] * gen_mid + gen_lin[...] + level[...]
+    stor_cost = 2.0 * stor_quad[...] * stor_mid + level[...] + back[...]
+    gen_base[...] = gen_mid - TAU * gen_cost
+    stor_base[...] = stor_mid - TAU * stor_cost
+    gen_held[...] = gen
+    stor_held[...] = stor
+
+
+def update_body(
+    first,
+    first_far,
+    second,
+    second_far,
+    gen_base,
+    stor_base,
+    gen_now,
+    stor_now,
+    gen_max,
+    stor_rate,
+    bar_low,
+    gen_next,
+    stor_next,
+    total,
+):
     row_count, gen_count = gen_now.shape
     half = row_count // 2
+    rate = stor_rate[...]
     bars = []
     for i, (near, far) in enumerate(((first, first_far), (second, second_far))):
         rows = slice(i * half, (i + 1) * half)
-        price = near[...].astype(jnp.float32) + far[...].astype(jnp.float32)
-        gen, stor = gen_now[rows], stor_now[rows]
-        gen_mid, stor_mid = gen, stor
-        if old:
-            gen_mid = gen + THETA * (gen - old[0][rows])
-            stor_mid = stor + THETA * (stor - old[1][rows])
-        gen_grad = 2.0 * gen_quad[...] * gen_mid + gen_lin[...] + level[rows] + price[:, :gen_count]
-        moved = jnp.clip(gen_mid - TAU * gen_grad, 0.0, gen_max[...])
-        stor_grad = 2.0 * stor_quad[...] * stor_mid + level[rows] + price[:, gen_count:] + back[rows]
-        rate = stor_rate[...]
-        shifted = jnp.clip(stor_mid - TAU * stor_grad, -rate, rate)
+        change = TAU * (near[...].astype(jnp.float32) + far[...].astype(jnp.float32))
+        moved = jnp.clip(gen_base[rows] - change[:, :gen_count], 0.0, gen_max[...])
+        shifted = jnp.clip(stor_base[rows] - change[:, gen_count:], -rate, rate)
         gen_next[rows] = moved
         stor_next[rows] = shifted
-        bar = jnp.concatenate([2.0 * moved - gen, 2.0 * shifted - stor], axis=1)
+        bar = jnp.concatenate(
+            [2.0 * moved - gen_now[rows], 2.0 * shifted - stor_now[rows]], axis=1
+        )
         bar_low[rows] = bar.astype(jnp.bfloat16)
         bars.append(bar)
     total[...] = lax.dot_general(
@@ -228,20 +234,35 @@
     )
 
 
-def updated(pairs, level, gen_params, stor_params, back, gen_now, stor_now, old):
-    row_count, gen_count = gen_now.shape
-    stor_count = stor_now.shape[1]
+def bases(level, gen_quad, gen_lin, stor_quad, back, gen_now, stor_now, old):
     operands = (
-        *in_fast(*pairs, level[:, None]),
+        *in_fast(level[:, None]),
         *in_main(
-            *(value[None, :] for value in gen_params),
-            *(value[None, :] for value in stor_params),
+            gen_quad[None, :],
+            gen_lin[None, :],
+            stor_quad[None, :],
             back,
             gen_now,
             stor_now,
             *old,
         ),
     )
+    in_vmem = pl.BlockSpec(memory_space=pltpu.VMEM)
+    gen, stor = pltpu.VMEM(gen_now.shape, jnp.float32), pltpu.VMEM(stor_now.shape, jnp.float32)
+    return pl.pallas_call(
+        base_body,
+        out_shape=(gen, stor, gen, stor),
+        in_specs=[in_vmem] * len(operands),
+        out_specs=(in_vmem,) * 4,
+        name="bases",
+        compiler_params=pltpu.CompilerParams(vmem_limit_bytes=VMEM_LIMIT),
+    )(*operands)
+
+
+def updated(pairs, held, gen_max, stor_rate):
+    row_count, gen_count = held[0].shape
+    stor_count = held[1].shape[1]
+    operands = (*in_fast(*pairs, *held), *in_main(gen_max[None, :], stor_rate[None, :]))
     in_vmem = pl.BlockSpec(memory_space=pltpu.VMEM)
     return pl.pallas_call(
         update_body,
@@ -409,15 +430,18 @@
         if iteration > 0:
             halves = later_prices(dual_own, dual_other, weight_own, weight_other)
         back = summed_hours(dual_store, True)
-        bar_low, gen_next, stor_next, total = updated(
-            summed_pairs(halves),
+        held = bases(
             price_level,
-            (gen_quad, gen_lin, gen_max),
-            (stor_quad, stor_rate),
+            gen_quad,
+            gen_lin,
+            stor_quad,
             back,
             gen_now,
             stor_now,
             (gen_old, stor_old) if iteration > 0 else (),
+        )
+        bar_low, gen_next, stor_next, total = updated(
+            summed_pairs(halves), held, gen_max, stor_rate
         )
         balance = total[0] - load_total
         stor_bar = 2.0 * stor_next - stor_now

time: 205 us -> 203 us (level)
  waiting for transfers between devices: 66.2 us -> 63.2 us
    ppermute x8, waiting for transfers between devices: 8.8 us -> 5.74 us  [from_side(): return lax.ppermute(x, 'lines', [(i, i ^ step) for i in range(4)])]
    pallas_call x0 -> x2, Pallas kernels: none -> 3.02 us  [bases(): pl.pallas_call(base_body, out_shape=(gen, stor, gen, stor), in_specs=[in_...]
  transfers between devices with their start and end apart: 25 -> 25, of which waited for: 17 -> 17; matrix products, arithmetic and copies ran while one was open for 11% -> 11% of each run, Pallas kernels for 1% -> 2%
where the time goes in v7:
time: 203 us; the launch traced here: 202 us
  waiting for transfers between devices  63.2 us (31%)
  starting transfers between devices  51.8 us (26%)
  blocking collectives  40.6 us (20%)
  matrix products  15.7 us (8%)
  Pallas kernels  13.3 us (7%)
  other arithmetic  10.1 us (5%)
  local copies, waits for them, and re-layouts  6.43 us (3%)
    ppermute x3, waiting for transfers between devices, doubled(): other = lax.ppermute(x, axis, [(i, i ^ step) for i in range(size)])  25.1 us
    all_to_all x2, waiting for transfers between devices, shards(): received = lax.all_to_all(sent, CHIPS, 0, 0, tiled=True)  25 us
    all_to_all x1, blocking collectives, shards(): lax.all_to_all(slot_bus.reshape(area_count, slots), AREAS, 0, 0, tiled=True)  22.2 us
    all_to_all x1, blocking collectives, gathered_duals(): lax.all_to_all(sent, CHIPS, 0, 0, tiled=True).reshape(-1, sent.shape[2])  18.4 us
    ppermute x8, starting transfers between devices, swapped(): return lax.ppermute(x, 'core', [(0, 1), (1, 0)])  14.8 us
    ppermute x8, starting transfers between devices, from_side(): return lax.ppermute(x, 'lines', [(i, i ^ step) for i in range(4)])  10.9 us
    all_to_all x2, starting transfers between devices, shards(): received = lax.all_to_all(sent, CHIPS, 0, 0, tiled=True)  8.48 us
    ppermute x3, starting transfers between devices, doubled(): other = lax.ppermute(x, axis, [(i, i ^ step) for i in range(size)])  8.42 us
  transfers between devices with their start and end apart: 25, of which 17 were waited for; matrix products, arithmetic and copies ran while one was open for 11% of the time, Pallas kernels for 2%

profile of v7, /device:TPU:1, one launch (start us, length us, event | category | flops | bytes accessed | tf_op | source)
XLA Modules:
  0.0 202.3 jit_solution(13562513463633188161)
XLA Ops:
  1.9 22.2 %all_to_all.32 = s32[64,1,8]{2,1,0:T(1,128)S(1)} all-to-all(s32[64,1,8]{2,1,0:T(1,128)S(1)} %bitcast.83), channel_id=1, replica_groups=mesh['lines'=4,'z'=8,'x'=4,'core'=2] {'z','x','core'}, dimensions={0} | all-to-all | bytes 4096 | tf_op jit(solution)/shard_map/all_to_all | solution.py:381
  25.5 2.6 %fusion.2 = bf16[64,8,1024]{2,1,0:T(8,128)(2,1)} fusion(bf16[1024,1280]{1,0:T(8,128)(2,1)S(1)} %copy-done, s32[512]{0:T(512)S(1)} %eq.148), kind=kOutput, calls=%fused_computation.4 | convolution fusion | flops 1343356928 | bytes 3672064 | tf_op jit(solution)/shard_map/dot_general | solution.py:389
  28.1 5.6 %all-to-all-start.1 = ((bf16[64,8,1024]{2,1,0:T(8,128)(2,1)}), bf16[64,8,1024]{2,1,0:T(8,128)(2,1)}, u32[]{:S(2)}, u32[]{:S(2)}) async-start(bf16[64,8,1024]{2,1,0:T(8,128)(2,1)} %fusion.2), calls=%async_computation.1 | async-start | bytes 2097152 | tf_op jit(solution)/shard_map/all_to_all | solution.py:392
  33.6 5.6 %collective-permute-start = (bf16[1,1,1,16,384]{4,3,2,1,0:T(8,128)(2,1)S(1)}, bf16[1,1,1,16,384]{4,3,2,1,0:T(8,128)(2,1)S(1)}, u32[]{:S(2)}, u32[]{:S(2)}) collective-permute-start(bf16[1,1,1,16,384]{4,3,2,1,0:T(8,128)(2,1)S(1)} %get-tuple-element.70), channel_id=1, source_target_pairs={{0,32},{8,40},{16,48},{24,56},{32,0},{40,8},{48,16},{56,24},{1,33}... | collective-permute-start | bytes 36872 | tf_op jit(solution)/shard_map/ppermute | solution.py:288
  39.2 21.9 %collective-permute-done = bf16[1,1,1,16,384]{4,3,2,1,0:T(8,128)(2,1)S(1)} collective-permute-done((bf16[1,1,1,16,384]{4,3,2,1,0:T(8,128)(2,1)S(1)}, bf16[1,1,1,16,384]{4,3,2,1,0:T(8,128)(2,1)S(1)}, u32[]{:S(2)}, u32[]{:S(2)}) %collective-permute-start) | collective-permute-done | bytes 12320 | tf_op jit(solution)/shard_map/ppermute | solution.py:288
  61.7 3.0 %collective-permute-done.1 = bf16[2,1,1,16,384]{4,3,2,1,0:T(8,128)(2,1)S(1)} collective-permute-done((bf16[2,1,1,16,384]{4,3,2,1,0:T(8,128)(2,1)S(1)}, bf16[2,1,1,16,384]{4,3,2,1,0:T(8,128)(2,1)S(1)}, u32[]{:S(2)}, u32[]{:S(2)}) %collective-permute-start.1) | collective-permute-done | bytes 24608 | tf_op jit(solution)/shard_map/ppermute | solution.py:288
  64.8 2.2 %collective-permute-start.2 = (bf16[2,2,1,16,384]{4,3,2,1,0:T(8,128)(2,1)S(1)}, bf16[2,2,1,16,384]{4,3,2,1,0:T(8,128)(2,1)S(1)}, u32[]{:S(2)}, u32[]{:S(2)}) collective-permute-start(bf16[2,2,1,16,384]{4,3,2,1,0:T(8,128)(2,1)S(1)} %maximum_select_fusion.4), channel_id=1, source_target_pairs={{0,8},{8,0},{16,24},{24,16},{32,40},{40,32},{48,56},{56,48},{1,9},... | collective-permute-start | bytes 147464 | tf_op jit(solution)/shard_map/ppermute | solution.py:288
  70.1 2.1 %collective-permute-start.5 = (bf16[8,1,16,384]{3,2,0,1:T(8,128)(2,1)S(1)}, bf16[8,1,16,384]{3,2,0,1:T(8,128)(2,1)S(1)}, u32[]{:S(2)}, u32[]{:S(2)}) collective-permute-start(bf16[8,1,16,384]{3,2,0,1:T(8,128)(2,1)S(1)} %bitcast.80), channel_id=1, source_target_pairs={{0,6},{2,4},{4,2},{6,0},{1,7},{3,5},{5,3},{7,1},{8,14},{10,12},{12... | collective-permute-start | bytes 294920 | tf_op jit(solution)/shard_map/ppermute | solution.py:303
  72.9 1.9 collective-permute-done.5
  74.8 2.4 %collective-permute-done.4 = bf16[8,1,16,384]{3,2,0,1:T(8,128)(2,1)S(1)} collective-permute-done((bf16[8,1,16,384]{3,2,0,1:T(8,128)(2,1)S(1)}, bf16[8,1,16,384]{3,2,0,1:T(8,128)(2,1)S(1)}, u32[]{:S(2)}, u32[]{:S(2)}) %collective-permute-start.4) | collective-permute-done | bytes 98336 | tf_op jit(solution)/shard_map/ppermute | solution.py:303
  77.4 6.0 %collective-permute-start.6 = (bf16[512,384]{1,0:T(8,128)(2,1)S(1)}, bf16[512,384]{1,0:T(8,128)(2,1)S(1)}, u32[]{:S(2)}, u32[]{:S(2)}) collective-permute-start(bf16[512,384]{1,0:T(8,128)(2,1)S(1)} %bitcast.72), channel_id=1, source_target_pairs={{0,1},{1,0},{2,3},{3,2},{4,5},{5,4},{6,7},{7,6},{8,9},{9,8},{10,11... | collective-permute-start | bytes 1179656 | tf_op jit(solution)/shard_map/ppermute | solution.py:29
  83.4 2.7 %fusion.11 = f32[1024,384]{1,0:T(8,128)} fusion(bf16[1024,1280]{1,0:T(8,128)(2,1)S(1)} %copy-done, f32[384,1280]{1,0:T(8,128)S(1)} %copy-done.13), kind=kOutput, calls=%fused_computation.18 | convolution fusion | flops 1007124480 | bytes 6160384 | tf_op jit(solution)/shard_map/dot_general | solution.py:411
  86.9 3.1 %weights.1 = (bf16[512,384]{1,0:T(8,128)(2,1)S(1)}, bf16[512,384]{1,0:T(8,128)(2,1)S(1)}, bf16[192,384]{1,0:T(8,128)(2,1)S(1)}, bf16[192,384]{1,0:T(8,128)(2,1)S(1)}) custom-call(s32[1]{0:T(128)} %bitcast.core, bf16[512,1024]{1,0:T(8,128)(2,1)} %bitcast.3.columns, s32[1,256]{1,0:T(1,128)S(1)} %bitcast.70, bf16[512,128]{1,0:T(8,128)(2,1)} %bitcast.78, ...), custom_call_target="tpu_custom_call" | custom-call | tf_op jit(solution)/shard_map/weights/pallas_call | solution.py:118
  93.2 1.7 reduce_sum.29
  95.0 2.0 collective-permute-start.9
  99.4 2.1 %collective-permute-done.9 = bf16[192,384]{1,0:T(8,128)(2,1)S(1)} collective-permute-done((bf16[192,384]{1,0:T(8,128)(2,1)S(1)}, bf16[192,384]{1,0:T(8,128)(2,1)S(1)}, u32[]{:S(2)}, u32[]{:S(2)}) %collective-permute-start.9) | collective-permute-done | bytes 147488 | tf_op jit(solution)/shard_map/ppermute | solution.py:37
  101.6 2.3 %fusion.17.back = f32[384,128]{1,0:T(8,128)} fusion(f32[384,128]{1,0:T(8,128)} %param.33, s32[384]{0:T(512)S(1)} %add_select_fusion), kind=kOutput, calls=%fused_computation.25 | convolution fusion | flops 227082240 | bytes 394752 | tf_op jit(solution)/shard_map/dot_general | solution.py:330
  107.1 2.5 %collective-permute-start.14 = (f32[384]{0:T(512)S(1)}, f32[384]{0:T(512)S(1)}, u32[]{:S(2)}, u32[]{:S(2)}) collective-permute-start(f32[384]{0:T(512)S(1)} %sub.94), channel_id=1, source_target_pairs={{0,1},{1,0},{2,3},{3,2},{4,5},{5,4},{6,7},{7,6},{8,9},{9,8},{10,11... | collective-permute-start | bytes 4616 | tf_op jit(solution)/shard_map/ppermute | solution.py:29
  114.9 3.9 %all-to-all-start.2 = ((bf16[32,56,128]{2,1,0:T(8,128)(2,1)}), bf16[32,56,128]{2,1,0:T(8,128)(2,1)S(1)}, u32[]{:S(2)}, u32[]{:S(2)}) async-start(bf16[32,56,128]{2,1,0:T(8,128)(2,1)} %pad_maximum_fusion), calls=%async_computation.2 | async-start | bytes 917504 | tf_op jit(solution)/shard_map/all_to_all | solution.py:473
  121.1 13.2 %all-to-all-done.2.received = bf16[32,56,128]{2,1,0:T(8,128)(2,1)S(1)} async-done(((bf16[32,56,128]{2,1,0:T(8,128)(2,1)}), bf16[32,56,128]{2,1,0:T(8,128)(2,1)S(1)}, u32[]{:S(2)}, u32[]{:S(2)}) %all-to-all-start.2) | async-done | bytes 458784 | tf_op jit(solution)/shard_map/all_to_all | solution.py:473
  135.2 18.4 %all_to_all.33 = bf16[32,16,384]{2,1,0:T(8,128)(2,1)S(1)} all-to-all(bf16[32,16,384]{2,1,0:T(8,128)(2,1)} %get-tuple-element.42), channel_id=1, replica_groups=mesh['lines'=4,'z'=8,'x'=4,'core'=2] {'z','x'}, dimensions={0} | all-to-all | bytes 786432 | tf_op jit(solution)/shard_map/all_to_all | solution.py:283
  153.6 3.0 %collective-permute-start.15 = (bf16[512,384]{1,0:T(8,128)(2,1)S(1)}, bf16[512,384]{1,0:T(8,128)(2,1)S(1)}, u32[]{:S(2)}, u32[]{:S(2)}) collective-permute-start(bf16[512,384]{1,0:T(8,128)(2,1)S(1)} %bitcast.67), channel_id=1, source_target_pairs={{0,1},{1,0},{2,3},{3,2},{4,5},{5,4},{6,7},{7,6},{8,9},{9,8},{10,11... | collective-permute-start | bytes 1179656 | tf_op jit(solution)/shard_map/ppermute | solution.py:29
  156.6 1.7 fusion.38
  158.3 1.8 prices.1
  162.0 2.3 %collective-permute-start.18 = (bf16[192,384]{1,0:T(8,128)(2,1)S(1)}, bf16[192,384]{1,0:T(8,128)(2,1)S(1)}, u32[]{:S(2)}, u32[]{:S(2)}) collective-permute-start(bf16[192,384]{1,0:T(8,128)(2,1)S(1)} %get-tuple-element.44), channel_id=1, source_target_pairs={{0,192},{64,128},{128,64},{192,0},{1,193},{65,129},{129,65},{193,1... | collective-permute-start | bytes 442376 | tf_op jit(solution)/shard_map/ppermute | solution.py:37
  165.6 2.4 %collective-permute-start.17 = (bf16[192,384]{1,0:T(8,128)(2,1)S(1)}, bf16[192,384]{1,0:T(8,128)(2,1)S(1)}, u32[]{:S(2)}, u32[]{:S(2)}) collective-permute-start(bf16[192,384]{1,0:T(8,128)(2,1)S(1)} %add_convert_fusion.1.first), channel_id=1, source_target_pairs={{0,192},{64,128},{128,64},{192,0},{1,193},{65,129},{129,65},{193,1... | collective-permute-start | bytes 442376 | tf_op jit(solution)/shard_map/ppermute | solution.py:37
  169.2 1.6 bases.3
  174.3 2.2 %collective-permute-start.21 = (f32[384]{0:T(512)S(1)}, f32[384]{0:T(512)S(1)}, u32[]{:S(2)}, u32[]{:S(2)}) collective-permute-start(f32[384]{0:T(512)S(1)} %sub.99), channel_id=1, source_target_pairs={{0,1},{1,0},{2,3},{3,2},{4,5},{5,4},{6,7},{7,6},{8,9},{9,8},{10,11... | collective-permute-start | bytes 4616 | tf_op jit(solution)/shard_map/ppermute | solution.py:29
  179.9 4.6 %all-to-all-start.4 = ((bf16[32,56,128]{2,1,0:T(8,128)(2,1)}), bf16[32,56,128]{2,1,0:T(8,128)(2,1)}, u32[]{:S(2)}, u32[]{:S(2)}) async-start(bf16[32,56,128]{2,1,0:T(8,128)(2,1)} %pad_maximum_fusion.1), calls=%async_computation.4 | async-start | bytes 917504 | tf_op jit(solution)/shard_map/all_to_all | solution.py:473
  185.9 2.3 %fusion.40 = f32[384,128]{1,0:T(8,128)} fusion(f32[384,128]{1,0:T(8,128)} %copy-done.22, s32[384]{0:T(512)S(1)} %add_select_fusion, f32[384,128]{1,0:T(8,128)S(1)} %copy-done.7, f32[384,128]{1,0:T(8,128)S(1)} %get-tuple-element.80, f32[128]{0:T(128)S(1)} %get-tuple-element.78, f32[128]{0:T(128)S(1)} %get-tuple-element.77, pred[384]{0:T(512)(128)(4,1)S(1)} %fusion.58), kind=kOutput, calls=%fused_computation.68 | convolution fusion | flops 227622912 | bytes 789376 | tf_op jit(solution)/shard_map/dot_general | solution.py:330
  188.2 11.8 %all-to-all-done.4.received = bf16[32,56,128]{2,1,0:T(8,128)(2,1)} async-done(((bf16[32,56,128]{2,1,0:T(8,128)(2,1)}), bf16[32,56,128]{2,1,0:T(8,128)(2,1)}, u32[]{:S(2)}, u32[]{:S(2)}) %all-to-all-start.4) | async-done | bytes 458784 | tf_op jit(solution)/shard_map/all_to_all | solution.py:473
  200.0 1.7 duals.3
  (142 shorter events, 38.2 us)
Async XLA Ops:
  0.6 24.8 %copy-start = (bf16[1024,1280]{1,0:T(8,128)(2,1)S(1)}, bf16[1024,1280]{1,0:T(8,128)(2,1)}, u32[]{:S(2)}) copy-start(bf16[1024,1280]{1,0:T(8,128)(2,1)} %param.17) | copy-start | bytes 7864324
  25.5 41.5 %copy-start.20 = (s32[128]{0:T(128)S(1)}, s32[128]{0:T(128)}, u32[]{:S(2)}) copy-start(s32[128]{0:T(128)} %param.26) | copy-start | bytes 1540
  28.1 58.1 %all-to-all-start.1 = ((bf16[64,8,1024]{2,1,0:T(8,128)(2,1)}), bf16[64,8,1024]{2,1,0:T(8,128)(2,1)}, u32[]{:S(2)}, u32[]{:S(2)}) async-start(bf16[64,8,1024]{2,1,0:T(8,128)(2,1)} %fusion.2), calls=%async_computation.1 | async-start | bytes 2097152 | tf_op jit(solution)/shard_map/all_to_all | solution.py:392
  33.6 27.4 %collective-permute-start = (bf16[1,1,1,16,384]{4,3,2,1,0:T(8,128)(2,1)S(1)}, bf16[1,1,1,16,384]{4,3,2,1,0:T(8,128)(2,1)S(1)}, u32[]{:S(2)}, u32[]{:S(2)}) collective-permute-start(bf16[1,1,1,16,384]{4,3,2,1,0:T(8,128)(2,1)S(1)} %get-tuple-element.70), channel_id=1, source_target_pairs={{0,32},{8,40},{16,48},{24,56},{32,0},{40,8},{48,16},{56,24},{1,33}... | collective-permute-start | bytes 36872 | tf_op jit(solution)/shard_map/ppermute | solution.py:288
  61.1 3.7 %collective-permute-start.1 = (bf16[2,1,1,16,384]{4,3,2,1,0:T(8,128)(2,1)S(1)}, bf16[2,1,1,16,384]{4,3,2,1,0:T(8,128)(2,1)S(1)}, u32[]{:S(2)}, u32[]{:S(2)}) collective-permute-start(bf16[2,1,1,16,384]{4,3,2,1,0:T(8,128)(2,1)S(1)} %maximum_select_fusion.6), channel_id=1, source_target_pairs={{0,16},{8,24},{16,0},{24,8},{32,48},{40,56},{48,32},{56,40},{1,17}... | collective-permute-start | bytes 73736 | tf_op jit(solution)/shard_map/ppermute | solution.py:288
  64.8 3.7 %collective-permute-start.2 = (bf16[2,2,1,16,384]{4,3,2,1,0:T(8,128)(2,1)S(1)}, bf16[2,2,1,16,384]{4,3,2,1,0:T(8,128)(2,1)S(1)}, u32[]{:S(2)}, u32[]{:S(2)}) collective-permute-start(bf16[2,2,1,16,384]{4,3,2,1,0:T(8,128)(2,1)S(1)} %maximum_select_fusion.4), channel_id=1, source_target_pairs={{0,8},{8,0},{16,24},{24,16},{32,40},{40,32},{48,56},{56,48},{1,9},... | collective-permute-start | bytes 147464 | tf_op jit(solution)/shard_map/ppermute | solution.py:288
  68.2 15.2 %copy-start.13 = (f32[384,1280]{1,0:T(8,128)S(1)}, f32[384,1280]{1,0:T(8,128)}, u32[]{:S(2)}) copy-start(f32[384,1280]{1,0:T(8,128)} %param.18) | copy-start | bytes 5898244
  68.5 4.4 %collective-permute-start.3 = (bf16[8,1,16,384]{3,2,0,1:T(8,128)(2,1)S(1)}, bf16[8,1,16,384]{3,2,0,1:T(8,128)(2,1)S(1)}, u32[]{:S(2)}, u32[]{:S(2)}) collective-permute-start(bf16[8,1,16,384]{3,2,0,1:T(8,128)(2,1)S(1)} %bitcast.79), channel_id=1, source_target_pairs={{0,2},{2,0},{4,6},{6,4},{1,3},{3,1},{5,7},{7,5},{8,10},{10,8},{12,... | collective-permute-start | bytes 294920 | tf_op jit(solution)/shard_map/ppermute | solution.py:303
  70.1 4.7 %collective-permute-start.5 = (bf16[8,1,16,384]{3,2,0,1:T(8,128)(2,1)S(1)}, bf16[8,1,16,384]{3,2,0,1:T(8,128)(2,1)S(1)}, u32[]{:S(2)}, u32[]{:S(2)}) collective-permute-start(bf16[8,1,16,384]{3,2,0,1:T(8,128)(2,1)S(1)} %bitcast.80), channel_id=1, source_target_pairs={{0,6},{2,4},{4,2},{6,0},{1,7},{3,5},{5,3},{7,1},{8,14},{10,12},{12... | collective-permute-start | bytes 294920 | tf_op jit(solution)/shard_map/ppermute | solution.py:303
  72.2 5.0 %collective-permute-start.4 = (bf16[8,1,16,384]{3,2,0,1:T(8,128)(2,1)S(1)}, bf16[8,1,16,384]{3,2,0,1:T(8,128)(2,1)S(1)}, u32[]{:S(2)}, u32[]{:S(2)}) collective-permute-start(bf16[8,1,16,384]{3,2,0,1:T(8,128)(2,1)S(1)} %bitcast.81), channel_id=1, source_target_pairs={{0,4},{2,6},{4,0},{6,2},{1,5},{3,7},{5,1},{7,3},{8,12},{10,14},{12... | collective-permute-start | bytes 294920 | tf_op jit(solution)/shard_map/ppermute | solution.py:303
  77.4 8.8 %collective-permute-start.6 = (bf16[512,384]{1,0:T(8,128)(2,1)S(1)}, bf16[512,384]{1,0:T(8,128)(2,1)S(1)}, u32[]{:S(2)}, u32[]{:S(2)}) collective-permute-start(bf16[512,384]{1,0:T(8,128)(2,1)S(1)} %bitcast.72), channel_id=1, source_target_pairs={{0,1},{1,0},{2,3},{3,2},{4,5},{5,4},{6,7},{7,6},{8,9},{9,8},{10,11... | collective-permute-start | bytes 1179656 | tf_op jit(solution)/shard_map/ppermute | solution.py:29
  90.1 23.4 %copy-start.1 = (bf16[512,384]{1,0:T(8,128)(2,1)}, bf16[512,384]{1,0:T(8,128)(2,1)S(1)}, u32[]{:S(2)}) copy-start(bf16[512,384]{1,0:T(8,128)(2,1)S(1)} %get-tuple-element.32.weight_own) | copy-start | bytes 1179652
  90.1 6.9 %collective-permute-start.7 = (bf16[192,384]{1,0:T(8,128)(2,1)S(1)}, bf16[192,384]{1,0:T(8,128)(2,1)}, u32[]{:S(2)}, u32[]{:S(2)}) collective-permute-start(bf16[192,384]{1,0:T(8,128)(2,1)S(1)} %get-tuple-element.33), channel_id=1, source_target_pairs={{0,64},{64,0},{128,192},{192,128},{1,65},{65,1},{129,193},{193,129... | collective-permute-start | bytes 442376 | tf_op jit(solution)/shard_map/ppermute | solution.py:37
  92.8 16.8 %collective-permute-start.13 = (f32[512,384]{1,0:T(8,128)}, f32[512,384]{1,0:T(8,128)}, u32[]{:S(2)}, u32[]{:S(2)}) collective-permute-start(f32[512,384]{1,0:T(8,128)} %bitcast.23), channel_id=1, source_target_pairs={{0,1},{1,0},{2,3},{3,2},{4,5},{5,4},{6,7},{7,6},{8,9},{9,8},{10,11... | collective-permute-start | bytes 2359304 | tf_op jit(solution)/shard_map/ppermute | solution.py:29
  95.0 6.5 %collective-permute-start.9 = (bf16[192,384]{1,0:T(8,128)(2,1)S(1)}, bf16[192,384]{1,0:T(8,128)(2,1)S(1)}, u32[]{:S(2)}, u32[]{:S(2)}) collective-permute-start(bf16[192,384]{1,0:T(8,128)(2,1)S(1)} %get-tuple-element.34), channel_id=1, source_target_pairs={{0,192},{64,128},{128,64},{192,0},{1,193},{65,129},{129,65},{193,1... | collective-permute-start | bytes 442376 | tf_op jit(solution)/shard_map/ppermute | solution.py:37
  97.9 7.4 %collective-permute-start.8 = (bf16[192,384]{1,0:T(8,128)(2,1)S(1)}, bf16[192,384]{1,0:T(8,128)(2,1)S(1)}, u32[]{:S(2)}, u32[]{:S(2)}) collective-permute-start(bf16[192,384]{1,0:T(8,128)(2,1)S(1)} %add_convert_fusion.3.first), channel_id=1, source_target_pairs={{0,192},{64,128},{128,64},{192,0},{1,193},{65,129},{129,65},{193,1... | collective-permute-start | bytes 442376 | tf_op jit(solution)/shard_map/ppermute | solution.py:37
  101.5 4.1 %collective-permute-start.10 = (bf16[192,384]{1,0:T(8,128)(2,1)S(1)}, bf16[192,384]{1,0:T(8,128)(2,1)S(1)}, u32[]{:S(2)}, u32[]{:S(2)}) collective-permute-start(bf16[192,384]{1,0:T(8,128)(2,1)S(1)} %add_convert_fusion.2.second), channel_id=1, source_target_pairs={{0,64},{64,0},{128,192},{192,128},{1,65},{65,1},{129,193},{193,129... | collective-permute-start | bytes 442376 | tf_op jit(solution)/shard_map/ppermute | solution.py:37
  107.0 49.5 %copy-start.6 = (f32[384,128]{1,0:T(8,128)}, f32[384,128]{1,0:T(8,128)S(1)}, u32[]{:S(2)}) copy-start(f32[384,128]{1,0:T(8,128)S(1)} %get-tuple-element.46.stor_now) | copy-start | bytes 589828
  107.1 4.3 %collective-permute-start.14 = (f32[384]{0:T(512)S(1)}, f32[384]{0:T(512)S(1)}, u32[]{:S(2)}, u32[]{:S(2)}) collective-permute-start(f32[384]{0:T(512)S(1)} %sub.94), channel_id=1, source_target_pairs={{0,1},{1,0},{2,3},{3,2},{4,5},{5,4},{6,7},{7,6},{8,9},{9,8},{10,11... | collective-permute-start | bytes 4616 | tf_op jit(solution)/shard_map/ppermute | solution.py:29
  110.8 1.8 collective-permute-start.11
  111.0 2.0 %collective-permute-start.12 = (bf16[384,384]{1,0:T(8,128)(2,1)S(1)}, bf16[384,384]{1,0:T(8,128)(2,1)S(1)}, u32[]{:S(2)}, u32[]{:S(2)}) collective-permute-start(bf16[384,384]{1,0:T(8,128)(2,1)S(1)} %get-tuple-element.39), channel_id=1, source_target_pairs={{0,1},{1,0},{2,3},{3,2},{4,5},{5,4},{6,7},{7,6},{8,9},{9,8},{10,11... | collective-permute-start | bytes 884744 | tf_op jit(solution)/shard_map/ppermute | solution.py:29
  113.9 42.6 %copy-start.21 = (f32[128]{0:T(128)S(1)}, f32[128]{0:T(128)}, u32[]{:S(2)}) copy-start(f32[128]{0:T(128)} %param.29) | copy-start | bytes 1540
  114.9 19.4 %all-to-all-start.2 = ((bf16[32,56,128]{2,1,0:T(8,128)(2,1)}), bf16[32,56,128]{2,1,0:T(8,128)(2,1)S(1)}, u32[]{:S(2)}, u32[]{:S(2)}) async-start(bf16[32,56,128]{2,1,0:T(8,128)(2,1)} %pad_maximum_fusion), calls=%async_computation.2 | async-start | bytes 917504 | tf_op jit(solution)/shard_map/all_to_all | solution.py:473
  153.6 4.7 %collective-permute-start.15 = (bf16[512,384]{1,0:T(8,128)(2,1)S(1)}, bf16[512,384]{1,0:T(8,128)(2,1)S(1)}, u32[]{:S(2)}, u32[]{:S(2)}) collective-permute-start(bf16[512,384]{1,0:T(8,128)(2,1)S(1)} %bitcast.67), channel_id=1, source_target_pairs={{0,1},{1,0},{2,3},{3,2},{4,5},{5,4},{6,7},{7,6},{8,9},{9,8},{10,11... | collective-permute-start | bytes 1179656 | tf_op jit(solution)/shard_map/ppermute | solution.py:29
  160.1 18.0 %copy-start.17 = (bf16[512,384]{1,0:T(8,128)(2,1)S(1)}, bf16[512,384]{1,0:T(8,128)(2,1)}, u32[]{:S(2)}) copy-start(bf16[512,384]{1,0:T(8,128)(2,1)} %copy-done.16) | copy-start | bytes 1179652
  160.1 5.5 %collective-permute-start.16 = (bf16[192,384]{1,0:T(8,128)(2,1)S(1)}, bf16[192,384]{1,0:T(8,128)(2,1)S(1)}, u32[]{:S(2)}, u32[]{:S(2)}) collective-permute-start(bf16[192,384]{1,0:T(8,128)(2,1)S(1)} %get-tuple-element.43), channel_id=1, source_target_pairs={{0,64},{64,0},{128,192},{192,128},{1,65},{65,1},{129,193},{193,129... | collective-permute-start | bytes 442376 | tf_op jit(solution)/shard_map/ppermute | solution.py:37
  162.0 6.3 %collective-permute-start.18 = (bf16[192,384]{1,0:T(8,128)(2,1)S(1)}, bf16[192,384]{1,0:T(8,128)(2,1)S(1)}, u32[]{:S(2)}, u32[]{:S(2)}) collective-permute-start(bf16[192,384]{1,0:T(8,128)(2,1)S(1)} %get-tuple-element.44), channel_id=1, source_target_pairs={{0,192},{64,128},{128,64},{192,0},{1,193},{65,129},{129,65},{193,1... | collective-permute-start | bytes 442376 | tf_op jit(solution)/shard_map/ppermute | solution.py:37
  165.6 5.8 %collective-permute-start.17 = (bf16[192,384]{1,0:T(8,128)(2,1)S(1)}, bf16[192,384]{1,0:T(8,128)(2,1)S(1)}, u32[]{:S(2)}, u32[]{:S(2)}) collective-permute-start(bf16[192,384]{1,0:T(8,128)(2,1)S(1)} %add_convert_fusion.1.first), channel_id=1, source_target_pairs={{0,192},{64,128},{128,64},{192,0},{1,193},{65,129},{129,65},{193,1... | collective-permute-start | bytes 442376 | tf_op jit(solution)/shard_map/ppermute | solution.py:37
  168.3 4.4 %collective-permute-start.19 = (bf16[192,384]{1,0:T(8,128)(2,1)S(1)}, bf16[192,384]{1,0:T(8,128)(2,1)S(1)}, u32[]{:S(2)}, u32[]{:S(2)}) collective-permute-start(bf16[192,384]{1,0:T(8,128)(2,1)S(1)} %add_convert_fusion.second), channel_id=1, source_target_pairs={{0,64},{64,0},{128,192},{192,128},{1,65},{65,1},{129,193},{193,129... | collective-permute-start | bytes 442376 | tf_op jit(solution)/shard_map/ppermute | solution.py:37
  174.3 3.1 %collective-permute-start.21 = (f32[384]{0:T(512)S(1)}, f32[384]{0:T(512)S(1)}, u32[]{:S(2)}, u32[]{:S(2)}) collective-permute-start(f32[384]{0:T(512)S(1)} %sub.99), channel_id=1, source_target_pairs={{0,1},{1,0},{2,3},{3,2},{4,5},{5,4},{6,7},{7,6},{8,9},{9,8},{10,11... | collective-permute-start | bytes 4616 | tf_op jit(solution)/shard_map/ppermute | solution.py:29
  176.5 1.6 collective-permute-start.20
  179.9 20.1 %all-to-all-start.4 = ((bf16[32,56,128]{2,1,0:T(8,128)(2,1)}), bf16[32,56,128]{2,1,0:T(8,128)(2,1)}, u32[]{:S(2)}, u32[]{:S(2)}) async-start(bf16[32,56,128]{2,1,0:T(8,128)(2,1)} %pad_maximum_fusion.1), calls=%async_computation.4 | async-start | bytes 917504 | tf_op jit(solution)/shard_map/all_to_all | solution.py:473
  (16 other events, 113.1 us)

commit v8 on v7

--- a/solution.py
+++ b/solution.py
@@ -19,10 +19,6 @@
 VMEM_LIMIT = 16 * 1024 * 1024
 AREAS = ("z", "x", "core")
 CHIPS = ("z", "x")
-
-
-def rounded(x):
-    return lax.reduce_precision(x, 8, 7)
 
 
 def swapped(x):
@@ -112,7 +108,7 @@
     half_lines, row_count = dual_own.shape
     gen_count = column.shape[0]
     units = gen_count + stor_own.shape[1]
-    weight = pltpu.VMEM((half_lines, units), jnp.bfloat16)
+    weight = pltpu.HBM((half_lines, units), jnp.bfloat16)
     in_vmem = pl.BlockSpec(memory_space=pltpu.VMEM)
     share_len = columns.shape[1] // (Z * X * CORES)
     own, other, first, second = pl.pallas_call(
@@ -176,6 +172,45 @@
         name="duals",
         compiler_params=pltpu.CompilerParams(vmem_limit_bytes=VMEM_LIMIT),
     )(*in_fast(received), dual, limit)
+
+
+def flow_body(bar, bar_far, weight_own, weight_far, load_flow, balance, sent):
+    flow = (
+        lax.dot_general(
+            weight_own[...], bar[...], CONTRACT_MINOR, preferred_element_type=jnp.float32
+        )
+        + lax.dot_general(
+            weight_far[...], bar_far[...], CONTRACT_MINOR, preferred_element_type=jnp.float32
+        )
+        - load_flow[...]
+    )
+    chips, rows, lanes = sent.shape
+    share_len = flow.shape[0] // chips
+    strips = flow.shape[1] // lanes
+    for i in range(strips):
+        strip = flow[:, i * lanes : (i + 1) * lanes].astype(jnp.bfloat16)
+        sent[:, i * share_len : (i + 1) * share_len] = strip.reshape(chips, share_len, lanes)
+    level = balance[...]
+    high = level.astype(jnp.bfloat16).astype(jnp.float32)
+    low = level - high
+    tail = [x[:, i * lanes : (i + 1) * lanes] for x in (high, low) for i in range(strips)]
+    tail.append(jnp.zeros((rows - strips * share_len - 2 * strips, lanes), jnp.float32))
+    tail = jnp.concatenate(tail, axis=0).astype(jnp.bfloat16)
+    sent[:, strips * share_len :] = jnp.broadcast_to(tail[None], (chips, *tail.shape))
+
+
+def flows_to_send(bar, bar_far, weight_own, weight_far, load_flow, balance):
+    lanes, chips = 128, Z * X
+    rows = load_flow.size // (chips * lanes) + 8
+    in_vmem = pl.BlockSpec(memory_space=pltpu.VMEM)
+    return pl.pallas_call(
+        flow_body,
+        out_shape=pltpu.HBM((chips, rows, lanes), jnp.bfloat16),
+        in_specs=[in_vmem] * 6,
+        out_specs=in_vmem,
+        name="flows",
+        compiler_params=pltpu.CompilerParams(vmem_limit_bytes=VMEM_LIMIT),
+    )(*in_fast(bar, bar_far), *in_main(weight_own, weight_far, load_flow), balance[None, :])
 
 
 def base_body(level, gen_quad, gen_lin, stor_quad, back, gen_now, stor_now, *refs):
@@ -268,8 +303,8 @@
         update_body,
         out_shape=(
             pltpu.VMEM((row_count, gen_count + stor_count), jnp.bfloat16),
-            pltpu.VMEM((row_count, gen_count), jnp.float32),
-            pltpu.VMEM((row_count, stor_count), jnp.float32),
+            pltpu.HBM((row_count, gen_count), jnp.float32),
+            pltpu.HBM((row_count, stor_count), jnp.float32),
             pltpu.VMEM((8, row_count), jnp.float32),
         ),
         in_specs=[in_vmem] * len(operands),
@@ -445,31 +480,11 @@
         )
         balance = total[0] - load_total
         stor_bar = 2.0 * stor_next - stor_now
-        flow_part = (
-            lax.dot_general(weight_own, bar_low, CONTRACT_MINOR, preferred_element_type=jnp.float32)
-            + lax.dot_general(
-                weight_far, swapped(bar_low), CONTRACT_MINOR, preferred_element_type=jnp.float32
-            )
-            - load_flow
-        )
         balance = balance + swapped(balance)
-        high = rounded(balance)
-        lanes = 128
-        strips = row_count // lanes
-        tail = jnp.concatenate(
-            [
-                high.reshape(strips, lanes),
-                (balance - high).reshape(strips, lanes),
-                jnp.zeros((8 - 2 * strips, lanes), jnp.float32),
-            ],
-            axis=0,
-        )
-        body = flow_part.reshape(chip_count, share_len, row_count)
-        sent = jnp.concatenate(
-            [body[:, :, i * lanes : (i + 1) * lanes] for i in range(strips)]
-            + [jnp.broadcast_to(tail[None], (chip_count, 8, lanes))],
-            axis=1,
-        ).astype(jnp.bfloat16)
+        strips = row_count // 128
+        sent = flows_to_send(
+            bar_low, swapped(bar_low), weight_own, weight_far, load_flow, balance
+        )
         received = lax.all_to_all(sent, CHIPS, 0, 0, tiled=True)
         tail, dual_flow, *spread = dual_updated(received, dual_flow, limit, iteration == 0)
         balance = (tail[:strips] + tail[strips : 2 * strips]).reshape(row_count)

time: 203 us -> 207 us (1.020)
  Pallas kernels: 13.3 us -> 19.4 us
  waiting for transfers between devices: 63.2 us -> 67.4 us
  starting transfers between devices: 51.8 us -> 49.4 us
    pallas_call x0 -> x2, Pallas kernels: none -> 5.66 us  [flows_to_send(): pl.pallas_call(flow_body, out_shape=pltpu.HBM((chips, rows, lanes), jnp.b...]
    ppermute x8, waiting for transfers between devices: 5.74 us -> 10.4 us  [from_side(): return lax.ppermute(x, 'lines', [(i, i ^ step) for i in range(4)])]
    ppermute x8, starting transfers between devices: 10.9 us -> 7.08 us  [from_side(): return lax.ppermute(x, 'lines', [(i, i ^ step) for i in range(4)])]
  transfers between devices with their start and end apart: 25 -> 25, of which waited for: 17 -> 13; matrix products, arithmetic and copies ran while one was open for 11% -> 10% of each run, Pallas kernels for 2% -> 2%
where the time goes in v8:
time: 207 us; the launch traced here: 206 us
  waiting for transfers between devices  67.4 us (33%)
  starting transfers between devices  49.4 us (24%)
  blocking collectives  39.7 us (19%)
  Pallas kernels  19.4 us (9%)
  matrix products  14 us (7%)
  other arithmetic  9.21 us (4%)
  local copies, waits for them, and re-layouts  5.45 us (3%)
    all_to_all x2, waiting for transfers between devices, shards(): received = lax.all_to_all(sent, CHIPS, 0, 0, tiled=True)  26.4 us
    ppermute x3, waiting for transfers between devices, doubled(): other = lax.ppermute(x, axis, [(i, i ^ step) for i in range(size)])  25.1 us
    all_to_all x1, blocking collectives, shards(): lax.all_to_all(slot_bus.reshape(area_count, slots), AREAS, 0, 0, tiled=True)  22.2 us
    all_to_all x1, blocking collectives, gathered_duals(): lax.all_to_all(sent, CHIPS, 0, 0, tiled=True).reshape(-1, sent.shape[2])  17.5 us
    ppermute x8, starting transfers between devices, swapped(): return lax.ppermute(x, 'core', [(0, 1), (1, 0)])  16.6 us
    ppermute x8, waiting for transfers between devices, from_side(): return lax.ppermute(x, 'lines', [(i, i ^ step) for i in range(4)])  10.4 us
    ppermute x3, starting transfers between devices, doubled(): other = lax.ppermute(x, axis, [(i, i ^ step) for i in range(size)])  8.42 us
    all_to_all x2, starting transfers between devices, shards(): received = lax.all_to_all(sent, CHIPS, 0, 0, tiled=True)  7.79 us
  transfers between devices with their start and end apart: 25, of which 13 were waited for; matrix products, arithmetic and copies ran while one was open for 10% of the time, Pallas kernels for 2%

profile of v8, /device:TPU:1, one launch (start us, length us, event | category | flops | bytes accessed | tf_op | source)
XLA Modules:
  0.0 205.6 jit_solution(8105641827947353418)
XLA Ops:
  1.9 22.2 %all_to_all.32 = s32[64,1,8]{2,1,0:T(1,128)S(1)} all-to-all(s32[64,1,8]{2,1,0:T(1,128)S(1)} %bitcast.63), channel_id=1, replica_groups=mesh['lines'=4,'z'=8,'x'=4,'core'=2] {'z','x','core'}, dimensions={0} | all-to-all | bytes 4096 | tf_op jit(solution)/shard_map/all_to_all | solution.py:416
  25.5 2.5 %fusion.2 = bf16[64,8,1024]{2,1,0:T(8,128)(2,1)} fusion(bf16[1024,1280]{1,0:T(8,128)(2,1)S(1)} %copy-done, s32[512]{0:T(512)S(1)} %eq.148), kind=kOutput, calls=%fused_computation.4 | convolution fusion | flops 1343356928 | bytes 3672064 | tf_op jit(solution)/shard_map/dot_general | solution.py:424
  28.0 5.6 %all-to-all-start.1 = ((bf16[64,8,1024]{2,1,0:T(8,128)(2,1)}), bf16[64,8,1024]{2,1,0:T(8,128)(2,1)}, u32[]{:S(2)}, u32[]{:S(2)}) async-start(bf16[64,8,1024]{2,1,0:T(8,128)(2,1)} %fusion.2), calls=%async_computation.1 | async-start | bytes 2097152 | tf_op jit(solution)/shard_map/all_to_all | solution.py:427
  33.6 5.6 %collective-permute-start = (bf16[1,1,1,16,384]{4,3,2,1,0:T(8,128)(2,1)S(1)}, bf16[1,1,1,16,384]{4,3,2,1,0:T(8,128)(2,1)S(1)}, u32[]{:S(2)}, u32[]{:S(2)}) collective-permute-start(bf16[1,1,1,16,384]{4,3,2,1,0:T(8,128)(2,1)S(1)} %get-tuple-element.64), channel_id=1, source_target_pairs={{0,32},{8,40},{16,48},{24,56},{32,0},{40,8},{48,16},{56,24},{1,33}... | collective-permute-start | bytes 36872 | tf_op jit(solution)/shard_map/ppermute | solution.py:323
  39.2 21.9 %collective-permute-done = bf16[1,1,1,16,384]{4,3,2,1,0:T(8,128)(2,1)S(1)} collective-permute-done((bf16[1,1,1,16,384]{4,3,2,1,0:T(8,128)(2,1)S(1)}, bf16[1,1,1,16,384]{4,3,2,1,0:T(8,128)(2,1)S(1)}, u32[]{:S(2)}, u32[]{:S(2)}) %collective-permute-start) | collective-permute-done | bytes 12320 | tf_op jit(solution)/shard_map/ppermute | solution.py:323
  61.7 3.0 %collective-permute-done.1 = bf16[2,1,1,16,384]{4,3,2,1,0:T(8,128)(2,1)S(1)} collective-permute-done((bf16[2,1,1,16,384]{4,3,2,1,0:T(8,128)(2,1)S(1)}, bf16[2,1,1,16,384]{4,3,2,1,0:T(8,128)(2,1)S(1)}, u32[]{:S(2)}, u32[]{:S(2)}) %collective-permute-start.1) | collective-permute-done | bytes 24608 | tf_op jit(solution)/shard_map/ppermute | solution.py:323
  64.7 2.2 %collective-permute-start.2 = (bf16[2,2,1,16,384]{4,3,2,1,0:T(8,128)(2,1)S(1)}, bf16[2,2,1,16,384]{4,3,2,1,0:T(8,128)(2,1)S(1)}, u32[]{:S(2)}, u32[]{:S(2)}) collective-permute-start(bf16[2,2,1,16,384]{4,3,2,1,0:T(8,128)(2,1)S(1)} %maximum_select_fusion.4), channel_id=1, source_target_pairs={{0,8},{8,0},{16,24},{24,16},{32,40},{40,32},{48,56},{56,48},{1,9},... | collective-permute-start | bytes 147464 | tf_op jit(solution)/shard_map/ppermute | solution.py:323
  70.1 2.8 %collective-permute-start.4 = (bf16[8,1,16,384]{3,2,0,1:T(8,128)(2,1)S(1)}, bf16[8,1,16,384]{3,2,0,1:T(8,128)(2,1)S(1)}, u32[]{:S(2)}, u32[]{:S(2)}) collective-permute-start(bf16[8,1,16,384]{3,2,0,1:T(8,128)(2,1)S(1)} %bitcast.60), channel_id=1, source_target_pairs={{0,4},{2,6},{4,0},{6,2},{1,5},{3,7},{5,1},{7,3},{8,12},{10,14},{12... | collective-permute-start | bytes 294920 | tf_op jit(solution)/shard_map/ppermute | solution.py:338
  73.2 2.0 collective-permute-done.4
  75.2 2.3 %collective-permute-done.5 = bf16[8,1,16,384]{3,2,0,1:T(8,128)(2,1)S(1)} collective-permute-done((bf16[8,1,16,384]{3,2,0,1:T(8,128)(2,1)S(1)}, bf16[8,1,16,384]{3,2,0,1:T(8,128)(2,1)S(1)}, u32[]{:S(2)}, u32[]{:S(2)}) %collective-permute-start.5) | collective-permute-done | bytes 98336 | tf_op jit(solution)/shard_map/ppermute | solution.py:338
  77.7 6.0 %collective-permute-start.6 = (bf16[512,384]{1,0:T(8,128)(2,1)S(1)}, bf16[512,384]{1,0:T(8,128)(2,1)S(1)}, u32[]{:S(2)}, u32[]{:S(2)}) collective-permute-start(bf16[512,384]{1,0:T(8,128)(2,1)S(1)} %bitcast.54), channel_id=1, source_target_pairs={{0,1},{1,0},{2,3},{3,2},{4,5},{5,4},{6,7},{7,6},{8,9},{9,8},{10,11... | collective-permute-start | bytes 1179656 | tf_op jit(solution)/shard_map/ppermute | solution.py:25
  83.7 2.7 %fusion.7 = f32[1024,384]{1,0:T(8,128)} fusion(bf16[1024,1280]{1,0:T(8,128)(2,1)S(1)} %copy-done, f32[384,1280]{1,0:T(8,128)S(1)} %copy-done.4), kind=kOutput, calls=%fused_computation.12 | convolution fusion | flops 1007124480 | bytes 6160384 | tf_op jit(solution)/shard_map/dot_general | solution.py:446
  87.2 3.6 %weights.1 = (bf16[512,384]{1,0:T(8,128)(2,1)}, bf16[512,384]{1,0:T(8,128)(2,1)}, bf16[192,384]{1,0:T(8,128)(2,1)S(1)}, bf16[192,384]{1,0:T(8,128)(2,1)S(1)}) custom-call(s32[1]{0:T(128)} %bitcast.core, bf16[512,1024]{1,0:T(8,128)(2,1)} %bitcast.3.columns, s32[1,256]{1,0:T(1,128)S(1)} %bitcast.52, bf16[512,128]{1,0:T(8,128)(2,1)} %bitcast.58, ...), custom_call_target="tpu_custom_call" | custom-call | tf_op jit(solution)/shard_map/weights/pallas_call | solution.py:114
  90.8 2.7 %collective-permute-start.9 = (bf16[192,384]{1,0:T(8,128)(2,1)S(1)}, bf16[192,384]{1,0:T(8,128)(2,1)}, u32[]{:S(2)}, u32[]{:S(2)}) collective-permute-start(bf16[192,384]{1,0:T(8,128)(2,1)S(1)} %get-tuple-element.33), channel_id=1, source_target_pairs={{0,192},{64,128},{128,64},{192,0},{1,193},{65,129},{129,65},{193,1... | collective-permute-start | bytes 442376 | tf_op jit(solution)/shard_map/ppermute | solution.py:33
  99.6 2.7 %collective-permute-done.7 = bf16[192,384]{1,0:T(8,128)(2,1)S(1)} collective-permute-done((bf16[192,384]{1,0:T(8,128)(2,1)S(1)}, bf16[192,384]{1,0:T(8,128)(2,1)S(1)}, u32[]{:S(2)}, u32[]{:S(2)}) %collective-permute-start.7) | collective-permute-done | bytes 147488 | tf_op jit(solution)/shard_map/ppermute | solution.py:33
  102.4 2.3 %fusion.13.back = f32[384,128]{1,0:T(8,128)} fusion(f32[384,128]{1,0:T(8,128)} %param.33, s32[384]{0:T(512)S(1)} %add_select_fusion), kind=kOutput, calls=%fused_computation.19 | convolution fusion | flops 227082240 | bytes 394752 | tf_op jit(solution)/shard_map/dot_general | solution.py:365
  108.0 1.9 update.2
  109.8 2.5 %collective-permute-start.11 = (bf16[384,384]{1,0:T(8,128)(2,1)S(1)}, bf16[384,384]{1,0:T(8,128)(2,1)S(1)}, u32[]{:S(2)}, u32[]{:S(2)}) collective-permute-start(bf16[384,384]{1,0:T(8,128)(2,1)S(1)} %get-tuple-element.38.bar), channel_id=1, source_target_pairs={{0,1},{1,0},{2,3},{3,2},{4,5},{5,4},{6,7},{7,6},{8,9},{9,8},{10,11... | collective-permute-start | bytes 884744 | tf_op jit(solution)/shard_map/ppermute | solution.py:25
  112.5 2.1 %bitcast_add_fusion.load_flow = f32[512,384]{1,0:T(8,128)} fusion(f32[512,384]{1,0:T(8,128)} %collective-permute-done.13, f32[32,1,16,384]{3,2,1,0:T(8,128)S(1)} %copy-done.2), kind=kLoop, calls=%fused_computation.14 | loop fusion | flops 196608 | bytes 2359296 | tf_op jit(solution)/shard_map/add | solution.py:450
  115.4 2.8 %flows.2 = bf16[32,56,128]{2,1,0:T(8,128)(2,1)} custom-call(bf16[384,384]{1,0:T(8,128)(2,1)S(1)} %get-tuple-element.38.bar, bf16[384,384]{1,0:T(8,128)(2,1)S(1)} %collective-permute-done.11.bar_far, bf16[512,384]{1,0:T(8,128)(2,1)} %get-tuple-element.39.weight_own, bf16[512,384]{1,0:T(8,128)(2,1)} %copy-done.7, f32[512,384]{1,0:T(8,128)} %bitcast_add_fusion.load_flow, ...), custom_call_target="tpu_custom_call" | custom-call | tf_op jit(solution)/shard_map/flows/pallas_call | solution.py:206
  118.3 3.9 %all-to-all-start.2 = ((bf16[32,56,128]{2,1,0:T(8,128)(2,1)}), bf16[32,56,128]{2,1,0:T(8,128)(2,1)S(1)}, u32[]{:S(2)}, u32[]{:S(2)}) async-start(bf16[32,56,128]{2,1,0:T(8,128)(2,1)} %flows.2), calls=%async_computation.2 | async-start | bytes 917504 | tf_op jit(solution)/shard_map/all_to_all | solution.py:488
  124.5 13.1 %all-to-all-done.2.received = bf16[32,56,128]{2,1,0:T(8,128)(2,1)S(1)} async-done(((bf16[32,56,128]{2,1,0:T(8,128)(2,1)}), bf16[32,56,128]{2,1,0:T(8,128)(2,1)S(1)}, u32[]{:S(2)}, u32[]{:S(2)}) %all-to-all-start.2) | async-done | bytes 458784 | tf_op jit(solution)/shard_map/all_to_all | solution.py:488
  138.5 17.5 %all_to_all.33 = bf16[32,16,384]{2,1,0:T(8,128)(2,1)S(1)} all-to-all(bf16[32,16,384]{2,1,0:T(8,128)(2,1)} %get-tuple-element.42), channel_id=1, replica_groups=mesh['lines'=4,'z'=8,'x'=4,'core'=2] {'z','x'}, dimensions={0} | all-to-all | bytes 786432 | tf_op jit(solution)/shard_map/all_to_all | solution.py:318
  156.0 3.4 %collective-permute-start.15 = (bf16[512,384]{1,0:T(8,128)(2,1)S(1)}, bf16[512,384]{1,0:T(8,128)(2,1)S(1)}, u32[]{:S(2)}, u32[]{:S(2)}) collective-permute-start(bf16[512,384]{1,0:T(8,128)(2,1)S(1)} %bitcast.49), channel_id=1, source_target_pairs={{0,1},{1,0},{2,3},{3,2},{4,5},{5,4},{6,7},{7,6},{8,9},{9,8},{10,11... | collective-permute-start | bytes 1179656 | tf_op jit(solution)/shard_map/ppermute | solution.py:25
  165.9 3.8 %collective-permute-done.18 = bf16[192,384]{1,0:T(8,128)(2,1)S(1)} collective-permute-done((bf16[192,384]{1,0:T(8,128)(2,1)S(1)}, bf16[192,384]{1,0:T(8,128)(2,1)S(1)}, u32[]{:S(2)}, u32[]{:S(2)}) %collective-permute-start.18) | collective-permute-done | bytes 147488 | tf_op jit(solution)/shard_map/ppermute | solution.py:33
  174.4 2.2 %collective-permute-done.17.first_far = bf16[192,384]{1,0:T(8,128)(2,1)S(1)} collective-permute-done((bf16[192,384]{1,0:T(8,128)(2,1)S(1)}, bf16[192,384]{1,0:T(8,128)(2,1)S(1)}, u32[]{:S(2)}, u32[]{:S(2)}) %collective-permute-start.17) | collective-permute-done | bytes 147488 | tf_op jit(solution)/shard_map/ppermute | solution.py:33
  176.6 1.9 update.3
  178.5 2.3 %collective-permute-start.20 = (bf16[384,384]{1,0:T(8,128)(2,1)S(1)}, bf16[384,384]{1,0:T(8,128)(2,1)S(1)}, u32[]{:S(2)}, u32[]{:S(2)}) collective-permute-start(bf16[384,384]{1,0:T(8,128)(2,1)S(1)} %get-tuple-element.54.bar), channel_id=1, source_target_pairs={{0,1},{1,0},{2,3},{3,2},{4,5},{5,4},{6,7},{7,6},{8,9},{9,8},{10,11... | collective-permute-start | bytes 884744 | tf_op jit(solution)/shard_map/ppermute | solution.py:25
  182.1 2.8 %flows.3 = bf16[32,56,128]{2,1,0:T(8,128)(2,1)} custom-call(bf16[384,384]{1,0:T(8,128)(2,1)S(1)} %get-tuple-element.54.bar, bf16[384,384]{1,0:T(8,128)(2,1)S(1)} %collective-permute-done.20.bar_far, bf16[512,384]{1,0:T(8,128)(2,1)} %get-tuple-element.39.weight_own, bf16[512,384]{1,0:T(8,128)(2,1)} %copy-done.7, f32[512,384]{1,0:T(8,128)} %bitcast_add_fusion.load_flow, ...), custom_call_target="tpu_custom_call" | custom-call | tf_op jit(solution)/shard_map/flows/pallas_call | solution.py:206
  184.9 3.9 %all-to-all-start.4 = ((bf16[32,56,128]{2,1,0:T(8,128)(2,1)}), bf16[32,56,128]{2,1,0:T(8,128)(2,1)S(1)}, u32[]{:S(2)}, u32[]{:S(2)}) async-start(bf16[32,56,128]{2,1,0:T(8,128)(2,1)} %flows.3), calls=%async_computation.4 | async-start | bytes 917504 | tf_op jit(solution)/shard_map/all_to_all | solution.py:488
  188.8 2.3 %fusion.36 = f32[384,128]{1,0:T(8,128)} fusion(f32[384,128]{1,0:T(8,128)} %copy-done.16, s32[384]{0:T(512)S(1)} %add_select_fusion, f32[384,128]{1,0:T(8,128)S(1)} %copy-done.11, f32[384,128]{1,0:T(8,128)S(1)} %copy-done.14, f32[128]{0:T(128)S(1)} %get-tuple-element.68, f32[128]{0:T(128)S(1)} %get-tuple-element.67, pred[384]{0:T(512)(128)(4,1)S(1)} %fusion.52), kind=kOutput, calls=%fused_computation.60 | convolution fusion | flops 227622912 | bytes 789376 | tf_op jit(solution)/shard_map/dot_general | solution.py:365
  191.1 13.2 %all-to-all-done.4.received = bf16[32,56,128]{2,1,0:T(8,128)(2,1)S(1)} async-done(((bf16[32,56,128]{2,1,0:T(8,128)(2,1)}), bf16[32,56,128]{2,1,0:T(8,128)(2,1)S(1)}, u32[]{:S(2)}, u32[]{:S(2)}) %all-to-all-start.4) | async-done | bytes 458784 | tf_op jit(solution)/shard_map/all_to_all | solution.py:488
  (118 shorter events, 34.6 us)
Async XLA Ops:
  0.6 24.8 %copy-start = (bf16[1024,1280]{1,0:T(8,128)(2,1)S(1)}, bf16[1024,1280]{1,0:T(8,128)(2,1)}, u32[]{:S(2)}) copy-start(bf16[1024,1280]{1,0:T(8,128)(2,1)} %param.17) | copy-start | bytes 7864324
  25.5 41.5 %copy-start.13 = (s32[128]{0:T(128)S(1)}, s32[128]{0:T(128)}, u32[]{:S(2)}) copy-start(s32[128]{0:T(128)} %param.26) | copy-start | bytes 1540
  28.0 58.5 %all-to-all-start.1 = ((bf16[64,8,1024]{2,1,0:T(8,128)(2,1)}), bf16[64,8,1024]{2,1,0:T(8,128)(2,1)}, u32[]{:S(2)}, u32[]{:S(2)}) async-start(bf16[64,8,1024]{2,1,0:T(8,128)(2,1)} %fusion.2), calls=%async_computation.1 | async-start | bytes 2097152 | tf_op jit(solution)/shard_map/all_to_all | solution.py:427
  33.6 27.4 %collective-permute-start = (bf16[1,1,1,16,384]{4,3,2,1,0:T(8,128)(2,1)S(1)}, bf16[1,1,1,16,384]{4,3,2,1,0:T(8,128)(2,1)S(1)}, u32[]{:S(2)}, u32[]{:S(2)}) collective-permute-start(bf16[1,1,1,16,384]{4,3,2,1,0:T(8,128)(2,1)S(1)} %get-tuple-element.64), channel_id=1, source_target_pairs={{0,32},{8,40},{16,48},{24,56},{32,0},{40,8},{48,16},{56,24},{1,33}... | collective-permute-start | bytes 36872 | tf_op jit(solution)/shard_map/ppermute | solution.py:323
  61.0 3.7 %collective-permute-start.1 = (bf16[2,1,1,16,384]{4,3,2,1,0:T(8,128)(2,1)S(1)}, bf16[2,1,1,16,384]{4,3,2,1,0:T(8,128)(2,1)S(1)}, u32[]{:S(2)}, u32[]{:S(2)}) collective-permute-start(bf16[2,1,1,16,384]{4,3,2,1,0:T(8,128)(2,1)S(1)} %maximum_select_fusion.6), channel_id=1, source_target_pairs={{0,16},{8,24},{16,0},{24,8},{32,48},{40,56},{48,32},{56,40},{1,17}... | collective-permute-start | bytes 73736 | tf_op jit(solution)/shard_map/ppermute | solution.py:323
  64.7 3.7 %collective-permute-start.2 = (bf16[2,2,1,16,384]{4,3,2,1,0:T(8,128)(2,1)S(1)}, bf16[2,2,1,16,384]{4,3,2,1,0:T(8,128)(2,1)S(1)}, u32[]{:S(2)}, u32[]{:S(2)}) collective-permute-start(bf16[2,2,1,16,384]{4,3,2,1,0:T(8,128)(2,1)S(1)} %maximum_select_fusion.4), channel_id=1, source_target_pairs={{0,8},{8,0},{16,24},{24,16},{32,40},{40,32},{48,56},{56,48},{1,9},... | collective-permute-start | bytes 147464 | tf_op jit(solution)/shard_map/ppermute | solution.py:323
  68.2 15.6 %copy-start.4 = (f32[384,1280]{1,0:T(8,128)S(1)}, f32[384,1280]{1,0:T(8,128)}, u32[]{:S(2)}) copy-start(f32[384,1280]{1,0:T(8,128)} %param.18) | copy-start | bytes 5898244
  68.5 4.7 %collective-permute-start.3 = (bf16[8,1,16,384]{3,2,0,1:T(8,128)(2,1)S(1)}, bf16[8,1,16,384]{3,2,0,1:T(8,128)(2,1)S(1)}, u32[]{:S(2)}, u32[]{:S(2)}) collective-permute-start(bf16[8,1,16,384]{3,2,0,1:T(8,128)(2,1)S(1)} %bitcast.59), channel_id=1, source_target_pairs={{0,2},{2,0},{4,6},{6,4},{1,3},{3,1},{5,7},{7,5},{8,10},{10,8},{12,... | collective-permute-start | bytes 294920 | tf_op jit(solution)/shard_map/ppermute | solution.py:338
  70.1 5.1 %collective-permute-start.4 = (bf16[8,1,16,384]{3,2,0,1:T(8,128)(2,1)S(1)}, bf16[8,1,16,384]{3,2,0,1:T(8,128)(2,1)S(1)}, u32[]{:S(2)}, u32[]{:S(2)}) collective-permute-start(bf16[8,1,16,384]{3,2,0,1:T(8,128)(2,1)S(1)} %bitcast.60), channel_id=1, source_target_pairs={{0,4},{2,6},{4,0},{6,2},{1,5},{3,7},{5,1},{7,3},{8,12},{10,14},{12... | collective-permute-start | bytes 294920 | tf_op jit(solution)/shard_map/ppermute | solution.py:338
  72.8 4.7 %collective-permute-start.5 = (bf16[8,1,16,384]{3,2,0,1:T(8,128)(2,1)S(1)}, bf16[8,1,16,384]{3,2,0,1:T(8,128)(2,1)S(1)}, u32[]{:S(2)}, u32[]{:S(2)}) collective-permute-start(bf16[8,1,16,384]{3,2,0,1:T(8,128)(2,1)S(1)} %bitcast.61), channel_id=1, source_target_pairs={{0,6},{2,4},{4,2},{6,0},{1,7},{3,5},{5,3},{7,1},{8,14},{10,12},{12... | collective-permute-start | bytes 294920 | tf_op jit(solution)/shard_map/ppermute | solution.py:338
  77.7 8.8 %collective-permute-start.6 = (bf16[512,384]{1,0:T(8,128)(2,1)S(1)}, bf16[512,384]{1,0:T(8,128)(2,1)S(1)}, u32[]{:S(2)}, u32[]{:S(2)}) collective-permute-start(bf16[512,384]{1,0:T(8,128)(2,1)S(1)} %bitcast.54), channel_id=1, source_target_pairs={{0,1},{1,0},{2,3},{3,2},{4,5},{5,4},{6,7},{7,6},{8,9},{9,8},{10,11... | collective-permute-start | bytes 1179656 | tf_op jit(solution)/shard_map/ppermute | solution.py:25
  90.8 6.8 %collective-permute-start.9 = (bf16[192,384]{1,0:T(8,128)(2,1)S(1)}, bf16[192,384]{1,0:T(8,128)(2,1)}, u32[]{:S(2)}, u32[]{:S(2)}) collective-permute-start(bf16[192,384]{1,0:T(8,128)(2,1)S(1)} %get-tuple-element.33), channel_id=1, source_target_pairs={{0,192},{64,128},{128,64},{192,0},{1,193},{65,129},{129,65},{193,1... | collective-permute-start | bytes 442376 | tf_op jit(solution)/shard_map/ppermute | solution.py:33
  94.8 17.7 %collective-permute-start.13 = (f32[512,384]{1,0:T(8,128)}, f32[512,384]{1,0:T(8,128)}, u32[]{:S(2)}, u32[]{:S(2)}) collective-permute-start(f32[512,384]{1,0:T(8,128)} %bitcast.23), channel_id=1, source_target_pairs={{0,1},{1,0},{2,3},{3,2},{4,5},{5,4},{6,7},{7,6},{8,9},{9,8},{10,11... | collective-permute-start | bytes 2359304 | tf_op jit(solution)/shard_map/ppermute | solution.py:25
  97.0 15.5 %copy-start.2 = (f32[32,1,16,384]{3,2,1,0:T(8,128)S(1)}, f32[32,1,16,384]{3,2,1,0:T(8,128)}, u32[]{:S(2)}) copy-start(f32[32,1,16,384]{3,2,1,0:T(8,128)} %get-tuple-element.59) | copy-start | bytes 2359300
  97.0 5.3 %collective-permute-start.7 = (bf16[192,384]{1,0:T(8,128)(2,1)S(1)}, bf16[192,384]{1,0:T(8,128)(2,1)S(1)}, u32[]{:S(2)}, u32[]{:S(2)}) collective-permute-start(bf16[192,384]{1,0:T(8,128)(2,1)S(1)} %get-tuple-element.32), channel_id=1, source_target_pairs={{0,64},{64,0},{128,192},{192,128},{1,65},{65,1},{129,193},{193,129... | collective-permute-start | bytes 442376 | tf_op jit(solution)/shard_map/ppermute | solution.py:33
  98.6 9.4 %collective-permute-start.10 = (bf16[192,384]{1,0:T(8,128)(2,1)S(1)}, bf16[192,384]{1,0:T(8,128)(2,1)S(1)}, u32[]{:S(2)}, u32[]{:S(2)}) collective-permute-start(bf16[192,384]{1,0:T(8,128)(2,1)S(1)} %add_convert_fusion.2.second), channel_id=1, source_target_pairs={{0,64},{64,0},{128,192},{192,128},{1,65},{65,1},{129,193},{193,129... | collective-permute-start | bytes 442376 | tf_op jit(solution)/shard_map/ppermute | solution.py:33
  102.3 5.6 %collective-permute-start.8 = (bf16[192,384]{1,0:T(8,128)(2,1)S(1)}, bf16[192,384]{1,0:T(8,128)(2,1)S(1)}, u32[]{:S(2)}, u32[]{:S(2)}) collective-permute-start(bf16[192,384]{1,0:T(8,128)(2,1)S(1)} %add_convert_fusion.3.first), channel_id=1, source_target_pairs={{0,192},{64,128},{128,64},{192,0},{1,193},{65,129},{129,65},{193,1... | collective-permute-start | bytes 442376 | tf_op jit(solution)/shard_map/ppermute | solution.py:33
  106.1 8.5 %collective-permute-start.12 = (bf16[512,384]{1,0:T(8,128)(2,1)S(1)}, bf16[512,384]{1,0:T(8,128)(2,1)S(1)}, u32[]{:S(2)}, u32[]{:S(2)}) collective-permute-start(bf16[512,384]{1,0:T(8,128)(2,1)S(1)} %copy-done.10), channel_id=1, source_target_pairs={{0,1},{1,0},{2,3},{3,2},{4,5},{5,4},{6,7},{7,6},{8,9},{9,8},{10,11... | collective-permute-start | bytes 1179656 | tf_op jit(solution)/shard_map/ppermute | solution.py:25
  109.8 4.8 %collective-permute-start.11 = (bf16[384,384]{1,0:T(8,128)(2,1)S(1)}, bf16[384,384]{1,0:T(8,128)(2,1)S(1)}, u32[]{:S(2)}, u32[]{:S(2)}) collective-permute-start(bf16[384,384]{1,0:T(8,128)(2,1)S(1)} %get-tuple-element.38.bar), channel_id=1, source_target_pairs={{0,1},{1,0},{2,3},{3,2},{4,5},{5,4},{6,7},{7,6},{8,9},{9,8},{10,11... | collective-permute-start | bytes 884744 | tf_op jit(solution)/shard_map/ppermute | solution.py:25
  112.4 2.3 %collective-permute-start.14 = (f32[384]{0:T(512)S(1)}, f32[384]{0:T(512)S(1)}, u32[]{:S(2)}, u32[]{:S(2)}) collective-permute-start(f32[384]{0:T(512)S(1)} %sub.81), channel_id=1, source_target_pairs={{0,1},{1,0},{2,3},{3,2},{4,5},{5,4},{6,7},{7,6},{8,9},{9,8},{10,11... | collective-permute-start | bytes 4616 | tf_op jit(solution)/shard_map/ppermute | solution.py:25
  115.4 44.0 %copy-start.15 = (f32[128]{0:T(128)S(1)}, f32[128]{0:T(128)}, u32[]{:S(2)}) copy-start(f32[128]{0:T(128)} %param.29) | copy-start | bytes 1540
  115.4 44.0 %copy-start.8 = (f32[384,128]{1,0:T(8,128)S(1)}, f32[384,128]{1,0:T(8,128)}, u32[]{:S(2)}) copy-start(f32[384,128]{1,0:T(8,128)} %refs_1_.1) | copy-start | bytes 589828
  118.3 19.3 %all-to-all-start.2 = ((bf16[32,56,128]{2,1,0:T(8,128)(2,1)}), bf16[32,56,128]{2,1,0:T(8,128)(2,1)S(1)}, u32[]{:S(2)}, u32[]{:S(2)}) async-start(bf16[32,56,128]{2,1,0:T(8,128)(2,1)} %flows.2), calls=%async_computation.2 | async-start | bytes 917504 | tf_op jit(solution)/shard_map/all_to_all | solution.py:488
  156.0 5.2 %collective-permute-start.15 = (bf16[512,384]{1,0:T(8,128)(2,1)S(1)}, bf16[512,384]{1,0:T(8,128)(2,1)S(1)}, u32[]{:S(2)}, u32[]{:S(2)}) collective-permute-start(bf16[512,384]{1,0:T(8,128)(2,1)S(1)} %bitcast.49), channel_id=1, source_target_pairs={{0,1},{1,0},{2,3},{3,2},{4,5},{5,4},{6,7},{7,6},{8,9},{9,8},{10,11... | collective-permute-start | bytes 1179656 | tf_op jit(solution)/shard_map/ppermute | solution.py:25
  161.2 17.3 %copy-start.16 = (f32[384,128]{1,0:T(8,128)}, f32[384,128]{1,0:T(8,128)S(1)}, u32[]{:S(2)}) copy-start(f32[384,128]{1,0:T(8,128)S(1)} %fusion.34) | copy-start | bytes 589828
  163.0 6.7 %collective-permute-start.18 = (bf16[192,384]{1,0:T(8,128)(2,1)S(1)}, bf16[192,384]{1,0:T(8,128)(2,1)S(1)}, u32[]{:S(2)}, u32[]{:S(2)}) collective-permute-start(bf16[192,384]{1,0:T(8,128)(2,1)S(1)} %get-tuple-element.44), channel_id=1, source_target_pairs={{0,192},{64,128},{128,64},{192,0},{1,193},{65,129},{129,65},{193,1... | collective-permute-start | bytes 442376 | tf_op jit(solution)/shard_map/ppermute | solution.py:33
  165.9 5.1 %collective-permute-start.16 = (bf16[192,384]{1,0:T(8,128)(2,1)S(1)}, bf16[192,384]{1,0:T(8,128)(2,1)S(1)}, u32[]{:S(2)}, u32[]{:S(2)}) collective-permute-start(bf16[192,384]{1,0:T(8,128)(2,1)S(1)} %get-tuple-element.43), channel_id=1, source_target_pairs={{0,64},{64,0},{128,192},{192,128},{1,65},{65,1},{129,193},{193,129... | collective-permute-start | bytes 442376 | tf_op jit(solution)/shard_map/ppermute | solution.py:33
  169.7 4.6 %collective-permute-start.19 = (bf16[192,384]{1,0:T(8,128)(2,1)S(1)}, bf16[192,384]{1,0:T(8,128)(2,1)S(1)}, u32[]{:S(2)}, u32[]{:S(2)}) collective-permute-start(bf16[192,384]{1,0:T(8,128)(2,1)S(1)} %add_convert_fusion.second), channel_id=1, source_target_pairs={{0,64},{64,0},{128,192},{192,128},{1,65},{65,1},{129,193},{193,129... | collective-permute-start | bytes 442376 | tf_op jit(solution)/shard_map/ppermute | solution.py:33
  171.0 5.5 %collective-permute-start.17 = (bf16[192,384]{1,0:T(8,128)(2,1)S(1)}, bf16[192,384]{1,0:T(8,128)(2,1)S(1)}, u32[]{:S(2)}, u32[]{:S(2)}) collective-permute-start(bf16[192,384]{1,0:T(8,128)(2,1)S(1)} %add_convert_fusion.1.first), channel_id=1, source_target_pairs={{0,192},{64,128},{128,64},{192,0},{1,193},{65,129},{129,65},{193,1... | collective-permute-start | bytes 442376 | tf_op jit(solution)/shard_map/ppermute | solution.py:33
  178.5 3.6 %collective-permute-start.20 = (bf16[384,384]{1,0:T(8,128)(2,1)S(1)}, bf16[384,384]{1,0:T(8,128)(2,1)S(1)}, u32[]{:S(2)}, u32[]{:S(2)}) collective-permute-start(bf16[384,384]{1,0:T(8,128)(2,1)S(1)} %get-tuple-element.54.bar), channel_id=1, source_target_pairs={{0,1},{1,0},{2,3},{3,2},{4,5},{5,4},{6,7},{7,6},{8,9},{9,8},{10,11... | collective-permute-start | bytes 884744 | tf_op jit(solution)/shard_map/ppermute | solution.py:25
  180.8 1.2 collective-permute-start.21
  184.9 19.5 %all-to-all-start.4 = ((bf16[32,56,128]{2,1,0:T(8,128)(2,1)}), bf16[32,56,128]{2,1,0:T(8,128)(2,1)S(1)}, u32[]{:S(2)}, u32[]{:S(2)}) async-start(bf16[32,56,128]{2,1,0:T(8,128)(2,1)} %flows.3), calls=%async_computation.4 | async-start | bytes 917504 | tf_op jit(solution)/shard_map/all_to_all | solution.py:488
  (10 other events, 77.7 us)

commit v9 on v7

--- a/solution.py
+++ b/solution.py
@@ -259,7 +259,7 @@
     )(*operands)
 
 
-def updated(pairs, held, gen_max, stor_rate):
+def updated(pairs, held, gen_max, stor_rate, place):
     row_count, gen_count = held[0].shape
     stor_count = held[1].shape[1]
     operands = (*in_fast(*pairs, *held), *in_main(gen_max[None, :], stor_rate[None, :]))
@@ -268,8 +268,8 @@
         update_body,
         out_shape=(
             pltpu.VMEM((row_count, gen_count + stor_count), jnp.bfloat16),
-            pltpu.VMEM((row_count, gen_count), jnp.float32),
-            pltpu.VMEM((row_count, stor_count), jnp.float32),
+            place((row_count, gen_count), jnp.float32),
+            place((row_count, stor_count), jnp.float32),
             pltpu.VMEM((8, row_count), jnp.float32),
         ),
         in_specs=[in_vmem] * len(operands),
@@ -441,7 +441,11 @@
             (gen_old, stor_old) if iteration > 0 else (),
         )
         bar_low, gen_next, stor_next, total = updated(
-            summed_pairs(halves), held, gen_max, stor_rate
+            summed_pairs(halves),
+            held,
+            gen_max,
+            stor_rate,
+            pltpu.VMEM if iteration == 0 else pltpu.HBM,
         )
         balance = total[0] - load_total
         stor_bar = 2.0 * stor_next - stor_now

time: 203 us -> 202 us (level)
  transfers between devices with their start and end apart: 25 -> 25, of which waited for: 17 -> 17; matrix products, arithmetic and copies ran while one was open for 11% -> 10% of each run, Pallas kernels for 2% -> 2%
where the time goes in v9:
time: 202 us; the launch traced here: 201 us
  waiting for transfers between devices  64.5 us (32%)
  starting transfers between devices  51.2 us (25%)
  blocking collectives  40.6 us (20%)
  matrix products  15.6 us (8%)
  Pallas kernels  12.8 us (6%)
  other arithmetic  10.1 us (5%)
  local copies, waits for them, and re-layouts  5 us (2%)
    all_to_all x2, waiting for transfers between devices, shards(): received = lax.all_to_all(sent, CHIPS, 0, 0, tiled=True)  26.4 us
    ppermute x3, waiting for transfers between devices, doubled(): other = lax.ppermute(x, axis, [(i, i ^ step) for i in range(size)])  25.1 us
    all_to_all x1, blocking collectives, shards(): lax.all_to_all(slot_bus.reshape(area_count, slots), AREAS, 0, 0, tiled=True)  22.2 us
    all_to_all x1, blocking collectives, gathered_duals(): lax.all_to_all(sent, CHIPS, 0, 0, tiled=True).reshape(-1, sent.shape[2])  18.4 us
    ppermute x8, starting transfers between devices, swapped(): return lax.ppermute(x, 'core', [(0, 1), (1, 0)])  14.8 us
    ppermute x8, starting transfers between devices, from_side(): return lax.ppermute(x, 'lines', [(i, i ^ step) for i in range(4)])  11 us
    ppermute x3, starting transfers between devices, doubled(): other = lax.ppermute(x, axis, [(i, i ^ step) for i in range(size)])  8.42 us
    all_to_all x2, starting transfers between devices, shards(): received = lax.all_to_all(sent, CHIPS, 0, 0, tiled=True)  7.79 us
  transfers between devices with their start and end apart: 25, of which 17 were waited for; matrix products, arithmetic and copies ran while one was open for 10% of the time, Pallas kernels for 2%

profile of v9, /device:TPU:1, one launch (start us, length us, event | category | flops | bytes accessed | tf_op | source)
XLA Modules:
  0.0 200.9 jit_solution(4829764230681337065)
XLA Ops:
  1.9 22.2 %all_to_all.32 = s32[64,1,8]{2,1,0:T(1,128)S(1)} all-to-all(s32[64,1,8]{2,1,0:T(1,128)S(1)} %bitcast.83), channel_id=1, replica_groups=mesh['lines'=4,'z'=8,'x'=4,'core'=2] {'z','x','core'}, dimensions={0} | all-to-all | bytes 4096 | tf_op jit(solution)/shard_map/all_to_all | solution.py:381
  25.5 2.6 %fusion.2 = bf16[64,8,1024]{2,1,0:T(8,128)(2,1)} fusion(bf16[1024,1280]{1,0:T(8,128)(2,1)S(1)} %copy-done, s32[512]{0:T(512)S(1)} %eq.148), kind=kOutput, calls=%fused_computation.4 | convolution fusion | flops 1343356928 | bytes 3672064 | tf_op jit(solution)/shard_map/dot_general | solution.py:389
  28.1 5.6 %all-to-all-start.1 = ((bf16[64,8,1024]{2,1,0:T(8,128)(2,1)}), bf16[64,8,1024]{2,1,0:T(8,128)(2,1)}, u32[]{:S(2)}, u32[]{:S(2)}) async-start(bf16[64,8,1024]{2,1,0:T(8,128)(2,1)} %fusion.2), calls=%async_computation.1 | async-start | bytes 2097152 | tf_op jit(solution)/shard_map/all_to_all | solution.py:392
  33.6 5.6 %collective-permute-start = (bf16[1,1,1,16,384]{4,3,2,1,0:T(8,128)(2,1)S(1)}, bf16[1,1,1,16,384]{4,3,2,1,0:T(8,128)(2,1)S(1)}, u32[]{:S(2)}, u32[]{:S(2)}) collective-permute-start(bf16[1,1,1,16,384]{4,3,2,1,0:T(8,128)(2,1)S(1)} %get-tuple-element.70), channel_id=1, source_target_pairs={{0,32},{8,40},{16,48},{24,56},{32,0},{40,8},{48,16},{56,24},{1,33}... | collective-permute-start | bytes 36872 | tf_op jit(solution)/shard_map/ppermute | solution.py:288
  39.2 21.9 %collective-permute-done = bf16[1,1,1,16,384]{4,3,2,1,0:T(8,128)(2,1)S(1)} collective-permute-done((bf16[1,1,1,16,384]{4,3,2,1,0:T(8,128)(2,1)S(1)}, bf16[1,1,1,16,384]{4,3,2,1,0:T(8,128)(2,1)S(1)}, u32[]{:S(2)}, u32[]{:S(2)}) %collective-permute-start) | collective-permute-done | bytes 12320 | tf_op jit(solution)/shard_map/ppermute | solution.py:288
  61.7 3.0 %collective-permute-done.1 = bf16[2,1,1,16,384]{4,3,2,1,0:T(8,128)(2,1)S(1)} collective-permute-done((bf16[2,1,1,16,384]{4,3,2,1,0:T(8,128)(2,1)S(1)}, bf16[2,1,1,16,384]{4,3,2,1,0:T(8,128)(2,1)S(1)}, u32[]{:S(2)}, u32[]{:S(2)}) %collective-permute-start.1) | collective-permute-done | bytes 24608 | tf_op jit(solution)/shard_map/ppermute | solution.py:288
  64.7 2.2 %collective-permute-start.2 = (bf16[2,2,1,16,384]{4,3,2,1,0:T(8,128)(2,1)S(1)}, bf16[2,2,1,16,384]{4,3,2,1,0:T(8,128)(2,1)S(1)}, u32[]{:S(2)}, u32[]{:S(2)}) collective-permute-start(bf16[2,2,1,16,384]{4,3,2,1,0:T(8,128)(2,1)S(1)} %maximum_select_fusion.4), channel_id=1, source_target_pairs={{0,8},{8,0},{16,24},{24,16},{32,40},{40,32},{48,56},{56,48},{1,9},... | collective-permute-start | bytes 147464 | tf_op jit(solution)/shard_map/ppermute | solution.py:288
  70.1 2.1 %collective-permute-start.5 = (bf16[8,1,16,384]{3,2,0,1:T(8,128)(2,1)S(1)}, bf16[8,1,16,384]{3,2,0,1:T(8,128)(2,1)S(1)}, u32[]{:S(2)}, u32[]{:S(2)}) collective-permute-start(bf16[8,1,16,384]{3,2,0,1:T(8,128)(2,1)S(1)} %bitcast.80), channel_id=1, source_target_pairs={{0,6},{2,4},{4,2},{6,0},{1,7},{3,5},{5,3},{7,1},{8,14},{10,12},{12... | collective-permute-start | bytes 294920 | tf_op jit(solution)/shard_map/ppermute | solution.py:303
  72.9 1.9 collective-permute-done.5
  74.8 2.4 %collective-permute-done.4 = bf16[8,1,16,384]{3,2,0,1:T(8,128)(2,1)S(1)} collective-permute-done((bf16[8,1,16,384]{3,2,0,1:T(8,128)(2,1)S(1)}, bf16[8,1,16,384]{3,2,0,1:T(8,128)(2,1)S(1)}, u32[]{:S(2)}, u32[]{:S(2)}) %collective-permute-start.4) | collective-permute-done | bytes 98336 | tf_op jit(solution)/shard_map/ppermute | solution.py:303
  77.4 6.0 %collective-permute-start.6 = (bf16[512,384]{1,0:T(8,128)(2,1)S(1)}, bf16[512,384]{1,0:T(8,128)(2,1)S(1)}, u32[]{:S(2)}, u32[]{:S(2)}) collective-permute-start(bf16[512,384]{1,0:T(8,128)(2,1)S(1)} %bitcast.72), channel_id=1, source_target_pairs={{0,1},{1,0},{2,3},{3,2},{4,5},{5,4},{6,7},{7,6},{8,9},{9,8},{10,11... | collective-permute-start | bytes 1179656 | tf_op jit(solution)/shard_map/ppermute | solution.py:29
  83.4 2.7 %fusion.11 = f32[1024,384]{1,0:T(8,128)} fusion(bf16[1024,1280]{1,0:T(8,128)(2,1)S(1)} %copy-done, f32[384,1280]{1,0:T(8,128)S(1)} %copy-done.13), kind=kOutput, calls=%fused_computation.18 | convolution fusion | flops 1007124480 | bytes 6160384 | tf_op jit(solution)/shard_map/dot_general | solution.py:411
  86.9 3.1 %weights.1 = (bf16[512,384]{1,0:T(8,128)(2,1)S(1)}, bf16[512,384]{1,0:T(8,128)(2,1)S(1)}, bf16[192,384]{1,0:T(8,128)(2,1)S(1)}, bf16[192,384]{1,0:T(8,128)(2,1)S(1)}) custom-call(s32[1]{0:T(128)} %bitcast.core, bf16[512,1024]{1,0:T(8,128)(2,1)} %bitcast.3.columns, s32[1,256]{1,0:T(1,128)S(1)} %bitcast.70, bf16[512,128]{1,0:T(8,128)(2,1)} %bitcast.78, ...), custom_call_target="tpu_custom_call" | custom-call | tf_op jit(solution)/shard_map/weights/pallas_call | solution.py:118
  93.2 1.7 reduce_sum.29
  95.0 2.0 collective-permute-start.9
  99.4 2.0 %collective-permute-done.9 = bf16[192,384]{1,0:T(8,128)(2,1)S(1)} collective-permute-done((bf16[192,384]{1,0:T(8,128)(2,1)S(1)}, bf16[192,384]{1,0:T(8,128)(2,1)S(1)}, u32[]{:S(2)}, u32[]{:S(2)}) %collective-permute-start.9) | collective-permute-done | bytes 147488 | tf_op jit(solution)/shard_map/ppermute | solution.py:37
  101.6 2.3 %fusion.17.back = f32[384,128]{1,0:T(8,128)} fusion(f32[384,128]{1,0:T(8,128)} %param.33, s32[384]{0:T(512)S(1)} %add_select_fusion), kind=kOutput, calls=%fused_computation.25 | convolution fusion | flops 227082240 | bytes 394752 | tf_op jit(solution)/shard_map/dot_general | solution.py:330
  107.0 2.5 %collective-permute-start.14 = (f32[384]{0:T(512)S(1)}, f32[384]{0:T(512)S(1)}, u32[]{:S(2)}, u32[]{:S(2)}) collective-permute-start(f32[384]{0:T(512)S(1)} %sub.94), channel_id=1, source_target_pairs={{0,1},{1,0},{2,3},{3,2},{4,5},{5,4},{6,7},{7,6},{8,9},{9,8},{10,11... | collective-permute-start | bytes 4616 | tf_op jit(solution)/shard_map/ppermute | solution.py:29
  114.8 3.9 %all-to-all-start.2 = ((bf16[32,56,128]{2,1,0:T(8,128)(2,1)}), bf16[32,56,128]{2,1,0:T(8,128)(2,1)S(1)}, u32[]{:S(2)}, u32[]{:S(2)}) async-start(bf16[32,56,128]{2,1,0:T(8,128)(2,1)} %pad_maximum_fusion), calls=%async_computation.2 | async-start | bytes 917504 | tf_op jit(solution)/shard_map/all_to_all | solution.py:477
  121.0 13.2 %all-to-all-done.2.received = bf16[32,56,128]{2,1,0:T(8,128)(2,1)S(1)} async-done(((bf16[32,56,128]{2,1,0:T(8,128)(2,1)}), bf16[32,56,128]{2,1,0:T(8,128)(2,1)S(1)}, u32[]{:S(2)}, u32[]{:S(2)}) %all-to-all-start.2) | async-done | bytes 458784 | tf_op jit(solution)/shard_map/all_to_all | solution.py:477
  135.1 18.4 %all_to_all.33 = bf16[32,16,384]{2,1,0:T(8,128)(2,1)S(1)} all-to-all(bf16[32,16,384]{2,1,0:T(8,128)(2,1)} %get-tuple-element.42), channel_id=1, replica_groups=mesh['lines'=4,'z'=8,'x'=4,'core'=2] {'z','x'}, dimensions={0} | all-to-all | bytes 786432 | tf_op jit(solution)/shard_map/all_to_all | solution.py:283
  153.5 3.0 %collective-permute-start.15 = (bf16[512,384]{1,0:T(8,128)(2,1)S(1)}, bf16[512,384]{1,0:T(8,128)(2,1)S(1)}, u32[]{:S(2)}, u32[]{:S(2)}) collective-permute-start(bf16[512,384]{1,0:T(8,128)(2,1)S(1)} %bitcast.67), channel_id=1, source_target_pairs={{0,1},{1,0},{2,3},{3,2},{4,5},{5,4},{6,7},{7,6},{8,9},{9,8},{10,11... | collective-permute-start | bytes 1179656 | tf_op jit(solution)/shard_map/ppermute | solution.py:29
  156.5 1.7 fusion.38
  158.3 1.8 prices.1
  161.9 2.4 %collective-permute-start.18 = (bf16[192,384]{1,0:T(8,128)(2,1)S(1)}, bf16[192,384]{1,0:T(8,128)(2,1)S(1)}, u32[]{:S(2)}, u32[]{:S(2)}) collective-permute-start(bf16[192,384]{1,0:T(8,128)(2,1)S(1)} %get-tuple-element.44), channel_id=1, source_target_pairs={{0,192},{64,128},{128,64},{192,0},{1,193},{65,129},{129,65},{193,1... | collective-permute-start | bytes 442376 | tf_op jit(solution)/shard_map/ppermute | solution.py:37
  165.6 2.4 %collective-permute-start.17 = (bf16[192,384]{1,0:T(8,128)(2,1)S(1)}, bf16[192,384]{1,0:T(8,128)(2,1)S(1)}, u32[]{:S(2)}, u32[]{:S(2)}) collective-permute-start(bf16[192,384]{1,0:T(8,128)(2,1)S(1)} %add_convert_fusion.1.first), channel_id=1, source_target_pairs={{0,192},{64,128},{128,64},{192,0},{1,193},{65,129},{129,65},{193,1... | collective-permute-start | bytes 442376 | tf_op jit(solution)/shard_map/ppermute | solution.py:37
  169.2 1.6 bases.3
  172.7 1.9 update.3
  174.7 2.2 %collective-permute-start.21 = (f32[384]{0:T(512)S(1)}, f32[384]{0:T(512)S(1)}, u32[]{:S(2)}, u32[]{:S(2)}) collective-permute-start(f32[384]{0:T(512)S(1)} %sub.99), channel_id=1, source_target_pairs={{0,1},{1,0},{2,3},{3,2},{4,5},{5,4},{6,7},{7,6},{8,9},{9,8},{10,11... | collective-permute-start | bytes 4616 | tf_op jit(solution)/shard_map/ppermute | solution.py:29
  180.2 3.9 %all-to-all-start.4 = ((bf16[32,56,128]{2,1,0:T(8,128)(2,1)}), bf16[32,56,128]{2,1,0:T(8,128)(2,1)S(1)}, u32[]{:S(2)}, u32[]{:S(2)}) async-start(bf16[32,56,128]{2,1,0:T(8,128)(2,1)} %pad_maximum_fusion.1), calls=%async_computation.4 | async-start | bytes 917504 | tf_op jit(solution)/shard_map/all_to_all | solution.py:477
  184.2 2.3 %fusion.40 = f32[384,128]{1,0:T(8,128)} fusion(f32[384,128]{1,0:T(8,128)} %copy-done.23, s32[384]{0:T(512)S(1)} %add_select_fusion, f32[384,128]{1,0:T(8,128)S(1)} %copy-done.7, f32[384,128]{1,0:T(8,128)S(1)} %copy-done.21, f32[128]{0:T(128)S(1)} %get-tuple-element.78, f32[128]{0:T(128)S(1)} %get-tuple-element.77, pred[384]{0:T(512)(128)(4,1)S(1)} %fusion.58), kind=kOutput, calls=%fused_computation.68 | convolution fusion | flops 227622912 | bytes 789376 | tf_op jit(solution)/shard_map/dot_general | solution.py:330
  186.5 13.2 %all-to-all-done.4.received = bf16[32,56,128]{2,1,0:T(8,128)(2,1)S(1)} async-done(((bf16[32,56,128]{2,1,0:T(8,128)(2,1)}), bf16[32,56,128]{2,1,0:T(8,128)(2,1)S(1)}, u32[]{:S(2)}, u32[]{:S(2)}) %all-to-all-start.4) | async-done | bytes 458784 | tf_op jit(solution)/shard_map/all_to_all | solution.py:477
  (142 shorter events, 36.0 us)
Async XLA Ops:
  0.6 24.8 %copy-start = (bf16[1024,1280]{1,0:T(8,128)(2,1)S(1)}, bf16[1024,1280]{1,0:T(8,128)(2,1)}, u32[]{:S(2)}) copy-start(bf16[1024,1280]{1,0:T(8,128)(2,1)} %param.17) | copy-start | bytes 7864324
  25.5 41.5 %copy-start.20 = (s32[128]{0:T(128)S(1)}, s32[128]{0:T(128)}, u32[]{:S(2)}) copy-start(s32[128]{0:T(128)} %param.26) | copy-start | bytes 1540
  28.1 58.1 %all-to-all-start.1 = ((bf16[64,8,1024]{2,1,0:T(8,128)(2,1)}), bf16[64,8,1024]{2,1,0:T(8,128)(2,1)}, u32[]{:S(2)}, u32[]{:S(2)}) async-start(bf16[64,8,1024]{2,1,0:T(8,128)(2,1)} %fusion.2), calls=%async_computation.1 | async-start | bytes 2097152 | tf_op jit(solution)/shard_map/all_to_all | solution.py:392
  33.6 27.4 %collective-permute-start = (bf16[1,1,1,16,384]{4,3,2,1,0:T(8,128)(2,1)S(1)}, bf16[1,1,1,16,384]{4,3,2,1,0:T(8,128)(2,1)S(1)}, u32[]{:S(2)}, u32[]{:S(2)}) collective-permute-start(bf16[1,1,1,16,384]{4,3,2,1,0:T(8,128)(2,1)S(1)} %get-tuple-element.70), channel_id=1, source_target_pairs={{0,32},{8,40},{16,48},{24,56},{32,0},{40,8},{48,16},{56,24},{1,33}... | collective-permute-start | bytes 36872 | tf_op jit(solution)/shard_map/ppermute | solution.py:288
  61.1 3.7 %collective-permute-start.1 = (bf16[2,1,1,16,384]{4,3,2,1,0:T(8,128)(2,1)S(1)}, bf16[2,1,1,16,384]{4,3,2,1,0:T(8,128)(2,1)S(1)}, u32[]{:S(2)}, u32[]{:S(2)}) collective-permute-start(bf16[2,1,1,16,384]{4,3,2,1,0:T(8,128)(2,1)S(1)} %maximum_select_fusion.6), channel_id=1, source_target_pairs={{0,16},{8,24},{16,0},{24,8},{32,48},{40,56},{48,32},{56,40},{1,17}... | collective-permute-start | bytes 73736 | tf_op jit(solution)/shard_map/ppermute | solution.py:288
  64.7 3.7 %collective-permute-start.2 = (bf16[2,2,1,16,384]{4,3,2,1,0:T(8,128)(2,1)S(1)}, bf16[2,2,1,16,384]{4,3,2,1,0:T(8,128)(2,1)S(1)}, u32[]{:S(2)}, u32[]{:S(2)}) collective-permute-start(bf16[2,2,1,16,384]{4,3,2,1,0:T(8,128)(2,1)S(1)} %maximum_select_fusion.4), channel_id=1, source_target_pairs={{0,8},{8,0},{16,24},{24,16},{32,40},{40,32},{48,56},{56,48},{1,9},... | collective-permute-start | bytes 147464 | tf_op jit(solution)/shard_map/ppermute | solution.py:288
  68.2 15.2 %copy-start.13 = (f32[384,1280]{1,0:T(8,128)S(1)}, f32[384,1280]{1,0:T(8,128)}, u32[]{:S(2)}) copy-start(f32[384,1280]{1,0:T(8,128)} %param.18) | copy-start | bytes 5898244
  68.5 4.4 %collective-permute-start.3 = (bf16[8,1,16,384]{3,2,0,1:T(8,128)(2,1)S(1)}, bf16[8,1,16,384]{3,2,0,1:T(8,128)(2,1)S(1)}, u32[]{:S(2)}, u32[]{:S(2)}) collective-permute-start(bf16[8,1,16,384]{3,2,0,1:T(8,128)(2,1)S(1)} %bitcast.79), channel_id=1, source_target_pairs={{0,2},{2,0},{4,6},{6,4},{1,3},{3,1},{5,7},{7,5},{8,10},{10,8},{12,... | collective-permute-start | bytes 294920 | tf_op jit(solution)/shard_map/ppermute | solution.py:303
  70.1 4.7 %collective-permute-start.5 = (bf16[8,1,16,384]{3,2,0,1:T(8,128)(2,1)S(1)}, bf16[8,1,16,384]{3,2,0,1:T(8,128)(2,1)S(1)}, u32[]{:S(2)}, u32[]{:S(2)}) collective-permute-start(bf16[8,1,16,384]{3,2,0,1:T(8,128)(2,1)S(1)} %bitcast.80), channel_id=1, source_target_pairs={{0,6},{2,4},{4,2},{6,0},{1,7},{3,5},{5,3},{7,1},{8,14},{10,12},{12... | collective-permute-start | bytes 294920 | tf_op jit(solution)/shard_map/ppermute | solution.py:303
  72.2 5.0 %collective-permute-start.4 = (bf16[8,1,16,384]{3,2,0,1:T(8,128)(2,1)S(1)}, bf16[8,1,16,384]{3,2,0,1:T(8,128)(2,1)S(1)}, u32[]{:S(2)}, u32[]{:S(2)}) collective-permute-start(bf16[8,1,16,384]{3,2,0,1:T(8,128)(2,1)S(1)} %bitcast.81), channel_id=1, source_target_pairs={{0,4},{2,6},{4,0},{6,2},{1,5},{3,7},{5,1},{7,3},{8,12},{10,14},{12... | collective-permute-start | bytes 294920 | tf_op jit(solution)/shard_map/ppermute | solution.py:303
  77.4 8.8 %collective-permute-start.6 = (bf16[512,384]{1,0:T(8,128)(2,1)S(1)}, bf16[512,384]{1,0:T(8,128)(2,1)S(1)}, u32[]{:S(2)}, u32[]{:S(2)}) collective-permute-start(bf16[512,384]{1,0:T(8,128)(2,1)S(1)} %bitcast.72), channel_id=1, source_target_pairs={{0,1},{1,0},{2,3},{3,2},{4,5},{5,4},{6,7},{7,6},{8,9},{9,8},{10,11... | collective-permute-start | bytes 1179656 | tf_op jit(solution)/shard_map/ppermute | solution.py:29
  90.1 23.4 %copy-start.1 = (bf16[512,384]{1,0:T(8,128)(2,1)}, bf16[512,384]{1,0:T(8,128)(2,1)S(1)}, u32[]{:S(2)}) copy-start(bf16[512,384]{1,0:T(8,128)(2,1)S(1)} %get-tuple-element.32.weight_own) | copy-start | bytes 1179652
  90.1 6.9 %collective-permute-start.7 = (bf16[192,384]{1,0:T(8,128)(2,1)S(1)}, bf16[192,384]{1,0:T(8,128)(2,1)}, u32[]{:S(2)}, u32[]{:S(2)}) collective-permute-start(bf16[192,384]{1,0:T(8,128)(2,1)S(1)} %get-tuple-element.33), channel_id=1, source_target_pairs={{0,64},{64,0},{128,192},{192,128},{1,65},{65,1},{129,193},{193,129... | collective-permute-start | bytes 442376 | tf_op jit(solution)/shard_map/ppermute | solution.py:37
  92.7 16.8 %collective-permute-start.13 = (f32[512,384]{1,0:T(8,128)}, f32[512,384]{1,0:T(8,128)}, u32[]{:S(2)}, u32[]{:S(2)}) collective-permute-start(f32[512,384]{1,0:T(8,128)} %bitcast.23), channel_id=1, source_target_pairs={{0,1},{1,0},{2,3},{3,2},{4,5},{5,4},{6,7},{7,6},{8,9},{9,8},{10,11... | collective-permute-start | bytes 2359304 | tf_op jit(solution)/shard_map/ppermute | solution.py:29
  95.0 6.5 %collective-permute-start.9 = (bf16[192,384]{1,0:T(8,128)(2,1)S(1)}, bf16[192,384]{1,0:T(8,128)(2,1)S(1)}, u32[]{:S(2)}, u32[]{:S(2)}) collective-permute-start(bf16[192,384]{1,0:T(8,128)(2,1)S(1)} %get-tuple-element.34), channel_id=1, source_target_pairs={{0,192},{64,128},{128,64},{192,0},{1,193},{65,129},{129,65},{193,1... | collective-permute-start | bytes 442376 | tf_op jit(solution)/shard_map/ppermute | solution.py:37
  97.9 7.4 %collective-permute-start.8 = (bf16[192,384]{1,0:T(8,128)(2,1)S(1)}, bf16[192,384]{1,0:T(8,128)(2,1)S(1)}, u32[]{:S(2)}, u32[]{:S(2)}) collective-permute-start(bf16[192,384]{1,0:T(8,128)(2,1)S(1)} %add_convert_fusion.3.first), channel_id=1, source_target_pairs={{0,192},{64,128},{128,64},{192,0},{1,193},{65,129},{129,65},{193,1... | collective-permute-start | bytes 442376 | tf_op jit(solution)/shard_map/ppermute | solution.py:37
  101.5 4.1 %collective-permute-start.10 = (bf16[192,384]{1,0:T(8,128)(2,1)S(1)}, bf16[192,384]{1,0:T(8,128)(2,1)S(1)}, u32[]{:S(2)}, u32[]{:S(2)}) collective-permute-start(bf16[192,384]{1,0:T(8,128)(2,1)S(1)} %add_convert_fusion.2.second), channel_id=1, source_target_pairs={{0,64},{64,0},{128,192},{192,128},{1,65},{65,1},{129,193},{193,129... | collective-permute-start | bytes 442376 | tf_op jit(solution)/shard_map/ppermute | solution.py:37
  107.0 49.5 %copy-start.6 = (f32[384,128]{1,0:T(8,128)}, f32[384,128]{1,0:T(8,128)S(1)}, u32[]{:S(2)}) copy-start(f32[384,128]{1,0:T(8,128)S(1)} %get-tuple-element.46.stor_now) | copy-start | bytes 589828
  107.0 4.4 %collective-permute-start.14 = (f32[384]{0:T(512)S(1)}, f32[384]{0:T(512)S(1)}, u32[]{:S(2)}, u32[]{:S(2)}) collective-permute-start(f32[384]{0:T(512)S(1)} %sub.94), channel_id=1, source_target_pairs={{0,1},{1,0},{2,3},{3,2},{4,5},{5,4},{6,7},{7,6},{8,9},{9,8},{10,11... | collective-permute-start | bytes 4616 | tf_op jit(solution)/shard_map/ppermute | solution.py:29
  110.8 1.8 collective-permute-start.11
  111.0 2.0 %collective-permute-start.12 = (bf16[384,384]{1,0:T(8,128)(2,1)S(1)}, bf16[384,384]{1,0:T(8,128)(2,1)S(1)}, u32[]{:S(2)}, u32[]{:S(2)}) collective-permute-start(bf16[384,384]{1,0:T(8,128)(2,1)S(1)} %get-tuple-element.39), channel_id=1, source_target_pairs={{0,1},{1,0},{2,3},{3,2},{4,5},{5,4},{6,7},{7,6},{8,9},{9,8},{10,11... | collective-permute-start | bytes 884744 | tf_op jit(solution)/shard_map/ppermute | solution.py:29
  113.9 42.6 %copy-start.22 = (f32[128]{0:T(128)S(1)}, f32[128]{0:T(128)}, u32[]{:S(2)}) copy-start(f32[128]{0:T(128)} %param.29) | copy-start | bytes 1540
  114.8 19.4 %all-to-all-start.2 = ((bf16[32,56,128]{2,1,0:T(8,128)(2,1)}), bf16[32,56,128]{2,1,0:T(8,128)(2,1)S(1)}, u32[]{:S(2)}, u32[]{:S(2)}) async-start(bf16[32,56,128]{2,1,0:T(8,128)(2,1)} %pad_maximum_fusion), calls=%async_computation.2 | async-start | bytes 917504 | tf_op jit(solution)/shard_map/all_to_all | solution.py:477
  153.5 4.7 %collective-permute-start.15 = (bf16[512,384]{1,0:T(8,128)(2,1)S(1)}, bf16[512,384]{1,0:T(8,128)(2,1)S(1)}, u32[]{:S(2)}, u32[]{:S(2)}) collective-permute-start(bf16[512,384]{1,0:T(8,128)(2,1)S(1)} %bitcast.67), channel_id=1, source_target_pairs={{0,1},{1,0},{2,3},{3,2},{4,5},{5,4},{6,7},{7,6},{8,9},{9,8},{10,11... | collective-permute-start | bytes 1179656 | tf_op jit(solution)/shard_map/ppermute | solution.py:29
  160.0 18.4 %copy-start.17 = (bf16[512,384]{1,0:T(8,128)(2,1)S(1)}, bf16[512,384]{1,0:T(8,128)(2,1)}, u32[]{:S(2)}) copy-start(bf16[512,384]{1,0:T(8,128)(2,1)} %copy-done.16) | copy-start | bytes 1179652
  160.0 5.5 %collective-permute-start.16 = (bf16[192,384]{1,0:T(8,128)(2,1)S(1)}, bf16[192,384]{1,0:T(8,128)(2,1)S(1)}, u32[]{:S(2)}, u32[]{:S(2)}) collective-permute-start(bf16[192,384]{1,0:T(8,128)(2,1)S(1)} %get-tuple-element.43), channel_id=1, source_target_pairs={{0,64},{64,0},{128,192},{192,128},{1,65},{65,1},{129,193},{193,129... | collective-permute-start | bytes 442376 | tf_op jit(solution)/shard_map/ppermute | solution.py:37
  161.9 6.3 %collective-permute-start.18 = (bf16[192,384]{1,0:T(8,128)(2,1)S(1)}, bf16[192,384]{1,0:T(8,128)(2,1)S(1)}, u32[]{:S(2)}, u32[]{:S(2)}) collective-permute-start(bf16[192,384]{1,0:T(8,128)(2,1)S(1)} %get-tuple-element.44), channel_id=1, source_target_pairs={{0,192},{64,128},{128,64},{192,0},{1,193},{65,129},{129,65},{193,1... | collective-permute-start | bytes 442376 | tf_op jit(solution)/shard_map/ppermute | solution.py:37
  165.6 5.8 %collective-permute-start.17 = (bf16[192,384]{1,0:T(8,128)(2,1)S(1)}, bf16[192,384]{1,0:T(8,128)(2,1)S(1)}, u32[]{:S(2)}, u32[]{:S(2)}) collective-permute-start(bf16[192,384]{1,0:T(8,128)(2,1)S(1)} %add_convert_fusion.1.first), channel_id=1, source_target_pairs={{0,192},{64,128},{128,64},{192,0},{1,193},{65,129},{129,65},{193,1... | collective-permute-start | bytes 442376 | tf_op jit(solution)/shard_map/ppermute | solution.py:37
  168.3 4.5 %collective-permute-start.19 = (bf16[192,384]{1,0:T(8,128)(2,1)S(1)}, bf16[192,384]{1,0:T(8,128)(2,1)S(1)}, u32[]{:S(2)}, u32[]{:S(2)}) collective-permute-start(bf16[192,384]{1,0:T(8,128)(2,1)S(1)} %add_convert_fusion.second), channel_id=1, source_target_pairs={{0,64},{64,0},{128,192},{192,128},{1,65},{65,1},{129,193},{193,129... | collective-permute-start | bytes 442376 | tf_op jit(solution)/shard_map/ppermute | solution.py:37
  174.7 3.0 %collective-permute-start.21 = (f32[384]{0:T(512)S(1)}, f32[384]{0:T(512)S(1)}, u32[]{:S(2)}, u32[]{:S(2)}) collective-permute-start(f32[384]{0:T(512)S(1)} %sub.99), channel_id=1, source_target_pairs={{0,1},{1,0},{2,3},{3,2},{4,5},{5,4},{6,7},{7,6},{8,9},{9,8},{10,11... | collective-permute-start | bytes 4616 | tf_op jit(solution)/shard_map/ppermute | solution.py:29
  176.9 1.6 collective-permute-start.20
  180.2 19.4 %all-to-all-start.4 = ((bf16[32,56,128]{2,1,0:T(8,128)(2,1)}), bf16[32,56,128]{2,1,0:T(8,128)(2,1)S(1)}, u32[]{:S(2)}, u32[]{:S(2)}) async-start(bf16[32,56,128]{2,1,0:T(8,128)(2,1)} %pad_maximum_fusion.1), calls=%async_computation.4 | async-start | bytes 917504 | tf_op jit(solution)/shard_map/all_to_all | solution.py:477
  (17 other events, 113.4 us)
